TPU v7x, 32 devices: a whole 2x2x4 slice. The times are simulated.
32 devices in a mesh: dp: 16 (over z, y, core), tensor: 2 (over x).
Axes of the slice: x: 2, y: 2, z: 4, core: 2. Of those that a mesh axis runs over, the one named last changes fastest.
Arguments:
- block_in: float32 [4096, 2048], P(('dp', 'tensor')), may hold values from -6 to 6
- positions: int32 [16, 256], P('dp'), may hold values from 0 to 255, each once within a row
- out_grad: float32 [4096, 2048], P(('dp', 'tensor')), may hold values from -6 to 6
- attn_weight: float32 [2048, 4, 2048], P('dp', None, 'tensor'), may hold values from -3 to 3
- mlp_weight: float32 [2048, 2, 8192], P('dp', None, 'tensor'), may hold values from -0.125 to 0.125
- small_params: float32 [12, 2048], P(None, ('dp', 'tensor')), may hold values from -1 to 2, as said below
- attn_first: float32 [2048, 4, 2048], P('dp', None, 'tensor'), may hold values from -12 to 12
- attn_second: float32 [2048, 4, 2048], P('dp', None, 'tensor'), may hold values from 1 to 100
- mlp_first: float32 [2048, 2, 8192], P('dp', None, 'tensor'), may hold values from -12 to 12
- mlp_second: float32 [2048, 2, 8192], P('dp', None, 'tensor'), may hold values from 1 to 100
- small_first: float32 [12, 2048], P(None, ('dp', 'tensor')), may hold values from -12 to 12
- small_second: float32 [12, 2048], P(None, ('dp', 'tensor')), may hold values from 1 to 100
Outputs:
- block_out: float32 [4096, 2048], P(('dp', 'tensor'))
- input_grad: float32 [4096, 2048], P(('dp', 'tensor'))
- attn_grad: float32 [2048, 4, 2048], P('dp', None, 'tensor')
- mlp_grad: float32 [2048, 2, 8192], P('dp', None, 'tensor')
- small_grad: float32 [12, 2048], P(None, ('dp', 'tensor'))
- attn_new: float32 [2048, 4, 2048], P('dp', None, 'tensor')
- attn_first_new: float32 [2048, 4, 2048], P('dp', None, 'tensor')
- attn_second_new: float32 [2048, 4, 2048], P('dp', None, 'tensor')
- mlp_new: float32 [2048, 2, 8192], P('dp', None, 'tensor')
- mlp_first_new: float32 [2048, 2, 8192], P('dp', None, 'tensor')
- mlp_second_new: float32 [2048, 2, 8192], P('dp', None, 'tensor')
- small_new: float32 [12, 2048], P(None, ('dp', 'tensor'))
- small_first_new: float32 [12, 2048], P(None, ('dp', 'tensor'))
- small_second_new: float32 [12, 2048], P(None, ('dp', 'tensor'))
Inputs may be any that keep to these rules, and one draw needn't show every extreme that they name: Each row of positions holds every position once. `small_params`: rows 0 and 2 are positive.
All inputs are finite; a program needn't handle non-finite values.
Results may differ from a plain program's by a relative error of at most 0.0092.
Values may be sent and summed in bfloat16 or wider, within the bound.
A program may use at most 448 MiB of HBM per device.

v0:
```python
import jax
import jax.numpy as jnp
from jax import lax
from jax.sharding import PartitionSpec as P

ROT = 64
ADAM_STEP = 3
HEAD_DIM = 256


norm_epsilon = 1e-05
learn_rate = 0.006
beta_first = 0.9
beta_second = 0.95
adam_epsilon = 1e-08
weight_decay = 0.1


def layer_stats(row_data):
    center = row_data - jnp.mean(row_data, axis=-1, keepdims=True)
    inverse = lax.rsqrt(jnp.mean(center * center, axis=-1, keepdims=True) + norm_epsilon)
    return (center * inverse, inverse)


def norm_back(grad_rows, gain_row, normed, inverse):
    scaled = grad_rows * gain_row
    return inverse * (
        scaled
        - jnp.mean(scaled, axis=-1, keepdims=True)
        - normed * jnp.mean(scaled * normed, axis=-1, keepdims=True)
    )


def angle_tables(places):
    half_dims = ROT // 2
    frequency = 10000.0 ** (-(jnp.arange(half_dims).astype(jnp.float32) * (2.0 / ROT)))
    angles = places.astype(jnp.float32)[:, None] * frequency[None, :]
    return (jnp.cos(angles)[:, None, :], jnp.sin(angles)[:, None, :])


def rotate(values, cos_table, sin_table):
    half_dims = ROT // 2
    low_half = values[..., :half_dims]
    high_half = values[..., half_dims:ROT]
    return jnp.concatenate(
        [
            low_half * cos_table - high_half * sin_table,
            high_half * cos_table + low_half * sin_table,
            values[..., ROT:],
        ],
        axis=-1,
    )


def rotate_back(grad_rows, cos_table, sin_table):
    half_dims = ROT // 2
    low_half = grad_rows[..., :half_dims]
    high_half = grad_rows[..., half_dims:ROT]
    return jnp.concatenate(
        [
            low_half * cos_table + high_half * sin_table,
            high_half * cos_table - low_half * sin_table,
            grad_rows[..., ROT:],
        ],
        axis=-1,
    )


def gelu_exact(pre_act):
    return 0.5 * pre_act * (1.0 + lax.erf(pre_act * 0.7071067811865476))


def gelu_slope(pre_act):
    return (
        0.5 * (1.0 + lax.erf(pre_act * 0.7071067811865476))
        + pre_act * jnp.exp(-0.5 * pre_act * pre_act) * 0.3989422804014327
    )


def adam_step(weight, gradient, moment_one, moment_two):
    one_new = beta_first * moment_one + (1.0 - beta_first) * gradient
    two_new = beta_second * moment_two + (1.0 - beta_second) * gradient * gradient
    corrected = (
        one_new
        / (1.0 - beta_first**ADAM_STEP)
        / (jnp.sqrt(two_new / (1.0 - beta_second**ADAM_STEP)) + adam_epsilon)
    )
    return (weight - learn_rate * (corrected + weight_decay * weight), one_new, two_new)


def attn_scores(queries, key_rows, visible, score_scale):
    scores = (
        jnp.einsum("qhd,khd->hqk", queries, key_rows, preferred_element_type=jnp.float32)
        * score_scale
    )
    return jnp.where(visible[None], scores, -jnp.inf)


def body(
    block_in,
    positions,
    out_grad,
    attn_weight,
    mlp_weight,
    small_params,
    attn_first,
    attn_second,
    mlp_first,
    mlp_second,
    small_first,
    small_second,
):
    f32 = jnp.float32
    bf16_type = jnp.bfloat16
    small_all = lax.all_gather(small_params, ("dp", "tensor"), axis=1, tiled=True)
    attn_low = lax.all_gather(attn_weight.astype(bf16_type), "dp", axis=0, tiled=True)
    mlp_low = lax.all_gather(mlp_weight.astype(bf16_type), "dp", axis=0, tiled=True)
    model_width = attn_low.shape[0]
    local_width = attn_low.shape[2]
    local_hidden = mlp_low.shape[2]
    local_heads = local_width // HEAD_DIM
    tensor_index = lax.axis_index("tensor")
    up_all = small_all[8:12].reshape(-1)
    query_bias = lax.dynamic_slice_in_dim(small_all[4], tensor_index * local_width, local_width)
    value_bias = lax.dynamic_slice_in_dim(small_all[5], tensor_index * local_width, local_width)
    up_bias = lax.dynamic_slice_in_dim(up_all, tensor_index * local_hidden, local_hidden)
    score_scale = HEAD_DIM ** (-0.5)
    normed, inverse = layer_stats(block_in)
    norm_one = (normed * small_all[0] + small_all[1]).astype(bf16_type)
    norm_two = (normed * small_all[2] + small_all[3]).astype(bf16_type)
    full_one, full_two = (
        lax.all_gather(norm_one, "tensor", axis=0, tiled=True),
        lax.all_gather(norm_two, "tensor", axis=0, tiled=True),
    )
    seq_rows = full_one.shape[0]
    places = positions[0]
    cos_table, sin_table = angle_tables(places)
    visible = places[None, :] <= places[:, None]
    query_pre = jnp.dot(full_one, attn_low[:, 0, :], preferred_element_type=f32) + query_bias
    key_pre = jnp.dot(full_one, attn_low[:, 1, :], preferred_element_type=f32)
    values_low = (
        (jnp.dot(full_one, attn_low[:, 2, :], preferred_element_type=f32) + value_bias)
        .astype(bf16_type)
        .reshape(seq_rows, local_heads, HEAD_DIM)
    )
    queries = rotate(
        query_pre.reshape(seq_rows, local_heads, HEAD_DIM), cos_table, sin_table
    ).astype(bf16_type)
    key_rows = rotate(
        key_pre.reshape(seq_rows, local_heads, HEAD_DIM), cos_table, sin_table
    ).astype(bf16_type)
    scores = attn_scores(queries, key_rows, visible, score_scale)
    row_max = jnp.max(scores, axis=-1, keepdims=True)
    log_total = row_max + jnp.log(jnp.sum(jnp.exp(scores - row_max), axis=-1, keepdims=True))
    probs_low = jnp.exp(scores - log_total).astype(bf16_type)
    attended = (
        jnp.einsum("hqk,khd->qhd", probs_low, values_low, preferred_element_type=f32)
        .astype(bf16_type)
        .reshape(seq_rows, local_width)
    )
    attn_part = jnp.einsum("sc,ic->si", attended, attn_low[:, 3, :], preferred_element_type=f32)
    pre_act = jnp.dot(full_two, mlp_low[:, 0, :], preferred_element_type=f32) + up_bias
    activation = gelu_exact(pre_act).astype(bf16_type)
    mlp_part = jnp.einsum("sf,if->si", activation, mlp_low[:, 1, :], preferred_element_type=f32)
    mixed = lax.psum_scatter(attn_part + mlp_part, "tensor", scatter_dimension=0, tiled=True)
    block_out = block_in + mixed + small_all[6] + small_all[7]
    grad_full = lax.all_gather(out_grad.astype(bf16_type), "tensor", axis=0, tiled=True)
    d_attended = (
        jnp.dot(grad_full, attn_low[:, 3, :], preferred_element_type=f32)
        .astype(bf16_type)
        .reshape(seq_rows, local_heads, HEAD_DIM)
    )
    attn_probs = jnp.exp(attn_scores(queries, key_rows, visible, score_scale) - log_total)
    probs_again = attn_probs.astype(bf16_type)
    d_probs = jnp.einsum("qhd,khd->hqk", d_attended, values_low, preferred_element_type=f32)
    d_scores = (
        attn_probs * (d_probs - jnp.sum(attn_probs * d_probs, axis=-1, keepdims=True)) * score_scale
    ).astype(bf16_type)
    d_query = rotate_back(
        jnp.einsum("hqk,khd->qhd", d_scores, key_rows, preferred_element_type=f32),
        cos_table,
        sin_table,
    ).reshape(seq_rows, local_width)
    d_key = rotate_back(
        jnp.einsum("hqk,qhd->khd", d_scores, queries, preferred_element_type=f32),
        cos_table,
        sin_table,
    ).reshape(seq_rows, local_width)
    d_value = jnp.einsum(
        "hqk,qhd->khd", probs_again, d_attended, preferred_element_type=f32
    ).reshape(seq_rows, local_width)
    dq_low = d_query.astype(bf16_type)
    dk_low = d_key.astype(bf16_type)
    dv_low = d_value.astype(bf16_type)
    d_norm_one = (
        jnp.einsum("sc,ic->si", dq_low, attn_low[:, 0, :], preferred_element_type=f32)
        + jnp.einsum("sc,ic->si", dk_low, attn_low[:, 1, :], preferred_element_type=f32)
        + jnp.einsum("sc,ic->si", dv_low, attn_low[:, 2, :], preferred_element_type=f32)
    )
    d_pre = jnp.dot(grad_full, mlp_low[:, 1, :], preferred_element_type=f32) * gelu_slope(pre_act)
    d_pre_low = d_pre.astype(bf16_type)
    d_norm_two = jnp.einsum("sf,if->si", d_pre_low, mlp_low[:, 0, :], preferred_element_type=f32)
    rows_one, rows_two = (
        lax.psum_scatter(d_norm_one, "tensor", scatter_dimension=0, tiled=True),
        lax.psum_scatter(d_norm_two, "tensor", scatter_dimension=0, tiled=True),
    )
    input_grad = (
        out_grad
        + norm_back(rows_one, small_all[0], normed, inverse)
        + norm_back(rows_two, small_all[2], normed, inverse)
    )
    grad_part = grad_full
    attn_grad = lax.psum_scatter(
        jnp.stack(
            [
                jnp.einsum("sc,sn->cn", full_one, dq_low, preferred_element_type=f32),
                jnp.einsum("sc,sn->cn", full_one, dk_low, preferred_element_type=f32),
                jnp.einsum("sc,sn->cn", full_one, dv_low, preferred_element_type=f32),
                jnp.einsum("sc,sn->cn", grad_part, attended, preferred_element_type=f32),
            ],
            axis=1,
        ),
        "dp",
        scatter_dimension=0,
        tiled=True,
    )
    grad_part = grad_full
    mlp_grad = lax.psum_scatter(
        jnp.stack(
            [
                jnp.einsum("sc,sn->cn", full_two, d_pre_low, preferred_element_type=f32),
                jnp.einsum("sc,sn->cn", grad_part, activation, preferred_element_type=f32),
            ],
            axis=1,
        ),
        "dp",
        scatter_dimension=0,
        tiled=True,
    )
    width_zeros = jnp.zeros((model_width,), f32)
    query_sum = lax.dynamic_update_slice_in_dim(
        width_zeros, jnp.sum(d_query, axis=0), tensor_index * local_width, 0
    )
    value_sum = lax.dynamic_update_slice_in_dim(
        width_zeros, jnp.sum(d_value, axis=0), tensor_index * local_width, 0
    )
    up_sum = lax.dynamic_update_slice_in_dim(
        jnp.zeros(up_all.shape, f32), jnp.sum(d_pre, axis=0), tensor_index * local_hidden, 0
    ).reshape(4, model_width)
    out_sum = jnp.sum(out_grad, axis=0)
    small_terms = jnp.concatenate(
        [
            jnp.stack(
                [
                    jnp.sum(rows_one * normed, axis=0),
                    jnp.sum(rows_one, axis=0),
                    jnp.sum(rows_two * normed, axis=0),
                    jnp.sum(rows_two, axis=0),
                    query_sum,
                    value_sum,
                    out_sum,
                    out_sum,
                ]
            ),
            up_sum,
        ],
        axis=0,
    )
    small_grad = lax.psum_scatter(small_terms, ("dp", "tensor"), scatter_dimension=1, tiled=True)
    attn_new, attn_first_new, attn_second_new = adam_step(
        attn_weight, attn_grad, attn_first, attn_second
    )
    mlp_new, mlp_first_new, mlp_second_new = adam_step(mlp_weight, mlp_grad, mlp_first, mlp_second)
    small_new, small_first_new, small_second_new = adam_step(
        small_params, small_grad, small_first, small_second
    )
    return (
        block_out,
        input_grad,
        attn_grad,
        mlp_grad,
        small_grad,
        attn_new,
        attn_first_new,
        attn_second_new,
        mlp_new,
        mlp_first_new,
        mlp_second_new,
        small_new,
        small_first_new,
        small_second_new,
    )


def solution(mesh):
    placed = (
        P(("dp", "tensor"), None),
        P("dp", None),
        P(("dp", "tensor"), None),
        P("dp", None, "tensor"),
        P("dp", None, "tensor"),
        P(None, ("dp", "tensor")),
        P("dp", None, "tensor"),
        P("dp", None, "tensor"),
        P("dp", None, "tensor"),
        P("dp", None, "tensor"),
        P(None, ("dp", "tensor")),
        P(None, ("dp", "tensor")),
    )
    return jax.shard_map(
        body,
        mesh=mesh,
        in_specs=placed,
        out_specs=(
            P(("dp", "tensor"), None),
            P(("dp", "tensor"), None),
            P("dp", None, "tensor"),
            P("dp", None, "tensor"),
            P(None, ("dp", "tensor")),
            P("dp", None, "tensor"),
            P("dp", None, "tensor"),
            P("dp", None, "tensor"),
            P("dp", None, "tensor"),
            P("dp", None, "tensor"),
            P("dp", None, "tensor"),
            P(None, ("dp", "tensor")),
            P(None, ("dp", "tensor")),
            P(None, ("dp", "tensor")),
        ),
        check_vma=False,
    )
```

profile of v0, /device:TPU:0, one launch (start us, length us, event | category | flops | bytes accessed | tf_op | source)
XLA Modules:
  0.0 1632.5 jit_solution(9339702588744221715)
XLA Ops:
  14.2 74.2 %all-gather = f32[32,64,12]{1,2,0:T(8,128)S(1)} all-gather(f32[1,64,12]{1,2,0:T(8,128)S(1)} %bitcast.173), channel_id=1, replica_groups=mesh['dp'=16,'tensor'=2] {'dp','tensor'}, dimensions={0}, use_global_device_ids=true | all-gather | bytes 101376 | tf_op jit(solution)/shard_map/all_gather | solution.py:115
  91.7 6.0 copy.178
  99.5 66.3 %all-gather.9.cloned.1.call-done = bf16[2048,4,1024]{2,0,1:T(8,128)(2,1)} async-done(((bf16[128,4,1024]{2,0,1:T(8,128)(2,1)}), bf16[2048,4,1024]{2,0,1:T(8,128)(2,1)}) %all-gather.9.cloned.1.call-update) | async-done | bytes 16777232 | tf_op jit(solution)/shard_map/all_gather | solution.py:116
  175.3 6.6 copy.104
  181.9 5.4 all-gather.7.cloned.1.call-done
  242.0 138.7 %all-gather.13.cloned.1.call-done = bf16[2048,2,4096]{2,0,1:T(8,128)(2,1)} async-done(((bf16[128,2,4096]{2,0,1:T(8,128)(2,1)}), bf16[2048,2,4096]{2,0,1:T(8,128)(2,1)}) %all-gather.13.cloned.1.call-update) | async-done | bytes 33554448 | tf_op jit(solution)/shard_map/all_gather | solution.py:117
  380.7 8.5 fusion.6
  389.2 12.2 fusion.77
  401.5 12.3 fusion.1
  416.6 12.9 fusion.4
  429.5 5.5 fusion.22
  437.2 5.8 convolution_bitcast_fusion.2
  461.1 23.5 %pad_maximum_fusion.1 = f32[2048,4,1024]{2,0,1:T(8,128)} fusion(f32[2048,1,1024]{2,0,1:T(8,128)} %convolution_bitcast_fusion.2, f32[2048,1,1024]{2,0,1:T(8,128)} %convolution_bitcast_fusion.3, f32[2048,1,1024]{2,0,1:T(8,128)} %convolution_bitcast_fusion.4, f32[2048,1,1024]{2,0,1:T(8,128)} %convolution_bitcast_fusion.5), kind=kLoop, calls=%fused_computation.2 | loop fusion | flops 25165824 | bytes 67108864 | tf_op jit(solution)/shard_map/stack | solution.py:214
  485.9 14.9 convolution_bitcast_fusion.1
  500.8 13.2 convolution_bitcast_fusion
  513.9 44.7 %pad_maximum_fusion = f32[2048,2,4096]{2,0,1:T(8,128)} fusion(f32[2048,1,4096]{2,0,1:T(8,128)} %convolution_bitcast_fusion, f32[2048,1,4096]{2,0,1:T(8,128)} %convolution_bitcast_fusion.1), kind=kLoop, calls=%fused_computation.1 | loop fusion | flops 16777216 | bytes 134217728 | tf_op jit(solution)/shard_map/stack | solution.py:229
  563.6 60.9 %reduce-scatter.19.cloned.1.call-done = f32[64,12]{1,0:T(8,128)} async-done(((f32[2048,12]{1,0:T(8,128)}), f32[64,12]{1,0:T(8,128)}) %reduce-scatter.19.cloned.1.call-update) | async-done | bytes 3088
  625.9 328.9 %reduce-scatter.15.cloned.1.call-done = f32[128,4,1024]{2,0,1:T(8,128)} async-done(((f32[2048,4,1024]{2,0,1:T(8,128)}), f32[128,4,1024]{2,0,1:T(8,128)}) %reduce-scatter.15.cloned.1.call-update) | async-done | bytes 2097168 | tf_op jit(solution)/shard_map/reduce_scatter | solution.py:213
  954.9 7.4 multiply_subtract_fusion.1
  973.0 617.8 %reduce-scatter.17.cloned.1.call-done = f32[128,2,4096]{2,0,1:T(8,128)} async-done(((f32[2048,2,4096]{2,0,1:T(8,128)}), f32[128,2,4096]{2,0,1:T(8,128)}) %reduce-scatter.17.cloned.1.call-update) | async-done | bytes 4194320 | tf_op jit(solution)/shard_map/reduce_scatter | solution.py:228
  1590.8 14.0 multiply_subtract_fusion
  1604.8 5.2 copy.131
  1610.1 5.2 copy.132
  1620.6 5.2 copy.127
  (196 shorter events, 122.1 us)
Async XLA Ops:
  7.2 81.4 %copy-start = (f32[128,2048]{1,0:T(8,128)S(1)}, f32[128,2048]{1,0:T(8,128)}, u32[]{:S(2)}) copy-start(f32[128,2048]{1,0:T(8,128)} %param.12) | copy-start | bytes 3145732
  7.2 92.2 %all-gather.15.cloned.1.call-start = ((), (), s32[]{:S(2)}) async-start(), calls=%async_computation.11 | async-start | bytes 1572864 | tf_op jit(solution)/shard_map/all_gather | solution.py:167
  10.4 155.4 %all-gather.9.cloned.1.call-start = ((), (), s32[]{:S(2)}) async-start(), calls=%async_computation.7 | async-start | bytes 17825792 | tf_op jit(solution)/shard_map/all_gather | solution.py:116
  14.1 173.2 %all-gather.7.cloned.1.call-start = ((), (), s32[]{:S(2)}) async-start(), calls=%async_computation.6 | async-start | bytes 1572864 | tf_op jit(solution)/shard_map/all_gather | solution.py:132
  91.1 150.9 %all-gather.11.cloned.1.call-start = ((), (), s32[]{:S(2)}) async-start(), calls=%async_computation.8 | async-start | bytes 1572864 | tf_op jit(solution)/shard_map/all_gather | solution.py:133
  91.7 289.0 %all-gather.13.cloned.1.call-start = ((), (), s32[]{:S(2)}) async-start(), calls=%async_computation.9 | async-start | bytes 35651584 | tf_op jit(solution)/shard_map/all_gather | solution.py:117
  97.8 359.4 %reduce-scatter.11.cloned.1.call-start = ((), (), s32[]{:S(2)}) async-start(), calls=%async_computation.12 | async-start | bytes 3145728 | tf_op jit(solution)/shard_map/reduce_scatter | solution.py:204
  99.3 106.1 %copy-start.23 = (f32[256,32]{0,1:T(8,128)}, f32[256,32]{0,1:T(8,128)S(1)}, u32[]{:S(2)}) copy-start(f32[256,32]{0,1:T(8,128)S(1)} %get-tuple-element.104) | copy-start | bytes 98308
  99.3 106.1 %copy-start.24 = (f32[256,32]{0,1:T(8,128)}, f32[256,32]{0,1:T(8,128)S(1)}, u32[]{:S(2)}) copy-start(f32[256,32]{0,1:T(8,128)S(1)} %get-tuple-element.105) | copy-start | bytes 98308
  236.9 143.8 %copy-start.36 = (f32[4096]{0:T(1024)S(1)}, f32[4096]{0:T(1024)}, u32[]{:S(2)}) copy-start(f32[4096]{0:T(1024)} %dynamic_slice.11) | copy-start | bytes 49156
  241.9 215.3 %reduce-scatter.13.cloned.1.call-start = ((), (), s32[]{:S(2)}) async-start(), calls=%async_computation.13 | async-start | bytes 3145728 | tf_op jit(solution)/shard_map/reduce_scatter | solution.py:205
  401.5 12.8 copy-start.30
  413.9 144.9 %reduce-scatter.9.cloned.1.call-start = ((), (), s32[]{:S(2)}) async-start(), calls=%async_computation.10 | async-start | bytes 3145728 | tf_op jit(solution)/shard_map/reduce_scatter | solution.py:165
  416.6 12.9 copy-start.13
  435.1 189.4 %reduce-scatter.19.cloned.1.call-start = ((), (), s32[]{:S(2)}) async-start(), calls=%async_computation.16 | async-start | bytes 1081344
  461.1 493.8 %reduce-scatter.15.cloned.1.call-start = ((), (), s32[]{:S(2)}) async-start(), calls=%async_computation.14 | async-start | bytes 35651584 | tf_op jit(solution)/shard_map/reduce_scatter | solution.py:213
  484.7 16.1 copy-start.17
  484.7 1106.2 %reduce-scatter.17.cloned.1.call-start = ((), (), s32[]{:S(2)}) async-start(), calls=%async_computation.15 | async-start | bytes 71303168 | tf_op jit(solution)/shard_map/reduce_scatter | solution.py:228
  485.9 14.9 copy-start.6
  558.7 66.6 %copy-start.32 = (f32[12,64]{1,0:T(8,128)S(1)}, f32[12,64]{1,0:T(8,128)}, u32[]{:S(2)}) copy-start(f32[12,64]{1,0:T(8,128)} %param.17) | copy-start | bytes 9220
  558.7 66.6 %copy-start.39 = (f32[12,64]{1,0:T(8,128)S(1)}, f32[12,64]{1,0:T(8,128)}, u32[]{:S(2)}) copy-start(f32[12,64]{1,0:T(8,128)} %param.22) | copy-start | bytes 9220
  558.7 66.6 %copy-start.40 = (f32[12,64]{1,0:T(8,128)S(1)}, f32[12,64]{1,0:T(8,128)}, u32[]{:S(2)}) copy-start(f32[12,64]{1,0:T(8,128)} %param.23) | copy-start | bytes 9220
  558.7 396.2 %copy-start.3 = (f32[128,4,1024]{2,1,0:T(4,128)S(1)}, f32[128,4,1024]{2,1,0:T(4,128)}, u32[]{:S(2)}) copy-start(f32[128,4,1024]{2,1,0:T(4,128)} %param.15) | copy-start | bytes 6291460
  625.3 337.0 %copy-start.33 = (f32[12,64]{1,0:T(8,128)}, f32[12,64]{1,0:T(8,128)S(1)}, u32[]{:S(2)}) copy-start(f32[12,64]{1,0:T(8,128)S(1)} %copy.143) | copy-start | bytes 9220
  (32 other events, 165.2 us)
Sparse Core Ops, SparseCore 0:
  10.5 25.2 all-gather.14
  38.5 127.1 all-gather.8
  167.9 19.4 all-gather.6
  189.3 21.2 all-gather.10
  212.6 168.0 all-gather.12
  383.4 31.8 reduce-scatter.10
  418.1 31.8 reduce-scatter.12
  452.8 31.8 reduce-scatter.8
  487.6 136.7 reduce-scatter.18
  628.5 326.2 reduce-scatter.14
  959.1 631.6 reduce-scatter.16
where the time goes:
time: 1640 us; the launch traced here: 1630 us
  waiting for transfers between devices  1220 us (74%)
  matrix products  141 us (9%)
  other arithmetic  108 us (7%)
  local copies, waits for them, and re-layouts  75.2 us (5%)
  blocking collectives  74.2 us (5%)
    reduce_scatter x1, waiting for transfers between devices, body(): lax.psum_scatter(jnp.stack([jnp.einsum('sc,sn->cn', full_two, d_pre_low,...  618 us
    reduce_scatter x1, waiting for transfers between devices, body(): lax.psum_scatter(jnp.stack([jnp.einsum('sc,sn->cn', full_one, dq_low, pre...  329 us
    all_gather x1, waiting for transfers between devices, body(): lax.all_gather(mlp_weight.astype(bf16_type), 'dp', axis=0, tiled=True)  139 us
    all_gather x1, blocking collectives, body(): lax.all_gather(small_params, ('dp', 'tensor'), axis=1, tiled=True)  74.2 us
    all_gather x1, waiting for transfers between devices, body(): lax.all_gather(attn_weight.astype(bf16_type), 'dp', axis=0, tiled=True)  66.3 us
    unnamed x12, waiting for transfers between devices  61.5 us
    unnamed x110, local copies, waits for them, and re-layouts  51.6 us
    another operation x1, other arithmetic, body(): jnp.stack([jnp.einsum('sc,sn->cn', full_two, d_pre_low, preferred_element...  44.7 us
  transfers between devices with their start and end apart: 11, of which 6 were waited for; matrix products, arithmetic and copies ran while one was open for 17% of the time, Pallas kernels for 0%

commit v1 on v0

v1 whole, which is shorter than its diff:
```python
import functools

import jax
import jax.numpy as jnp
from jax import lax
from jax.experimental import pallas as pl
from jax.experimental.pallas import tpu as pltpu
from jax.sharding import PartitionSpec as P

ROT = 64
ADAM_STEP = 3
HEAD_DIM = 256
Z = 4

norm_epsilon = 1e-05
learn_rate = 0.006
beta_first = 0.9
beta_second = 0.95
adam_epsilon = 1e-08
weight_decay = 0.1

f32 = jnp.float32
bf16 = jnp.bfloat16


def layer_stats(row_data):
    center = row_data - jnp.mean(row_data, axis=-1, keepdims=True)
    inverse = lax.rsqrt(jnp.mean(center * center, axis=-1, keepdims=True) + norm_epsilon)
    return (center * inverse, inverse)


def angle_tables(places):
    half_dims = ROT // 2
    frequency = 10000.0 ** (-(jnp.arange(half_dims).astype(f32) * (2.0 / ROT)))
    angles = places[..., None] * frequency
    return (jnp.cos(angles), jnp.sin(angles))


def rotate(values, cos_table, sin_table):
    half_dims = ROT // 2
    low_half = values[..., :half_dims]
    high_half = values[..., half_dims:ROT]
    return jnp.concatenate(
        [
            low_half * cos_table - high_half * sin_table,
            high_half * cos_table + low_half * sin_table,
            values[..., ROT:],
        ],
        axis=-1,
    )


def gelu_exact(pre_act):
    return 0.5 * pre_act * (1.0 + lax.erf(pre_act * 0.7071067811865476))


def gelu_slope(pre_act):
    return (
        0.5 * (1.0 + lax.erf(pre_act * 0.7071067811865476))
        + pre_act * jnp.exp(-0.5 * pre_act * pre_act) * 0.3989422804014327
    )


def adam_step(weight, gradient, moment_one, moment_two):
    one_new = beta_first * moment_one + (1.0 - beta_first) * gradient
    two_new = beta_second * moment_two + (1.0 - beta_second) * gradient * gradient
    corrected = (
        one_new
        / (1.0 - beta_first**ADAM_STEP)
        / (jnp.sqrt(two_new / (1.0 - beta_second**ADAM_STEP)) + adam_epsilon)
    )
    return (weight - learn_rate * (corrected + weight_decay * weight), one_new, two_new)


class Grid:
    def __init__(self, dp, tensor):
        assert tensor == 2 and dp % (2 * Z) == 0
        self.dp, self.m = dp, dp // (2 * Z)
        index = lax.axis_index("dp")
        self.index = index * 2 + lax.axis_index("tensor")
        self.z_now = index // (2 * self.m)
        self.m_now = (index // 2) % self.m
        self.c_now = index % 2
        self.t_now = lax.axis_index("tensor")
        self.diag = self.c_now == self.t_now


def split_kernel(attn, mlp, qk, vo, up, dn):
    quarter_a = attn.shape[2] // Z
    quarter_m = mlp.shape[2] // Z
    for q in range(Z):
        for j in range(4):
            block = attn[:, j, q * quarter_a : (q + 1) * quarter_a].astype(bf16)
            (qk, qk, vo, vo)[j][q, :, (j % 2) * quarter_a : (j % 2 + 1) * quarter_a] = block
        for j in range(2):
            (up, dn)[j][q] = mlp[:, j, q * quarter_m : (q + 1) * quarter_m].astype(bf16)


def split_weights(attn_weight, mlp_weight):
    rows, _, width = attn_weight.shape
    hidden = mlp_weight.shape[2]
    step = min(rows, 32)
    shapes = [2 * width // Z] * 2 + [hidden // Z] * 2
    return pl.pallas_call(
        split_kernel,
        grid=(rows // step,),
        in_specs=[
            pl.BlockSpec((step, 4, width), lambda i: (i, 0, 0)),
            pl.BlockSpec((step, 2, hidden), lambda i: (i, 0, 0)),
        ],
        out_specs=[pl.BlockSpec((Z, step, n), lambda i: (0, i, 0)) for n in shapes],
        out_shape=[jax.ShapeDtypeStruct((Z, rows, n), bf16) for n in shapes],
        name="split_weights",
    )(attn_weight, mlp_weight)


MESH = pl.DeviceIdType.MESH
M_FIRST = (True, False, True, False)


class Links:
    def __init__(self, m_size):
        self.m_size = m_size
        index = lax.axis_index("dp")
        self.z, self.m, self.c = index // (2 * m_size), (index // 2) % m_size, index % 2
        self.t = lax.axis_index("tensor")
        self.sends = []

    def to(self, z=None, m=None, c=None, t=None):
        z, m, c = (own if v is None else v for v, own in ((z, self.z), (m, self.m), (c, self.c)))
        return ((z * self.m_size + m) * 2 + c, self.t if t is None else t)

    def copy(self, src, dst, send_sem, recv_sem, target):
        return pltpu.make_async_remote_copy(
            src_ref=src, dst_ref=dst, send_sem=send_sem, recv_sem=recv_sem, device_id=target, device_id_type=MESH
        )

    def send(self, src, dst, send_sem, recv_sem, target):
        one = self.copy(src, dst, send_sem, recv_sem, target)
        one.start()
        self.sends.append(one)

    def landed(self, dst, recv_sem):
        self.copy(dst, dst, recv_sem, recv_sem, self.to(c=1 - self.c)).wait_recv()

    def drain(self):
        for one in self.sends:
            one.wait_send()

    def partners(self):
        other = 1 - self.t
        out = [self.to(z=self.z ^ k) for k in range(1, Z)]
        out += [self.to(m=self.m ^ j) for j in range(1, self.m_size)]
        out += [self.to(c=1 - self.c), self.to(t=other), self.to(c=1 - self.c, t=other)]
        return out

    def meet(self):
        barrier = pltpu.get_barrier_semaphore()
        everyone = self.partners()
        for target in everyone:
            pl.semaphore_signal(barrier, inc=1, device_id=target, device_id_type=MESH)
        pl.semaphore_wait(barrier, len(everyone))


def gather_kernel(m_size, *refs):
    pieces, low, mine_small = refs[:4], refs[4], refs[5]
    full, act, table = refs[6:10], refs[10], refs[11]
    stage, stage_m = refs[12:16], refs[16:20]
    (zs, zr, ps, pr, ms, mr, near_s, far_s, xr, as_, ar, ws, wr, ss, sr) = refs[20:35]
    bounce, bounce_low, lin, lout = refs[35:39], refs[39], refs[40], refs[41]
    net = Links(m_size)
    z, m, c, t = net.z, net.m, net.c, net.t
    rows = pieces[0].shape[1]
    half = low.shape[1]
    role = lax.rem(c + t, 2)

    def by_role(do):
        @pl.when(role == 0)
        def _():
            do(True)

        @pl.when(role == 1)
        def _():
            do(False)

    def block(zz, mm, cc, count=1):
        start = ((zz * m_size + mm) * 2 + cc) * rows
        return pl.ds(pl.multiple_of(start, rows), count * rows)

    own_place = pl.ds(pl.multiple_of(z * 2 * half + t * half, half), half)
    place = lambda zz, h: pl.ds(pl.multiple_of(zz * 2 * half + (t ^ h) * half, half), half)

    loads = [pltpu.make_async_copy(pieces[ch].at[z], bounce[ch], lin.at[ch]) for ch in range(4)]
    loads.append(pltpu.make_async_copy(low.at[0], bounce_low, lin.at[4]))
    stores = [pltpu.make_async_copy(bounce[ch], full[ch].at[block(z, m, c)], lout.at[ch]) for ch in range(4)]
    stores.append(pltpu.make_async_copy(bounce_low, act.at[0, own_place], lout.at[4]))

    def load_own(diag):
        if diag:
            for one in loads:
                one.start()

    by_role(load_own)
    net.meet()

    near = net.copy(low.at[1], act.at[1, own_place], near_s, xr.at[0], net.to(c=1 - c))
    far = [
        net.copy(low.at[0], act.at[0, own_place], near_s, xr.at[1], net.to(t=1 - t)),
        net.copy(low.at[1], act.at[1, own_place], far_s, xr.at[1], net.to(c=1 - c, t=1 - t)),
    ]

    def rows_out(diag):
        if diag:
            near.start()
        else:
            for one in far:
                one.start()

    by_role(rows_out)

    steps = [(1, net.to(t=1 - t)), (2, net.to(c=1 - c))]
    j = 1
    while j < m_size:
        steps.append((4 * j, net.to(m=m ^ j)))
        j *= 2
    steps += [(4 * m_size, net.to(z=z ^ 1)), (8 * m_size, net.to(z=z ^ 3))]
    flat = ((z * m_size + m) * 2 + c) * 2 + t
    small_own = pltpu.make_async_copy(mine_small, table.at[flat], ss.at[len(steps)])
    small_own.start()
    state = {"small": 0}

    def small_send():
        i = state["small"]
        if i < len(steps):
            size, target = steps[i]
            span = table.at[pl.ds(flat // size * size, size)]
            net.send(span, span, ss.at[i], sr.at[i], target)

    def small_next():
        i = state["small"]
        if i < len(steps):
            size = steps[i][0]
            net.landed(table.at[pl.ds((flat // size ^ 1) * size, size)], sr.at[i])
            state["small"] += 1
            small_send()

    def spot(diag, ch, zz, j):
        if diag:
            return full[ch].at[block(zz, m ^ j, c)]
        return stage_m[ch].at[m ^ j, zz] if j else stage[ch].at[zz]

    order = [(ch, k) for ch in range(4) for k in (0, 1, 3, 2)]

    def quarters_out(diag):
        for ch, k in order:
            if k:
                net.copy(
                    pieces[ch].at[z ^ k], spot(diag, ch, z, 0), zs.at[ch, k], zr.at[ch, k], net.to(z=z ^ k)
                ).start()

    by_role(quarters_out)
    small_own.wait()
    small_send()

    def store_own(diag):
        if diag:
            for load, store in zip(loads, stores):
                load.wait()
                store.start()

    by_role(store_own)

    def source(diag, ch, k, j):
        return pieces[ch].at[z] if k == 0 and j == 0 else spot(diag, ch, z ^ k, j)

    def spread(diag, ch, k, j):
        src = source(diag, ch, k, j)
        dst = full[ch].at[block(z ^ k, m ^ j, c)]
        net.copy(src, dst, ps.at[ch, j, k, 1], pr.at[ch, j, k, c], net.to(c=t, t=1 - t)).start()
        if not diag:
            net.copy(src, dst, ps.at[ch, j, k, 0], pr.at[ch, j, k, c], net.to(c=1 - c)).start()

    def spread_landed(diag, ch, k, j):
        for cc in (1 - c,) if diag else (1 - c, c):
            net.landed(full[ch].at[block(z ^ k, m ^ j, cc)], pr.at[ch, j, k, cc])

    def first(ch, k):
        def do(diag):
            if k:
                net.landed(spot(diag, ch, z ^ k, 0), zr.at[ch, k])
            if M_FIRST[ch]:
                for j in range(1, m_size):
                    dst = full[ch].at[block(z ^ k, m, c)] if diag else stage_m[ch].at[m, z ^ k]
                    net.copy(
                        source(diag, ch, k, 0), dst, ms.at[ch, j, k], mr.at[ch, j, k], net.to(m=m ^ j)
                    ).start()
            spread(diag, ch, k, 0)

        by_role(do)

    def second(ch, k):
        def do(diag):
            if M_FIRST[ch]:
                for j in range(1, m_size):
                    net.landed(spot(diag, ch, z ^ k, j), mr.at[ch, j, k])
                    spread(diag, ch, k, j)
            else:
                if diag and k == 0:
                    stores[ch].wait()
                spread_landed(diag, ch, k, 0)
                both = full[ch].at[block(z ^ k, m, 0, 2)]
                for j in range(1, m_size):
                    net.copy(both, both, ms.at[ch, j, k], mr.at[ch, j, k], net.to(m=m ^ j)).start()

        by_role(do)

    def third(ch, k):
        def do(diag):
            if M_FIRST[ch]:
                for j in range(m_size):
                    spread_landed(diag, ch, k, j)
                if diag and k == 0:
                    stores[ch].wait()
            else:
                for j in range(1, m_size):
                    net.landed(full[ch].at[block(z ^ k, m ^ j, 0, 2)], mr.at[ch, j, k])

        by_role(do)

    def drain(ch, k):
        def do(diag):
            if k:
                src = pieces[ch].at[z ^ k]
                net.copy(src, src, zs.at[ch, k], zr.at[ch, k], net.to(z=z ^ k)).wait_send()
            if M_FIRST[ch]:
                src = source(diag, ch, k, 0)
            else:
                src = full[ch].at[block(z ^ k, m, 0, 2)]
            for j in range(1, m_size):
                net.copy(src, src, ms.at[ch, j, k], mr.at[ch, j, k], net.to(m=m ^ j)).wait_send()
            for j in range(m_size if M_FIRST[ch] else 1):
                src = source(diag, ch, k, j)
                for side in (1,) if diag else (1, 0):
                    net.copy(src, src, ps.at[ch, j, k, side], pr.at[ch, j, k, 0], net.to(c=1 - c)).wait_send()

        by_role(do)

    own_first = [p for p in order if p[1] == 0] + [p for p in order if p[1]]

    def rows_start(h):
        def do(diag):
            if h:
                net.landed(act.at[0 if diag else 1, place(z, 1)], xr.at[1])
            elif diag:
                stores[4].wait()
            else:
                net.landed(act.at[1, place(z, 0)], xr.at[0])

        by_role(do)
        src = act.at[role, place(z, h)]
        net.send(src, src, as_.at[h, 0], ar.at[h, 0], net.to(z=z ^ 3))
        net.send(src, src, as_.at[h, 1], ar.at[h, 1], net.to(z=z ^ 1))
        net.send(src, src, ws.at[0, h], wr.at[0, h], net.to(c=1 - c))

    def rows_far(h):
        src = act.at[role, place(z ^ 3, h)]
        net.landed(src, ar.at[h, 0])
        net.send(src, src, as_.at[h, 2], ar.at[h, 2], net.to(z=z ^ 1))
        net.send(src, src, ws.at[3, h], wr.at[3, h], net.to(c=1 - c))

    def rows_last(h, k):
        src = act.at[role, place(z ^ k, h)]
        net.landed(src, ar.at[h, k])
        net.send(src, src, ws.at[k, h], wr.at[k, h], net.to(c=1 - c))

    for ch, k in own_first[:4]:
        first(ch, k)
    small_next()
    rows_start(0)
    small_next()
    rows_start(1)
    small_next()
    pending = list(own_first[:4])
    for i, (ch, k) in enumerate(own_first[4:]):
        first(ch, k)
        pending.append((ch, k))
        if len(pending) > 3:
            second(*pending.pop(0))
        if i % 3 == 2:
            small_next()
    rows_far(0)
    while pending:
        second(*pending.pop(0))
    while state["small"] < len(steps):
        small_next()
    rows_far(1)
    for h in range(2):
        rows_last(h, 1)
    for ch, k in own_first:
        third(ch, k)
    for h in range(2):
        rows_last(h, 2)
    for k in (0, 3, 1, 2):
        for h in range(2):
            net.landed(act.at[1 - role, place(z ^ k, h)], wr.at[k, h])
    net.drain()
    for ch, k in order:
        drain(ch, k)

    def rows_drain(diag):
        if diag:
            near.wait_send()
        else:
            for one in far:
                one.wait_send()

    by_role(rows_drain)


def gather(pieces, low, small, m_size):
    rows = pieces[0].shape[1]
    width = low.shape[2]
    devices = m_size * 4 * Z
    cols = [p.shape[2] for p in pieces]
    stages = [jax.ShapeDtypeStruct((Z, rows, n), bf16) for n in cols]
    stages_m = [jax.ShapeDtypeStruct((m_size, Z, rows, n), bf16) for n in cols]
    sem = pltpu.SemaphoreType.DMA
    doubling = m_size.bit_length() - 1 + 4
    outs = pl.pallas_call(
        functools.partial(gather_kernel, m_size),
        out_shape=[jax.ShapeDtypeStruct((width, n), bf16) for n in cols]
        + [
            jax.ShapeDtypeStruct((2, Z * 2 * low.shape[1], width), bf16),
            jax.ShapeDtypeStruct((devices,) + small.shape, f32),
        ]
        + stages
        + stages_m,
        in_specs=[pl.BlockSpec(memory_space=pl.ANY)] * 6,
        out_specs=[pl.BlockSpec(memory_space=pl.ANY)] * 14,
        scratch_shapes=[
            sem((4, Z)),
            sem((4, Z)),
            sem((4, m_size, Z, 2)),
            sem((4, m_size, Z, 2)),
            sem((4, m_size, Z)),
            sem((4, m_size, Z)),
            sem,
            sem,
            sem((2,)),
            sem((2, 3)),
            sem((2, 3)),
            sem((Z, 2)),
            sem((Z, 2)),
            sem((doubling + 1,)),
            sem((doubling,)),
        ]
        + [pltpu.VMEM((rows, n), bf16) for n in cols]
        + [pltpu.VMEM(low.shape[1:], bf16), sem((5,)), sem((5,))],
        compiler_params=pltpu.CompilerParams(collective_id=0, has_side_effects=True),
        name="gather_all",
    )(*pieces, low, small)
    return outs[:4], outs[4], outs[5]


def out_kernel(blocks, scalar, y_ref, one, two, plain, par, keep, send, sums):
    diag = scalar[blocks] == 1

    @pl.when(pl.program_id(0) == 0)
    def _():
        sums[...] = jnp.zeros_like(sums)

    for p in range(blocks):
        dst = pl.ds(pl.multiple_of(scalar[p] * 128, 128), 128)
        src = slice(p * 128, (p + 1) * 128)
        y, d_one, d_two = y_ref[:, src], one[:, src], two[:, src]
        x = plain[:, src].astype(f32)
        u = d_one * par[0:1, dst] + d_two * par[2:3, dst]
        keep[:, dst] = jnp.where(diag, y, u).astype(bf16)
        send[:, dst] = jnp.where(diag, u, y).astype(bf16)
        rows = [jnp.sum(v, axis=0, keepdims=True) for v in (d_one * x, d_one, d_two * x, d_two)]
        for i, row in enumerate(rows):
            sums[i : i + 1, dst] += row


def place_outs(y, d_one, d_two, plain, par, order, diag):
    rows, width = y.shape
    blocks = order.shape[0]
    if (width // blocks) % 128:
        back = jnp.argsort(order)
        take = lambda v: jnp.take(v.reshape(v.shape[0], blocks, -1), back, axis=1).reshape(v.shape)
        y, d_one, d_two, x = take(y), take(d_one), take(d_two), take(plain).astype(f32)
        u = d_one * par[0] + d_two * par[2]
        sums = jnp.stack([jnp.sum(v, axis=0) for v in (d_one * x, d_one, d_two * x, d_two)])
        return jnp.where(diag, y, u).astype(bf16), jnp.where(diag, u, y).astype(bf16), sums
    per = width // 128 // blocks
    order = (order[:, None] * per + jnp.arange(per)[None]).reshape(-1)
    blocks = blocks * per
    step = 256
    spec = pl.BlockSpec((step, width), lambda i, s: (i, 0))
    whole = pl.BlockSpec((4, width), lambda i, s: (0, 0))
    return pl.pallas_call(
        functools.partial(out_kernel, blocks),
        grid_spec=pltpu.PrefetchScalarGridSpec(
            num_scalar_prefetch=1,
            grid=(rows // step,),
            in_specs=[spec] * 4 + [whole],
            out_specs=[spec, spec, whole],
        ),
        out_shape=[jax.ShapeDtypeStruct((rows, width), bf16)] * 2
        + [jax.ShapeDtypeStruct((4, width), f32)],
        name="place_outs",
    )(
        jnp.concatenate([order, diag.astype(jnp.int32).reshape(1)]).astype(jnp.int32),
        y,
        d_one,
        d_two,
        plain,
        par,
    )


def add_rows(dst, sources):
    step = min(dst.shape[0], 32)

    @pl.loop(0, dst.shape[0] // step)
    def _(i):
        span = pl.ds(pl.multiple_of(i * step, step), step)
        total = sources[0][span, :].astype(f32)
        for one in sources[1:]:
            total = total + one[span, :].astype(f32)
        dst[span, :] = total.astype(dst.dtype)


def scatter_kernel(m_size, *refs):
    grads, keep, give, terms = refs[:4], refs[4], refs[5], refs[6]
    own, rows_out, small_out = refs[7:11], refs[11], refs[12]
    home_first, x_first, mid_first, far_first, sum_first = (refs[13 + 2 * i : 15 + 2 * i] for i in range(5))
    own_last, far_last, sum_last, home_last, x_last, sum_far = (refs[23 + 2 * i : 25 + 2 * i] for i in range(6))
    got, kept, total, got_z, three, final, current, got_small = refs[35:43]
    (cl, cs, cr, fs, fr, zs, zr, zl, dl, ds_, dr, es, er, kl, gs, gr, ys, yr, rs, rr, rl, ss, sr) = refs[43:]
    net = Links(m_size)
    z, m, c, t = net.z, net.m, net.c, net.t
    half = rows_out.shape[1]
    role = lax.rem(c + t, 2)
    first_chunks = [ch for ch in range(4) if M_FIRST[ch]]
    last_chunks = [ch for ch in range(4) if not M_FIRST[ch]]
    pairs_first = [(i, ch) for i, ch in enumerate(first_chunks)]
    pairs_last = [(i, ch) for i, ch in enumerate(last_chunks)]
    ks = (3, 2, 1, 0)

    def by_role(do):
        @pl.when(role == 0)
        def _():
            do(True)

        @pl.when(role == 1)
        def _():
            do(False)

    loads_keep = [pltpu.make_async_copy(keep.at[z ^ k], kept.at[k], kl.at[k]) for k in range(Z)]
    loads_last = {
        (i, k): pltpu.make_async_copy(grads[ch].at[z ^ k, m], own_last[i].at[k], dl.at[i, k])
        for i, ch in pairs_last
        for k in ks
    }
    loads_first = {
        (i, j, k): pltpu.make_async_copy(grads[ch].at[z ^ k, m ^ j, c], home_first[i].at[j, k], cl.at[i, j, k])
        for i, ch in pairs_first
        for j in range(m_size)
        for k in ks
    }
    for one in loads_keep:
        one.start()
    for one in loads_last.values():
        one.start()

    def load_first(diag):
        if diag:
            for one in loads_first.values():
                one.start()

    by_role(load_first)
    current[...] = terms[...]
    net.meet()

    flat = ((z * m_size + m) * 2 + c) * 2 + t
    steps = [(1, net.to(t=1 - t)), (2, net.to(c=1 - c))]
    j = 1
    while j < m_size:
        steps.append((4 * j, net.to(m=m ^ j)))
        j *= 2
    steps += [(4 * m_size, net.to(z=z ^ 1)), (8 * m_size, net.to(z=z ^ 3))]
    steps = steps[::-1]
    state = {"small": 0}

    def small_send():
        i = state["small"]
        if i < len(steps):
            size, target = steps[i]
            net.send(
                current.at[pl.ds((flat // size ^ 1) * size, size)],
                got_small.at[pl.ds(size, size)],
                ss.at[i],
                sr.at[i],
                target,
            )

    def small_next():
        i = state["small"]
        if i < len(steps):
            size = steps[i][0]
            net.landed(got_small.at[pl.ds(size, size)], sr.at[i])
            span = pl.ds(flat // size * size, size)
            current[span] = current[span] + got_small[pl.ds(size, size)]
            state["small"] += 1
            small_send()

    for k in (1, 2, 3, 0):
        net.send(give.at[z ^ k], got.at[k], gs.at[k], gr.at[k], net.to(c=1 - c))
    small_send()

    def to_owner(diag, source, home, far, sems, i, jk):
        send_sem, recv_sem = sems
        if diag:
            net.copy(source(1 - c), home, send_sem.at[i, *jk, 0], recv_sem.at[i, *jk, 0], net.to(c=1 - c)).start()
        else:
            net.copy(source(c), far, send_sem.at[i, *jk, 0], recv_sem.at[i, *jk, 1], net.to(t=1 - t)).start()
            net.copy(
                source(1 - c), far, send_sem.at[i, *jk, 1], recv_sem.at[i, *jk, 1], net.to(c=1 - c, t=1 - t)
            ).start()

    def collect_first(i, ch, j, k):
        def do(diag):
            to_owner(
                diag,
                lambda cc: grads[ch].at[z ^ k, m ^ j, cc],
                home_first[i].at[j, k],
                x_first[i].at[j, k],
                (cs, cr),
                i,
                (j, k),
            )

        by_role(do)

    for k in ks:
        for i, ch in pairs_last:
            for j in range(1, m_size):
                net.send(grads[ch].at[z ^ k, m ^ j], far_last[i].at[j - 1, k], ds_.at[i, j, k], dr.at[i, j, k], net.to(m=m ^ j))
        for i, ch in pairs_first:
            for j in range(1, m_size):
                collect_first(i, ch, j, k)
    for k in ks:
        for i, ch in pairs_first:
            collect_first(i, ch, 0, k)

    def collected_first(i, j, k):
        def do(diag):
            if diag:
                loads_first[i, j, k].wait()
            else:
                net.landed(home_first[i].at[j, k], cr.at[i, j, k, 0])

        by_role(do)
        net.landed(x_first[i].at[j, k], cr.at[i, j, k, 1])

    for one in loads_keep:
        one.wait()
    for k in (1, 2, 3, 0):
        net.landed(got.at[k], gr.at[k])
        add_rows(total.at[k], [kept.at[k], got.at[k]])
        if k in (1, 2):
            net.send(total.at[k], got_z.at[k - 1], ys.at[k], yr.at[k], net.to(z=z ^ 1))
    small_next()

    def to_z(ch, tile, k):
        if k:
            net.send(tile, own[ch].at[z], zs.at[ch, k], zr.at[ch, k], net.to(z=z ^ k))
        else:
            pltpu.make_async_copy(tile, own[ch].at[z], zl.at[ch]).start()

    def middle(k):
        for i, ch in pairs_first:
            for j in range(1, m_size):
                collected_first(i, j, k)
                add_rows(mid_first[i].at[j - 1, k], [home_first[i].at[j, k], x_first[i].at[j, k]])
                net.send(mid_first[i].at[j - 1, k], far_first[i].at[j - 1, k], fs.at[i, j, k], fr.at[i, j, k], net.to(m=m ^ j))
        for i, ch in pairs_last:
            loads_last[i, k].wait()
            for j in range(1, m_size):
                net.landed(far_last[i].at[j - 1, k], dr.at[i, j, k])
            for cc in range(2):
                add_rows(
                    sum_last[i].at[k, cc],
                    [own_last[i].at[k, cc]] + [far_last[i].at[j - 1, k, cc] for j in range(1, m_size)],
                )

            def do(diag):
                to_owner(
                    diag,
                    lambda cc: sum_last[i].at[k, cc],
                    home_last[i].at[k],
                    x_last[i].at[k],
                    (es, er),
                    i,
                    (k,),
                )

            by_role(do)

    def finish(k):
        for i, ch in pairs_first:
            collected_first(i, 0, k)
            for j in range(1, m_size):
                net.landed(far_first[i].at[j - 1, k], fr.at[i, j, k])
            add_rows(
                sum_first[i].at[k],
                [home_first[i].at[0, k], x_first[i].at[0, k]] + [far_first[i].at[j - 1, k] for j in range(1, m_size)],
            )
            to_z(ch, sum_first[i].at[k], k)
        for i, ch in pairs_last:

            def do(diag):
                net.landed(x_last[i].at[k], er.at[i, k, 1])
                if diag:
                    add_rows(sum_far[i].at[k], [sum_last[i].at[k, c], x_last[i].at[k]])
                else:
                    net.landed(home_last[i].at[k], er.at[i, k, 0])
                    add_rows(sum_far[i].at[k], [home_last[i].at[k], x_last[i].at[k]])

            by_role(do)
            to_z(ch, sum_far[i].at[k], k)

    middle(3)
    small_next()
    middle(2)
    net.landed(got_z.at[1], yr.at[2])
    add_rows(three, [total.at[3], got_z.at[1]])
    net.send(three, got_z.at[2], ys.at[3], yr.at[3], net.to(z=z ^ 3))
    small_next()
    middle(1)
    finish(3)
    small_next()
    middle(0)
    finish(2)
    while state["small"] < len(steps):
        small_next()
    small_out[...] = current[flat]
    finish(1)
    net.landed(got_z.at[0], yr.at[1])
    net.landed(got_z.at[2], yr.at[3])
    add_rows(final, [total.at[0], got_z.at[0], got_z.at[2]])
    mine = final.at[pl.ds(pl.multiple_of(t * half, half), half)]
    other = final.at[pl.ds(pl.multiple_of((1 - t) * half, half), half)]
    keep_rows = pltpu.make_async_copy(mine, rows_out.at[0], rl)

    def rows_back(diag):
        if diag:
            keep_rows.start()
            net.copy(other, rows_out.at[0], rs.at[0], rr.at[0], net.to(t=1 - t)).start()
        else:
            net.copy(mine, rows_out.at[1], rs.at[0], rr.at[1], net.to(c=1 - c)).start()
            net.copy(other, rows_out.at[1], rs.at[1], rr.at[1], net.to(c=1 - c, t=1 - t)).start()

    by_role(rows_back)
    finish(0)
    for ch in range(4):
        for k in range(1, Z):
            net.landed(own[ch].at[z ^ k], zr.at[ch, k])
        pltpu.make_async_copy(own[ch].at[z], own[ch].at[z], zl.at[ch]).wait()

    def rows_done(diag):
        net.landed(rows_out.at[1], rr.at[1])
        if diag:
            keep_rows.wait()
            net.copy(other, rows_out.at[0], rs.at[0], rr.at[0], net.to(t=1 - t)).wait_send()
        else:
            net.landed(rows_out.at[0], rr.at[0])
            net.copy(mine, rows_out.at[1], rs.at[0], rr.at[1], net.to(c=1 - c)).wait_send()
            net.copy(other, rows_out.at[1], rs.at[1], rr.at[1], net.to(c=1 - c, t=1 - t)).wait_send()

    by_role(rows_done)

    def owners_done(diag):
        for k in ks:
            for side in range(1 if diag else 2):
                for i, ch in pairs_first:
                    for j in range(m_size):
                        src = grads[ch].at[z ^ k, m ^ j, 0]
                        net.copy(src, src, cs.at[i, j, k, side], cr.at[i, j, k, 0], net.to(c=1 - c)).wait_send()
                for i, ch in pairs_last:
                    src = sum_last[i].at[k, 0]
                    net.copy(src, src, es.at[i, k, side], er.at[i, k, 0], net.to(c=1 - c)).wait_send()

    by_role(owners_done)
    net.drain()


def scatter(grads, keep, give, terms, m_size, rows):
    cols = [g.shape[1] for g in grads]
    width = keep.shape[1]
    block = width // (2 * Z * m_size)
    seq = keep.shape[0] // Z
    first = [n for ch, n in enumerate(cols) if M_FIRST[ch]]
    last = [n for ch, n in enumerate(cols) if not M_FIRST[ch]]
    nf, nl = len(first), len(last)
    sem = pltpu.SemaphoreType.DMA
    vmem = lambda *shape: pltpu.VMEM(shape, bf16)
    doubling = m_size.bit_length() - 1 + 4
    any_spec = pl.BlockSpec(memory_space=pl.ANY)
    in_vmem = pl.BlockSpec(memory_space=pltpu.VMEM)
    far = m_size - 1
    outs = pl.pallas_call(
        functools.partial(scatter_kernel, m_size),
        out_shape=[jax.ShapeDtypeStruct((Z, block, n), bf16) for n in cols]
        + [jax.ShapeDtypeStruct((2, rows, width), bf16), jax.ShapeDtypeStruct(terms.shape[1:], f32)],
        in_specs=[any_spec] * 6 + [in_vmem],
        out_specs=[any_spec] * 5 + [in_vmem],
        scratch_shapes=[vmem(m_size, Z, block, n) for n in first] * 2
        + [vmem(far, Z, block, n) for n in first] * 2
        + [vmem(Z, block, n) for n in first]
        + [vmem(Z, 2, block, n) for n in last]
        + [vmem(far, Z, 2, block, n) for n in last]
        + [vmem(Z, 2, block, n) for n in last]
        + [vmem(Z, block, n) for n in last] * 3
        + [vmem(Z, seq, width)] * 3
        + [vmem(3, seq, width), vmem(seq, width), vmem(seq, width)]
        + [pltpu.VMEM(terms.shape, f32)] * 2
        + [
            sem((nf, m_size, Z)),
            sem((nf, m_size, Z, 2)),
            sem((nf, m_size, Z, 2)),
            sem((nf, m_size, Z)),
            sem((nf, m_size, Z)),
            sem((4, Z)),
            sem((4, Z)),
            sem((4,)),
            sem((nl, Z)),
            sem((nl, m_size, Z)),
            sem((nl, m_size, Z)),
            sem((nl, Z, 2)),
            sem((nl, Z, 2)),
            sem((Z,)),
            sem((Z,)),
            sem((Z,)),
            sem((Z,)),
            sem((Z,)),
            sem((2,)),
            sem((2,)),
            sem,
            sem((doubling,)),
            sem((doubling,)),
        ],
        compiler_params=pltpu.CompilerParams(
            collective_id=1, has_side_effects=True, vmem_limit_bytes=60 * 1024 * 1024
        ),
        name="scatter_all",
    )(
        *[g.reshape(Z, m_size, 2, block, -1) for g in grads],
        keep.reshape(Z, seq, width),
        give.reshape(Z, seq, width),
        terms,
    )
    return outs[:4], outs[4], outs[5]


def adam_kernel(per, *refs):
    count = len(refs) - 7
    grads, (weight, one, two), outs = refs[:count], refs[count : count + 3], refs[count + 3 :]
    cols = weight.shape[2]
    for j in range(weight.shape[1]):
        g = grads[j // per][0, :, (j % per) * cols : (j % per + 1) * cols].astype(f32)
        w_new, one_new, two_new = adam_step(weight[:, j, :], g, one[:, j, :], two[:, j, :])
        for ref, value in zip(outs, (g, w_new, one_new, two_new)):
            ref[:, j, :] = value


def adam_update(grads, per, weight, one, two):
    rows, kinds, width = weight.shape
    cols = width // Z
    spec = pl.BlockSpec((rows, kinds, cols), lambda q: (0, 0, q))
    return pl.pallas_call(
        functools.partial(adam_kernel, per),
        grid=(Z,),
        in_specs=[pl.BlockSpec((1, rows, per * cols), lambda q: (q, 0, 0))] * len(grads) + [spec] * 3,
        out_specs=[spec] * 4,
        out_shape=[jax.ShapeDtypeStruct(weight.shape, f32)] * 4,
        name="adam_update",
    )(*grads, weight, one, two)


def body(
    block_in,
    positions,
    out_grad,
    attn_weight,
    mlp_weight,
    small_params,
    attn_first,
    attn_second,
    mlp_first,
    mlp_second,
    small_first,
    small_second,
):
    grid = Grid(lax.axis_size("dp"), lax.axis_size("tensor"))
    z, m, c, t, diag = grid.z_now, grid.m_now, grid.c_now, grid.t_now, grid.diag
    devices = grid.dp * 2
    rows, width = block_in.shape
    seq = 2 * rows
    part = small_params.shape[1]

    normed, inverse = layer_stats(block_in)
    x_low, g_low = normed.astype(bf16), out_grad.astype(bf16)

    pieces = split_weights(attn_weight, mlp_weight)
    tile = -(-12 * part // 1024) * 1024
    small_tile = jnp.concatenate(
        [small_params.reshape(-1), jnp.zeros((tile - 12 * part,), f32), positions[0].astype(f32)]
        + [jnp.zeros((1024 - seq,), f32)]
    ).reshape(-1, 128)
    weights, acts, table = gather(pieces, jnp.stack([x_low, g_low]), small_tile, grid.m)
    w_qk, w_vo, w_up, w_dn = weights
    everyone = table.reshape(devices, -1)
    small_all = jnp.transpose(everyone[:, : 12 * part].reshape(devices, 12, part), (1, 0, 2)).reshape(12, width)
    group = (jnp.arange(Z) * grid.m + m) * 4 + t * 2
    places = jnp.take(everyone[:, tile : tile + seq], group, axis=0)
    plain, grads = acts[0], acts[1]
    x_group = plain.astype(f32)
    one_low = (x_group * small_all[0] + small_all[1]).astype(bf16)
    two_low = (x_group * small_all[2] + small_all[3]).astype(bf16)
    order = jnp.arange(grid.dp)

    head = c * Z + z
    hidden = w_up.shape[1]
    query_bias = lax.dynamic_slice_in_dim(small_all[4], head * HEAD_DIM, HEAD_DIM)
    value_bias = lax.dynamic_slice_in_dim(small_all[5], head * HEAD_DIM, HEAD_DIM)
    up_bias = lax.dynamic_slice_in_dim(small_all[8:12].reshape(-1), head * hidden, hidden)

    dot = functools.partial(jnp.einsum, preferred_element_type=f32)

    cos_table, sin_table = angle_tables(places)
    score_scale = HEAD_DIM ** (-0.5)
    visible = places[:, None, :] <= places[:, :, None]
    qk = dot("sd,dn->sn", one_low, w_qk)
    w_v, w_o = w_vo[:, :HEAD_DIM], w_vo[:, HEAD_DIM:]
    per_seq = lambda v: v.reshape(Z, seq, HEAD_DIM)
    queries = rotate(per_seq(qk[:, :HEAD_DIM] + query_bias), cos_table, sin_table).astype(bf16)
    key_rows = rotate(per_seq(qk[:, HEAD_DIM:]), cos_table, sin_table).astype(bf16)
    values = per_seq((dot("sd,dn->sn", one_low, w_v) + value_bias).astype(bf16))
    scores = dot("nqd,nkd->nqk", queries, key_rows) * score_scale
    scores = jnp.where(visible, scores, -jnp.inf)
    row_max = jnp.max(scores, axis=-1, keepdims=True)
    log_total = row_max + jnp.log(jnp.sum(jnp.exp(scores - row_max), axis=-1, keepdims=True))
    probs = jnp.exp(scores - log_total)
    probs_low = probs.astype(bf16)
    attended = dot("nqk,nkd->nqd", probs_low, values).astype(bf16)
    d_attended = per_seq(dot("sd,dn->sn", grads, w_o).astype(bf16))
    d_probs = dot("nqd,nkd->nqk", d_attended, values)
    d_scores = (probs * (d_probs - jnp.sum(probs * d_probs, axis=-1, keepdims=True)) * score_scale).astype(bf16)
    d_query = rotate(dot("nqk,nkd->nqd", d_scores, key_rows), cos_table, -sin_table)
    d_key = rotate(dot("nqk,nqd->nkd", d_scores, queries), cos_table, -sin_table)
    d_value = dot("nqk,nqd->nkd", probs_low, d_attended)
    flat = lambda v: v.reshape(Z * seq, HEAD_DIM)
    attended, d_query, d_key, d_value = flat(attended), flat(d_query), flat(d_key), flat(d_value)
    dqk_low = jnp.concatenate([d_query, d_key], axis=1).astype(bf16)
    dv_low = d_value.astype(bf16)
    d_one = dot("sn,dn->sd", dqk_low, w_qk) + dot("sn,dn->sd", dv_low, w_v)
    y_attn = dot("sn,dn->sd", attended, w_o)
    grad_qk = dot("sd,sn->dn", one_low, dqk_low).astype(bf16)
    grad_vo = jnp.concatenate(
        [dot("sd,sn->dn", one_low, dv_low).astype(bf16), dot("sd,sn->dn", grads, attended).astype(bf16)], axis=1
    )

    pre_act = dot("sd,dn->sn", two_low, w_up) + up_bias
    activation = gelu_exact(pre_act).astype(bf16)
    d_pre = dot("sd,dn->sn", grads, w_dn) * gelu_slope(pre_act)
    d_pre_low = d_pre.astype(bf16)
    y_part = dot("sn,dn->sd", activation, w_dn) + y_attn
    d_two = dot("sn,dn->sd", d_pre_low, w_up)
    grad_up = dot("sd,sn->dn", two_low, d_pre_low).astype(bf16)
    grad_dn = dot("sd,sn->dn", grads, activation).astype(bf16)

    keep, give, norm_sums = place_outs(y_part, d_one, d_two, plain, small_all[:4], order, diag)
    spread_cols = lambda v, n: lax.dynamic_update_slice_in_dim(
        jnp.zeros((n,), f32), v, head * v.shape[0], 0
    )
    out_sum = jnp.sum(out_grad, axis=0)
    small_terms = jnp.concatenate(
        [
            norm_sums,
            spread_cols(jnp.sum(d_query, axis=0), width)[None],
            spread_cols(jnp.sum(d_value, axis=0), width)[None],
            out_sum[None],
            out_sum[None],
            spread_cols(jnp.sum(d_pre, axis=0), 4 * width).reshape(4, width),
        ],
        axis=0,
    )
    terms = jnp.transpose(small_terms.reshape(12, devices, part), (1, 0, 2)).reshape(devices, 12 * part)
    terms = jnp.pad(terms, ((0, 0), (0, tile - 12 * part))).reshape(devices, -1, 128)
    own, own_rows, own_small = scatter([grad_qk, grad_vo, grad_up, grad_dn], keep, give, terms, grid.m, rows)
    y_rows, u_rows = own_rows[0].astype(f32), own_rows[1].astype(f32)
    block_out = block_in + y_rows + small_all[6] + small_all[7]
    input_grad = out_grad + inverse * (
        u_rows
        - jnp.mean(u_rows, axis=-1, keepdims=True)
        - normed * jnp.mean(u_rows * normed, axis=-1, keepdims=True)
    )
    attn_out = adam_update(own[:2], 2, attn_weight, attn_first, attn_second)
    mlp_out = adam_update(own[2:], 1, mlp_weight, mlp_first, mlp_second)
    small_grad = own_small.reshape(-1)[: 12 * part].reshape(12, part)
    small_new, small_first_new, small_second_new = adam_step(small_params, small_grad, small_first, small_second)

    attn_grad, attn_new, attn_first_new, attn_second_new = attn_out
    mlp_grad, mlp_new, mlp_first_new, mlp_second_new = mlp_out
    return (
        block_out,
        input_grad,
        attn_grad,
        mlp_grad,
        small_grad,
        attn_new,
        attn_first_new,
        attn_second_new,
        mlp_new,
        mlp_first_new,
        mlp_second_new,
        small_new,
        small_first_new,
        small_second_new,
    )


def solution(mesh):
    rows = P(("dp", "tensor"), None)
    weights = P("dp", None, "tensor")
    small = P(None, ("dp", "tensor"))
    return jax.shard_map(
        body,
        mesh=mesh,
        in_specs=(rows, P("dp", None), rows, weights, weights, small, weights, weights, weights, weights, small, small),
        out_specs=(rows, rows) + (weights,) * 2 + (small,) + (weights,) * 6 + (small,) * 3,
        check_vma=False,
    )
```

time: 1640 us -> 565 us (0.34)
  waiting for transfers between devices: 1220 us -> 0 us
  Pallas kernels: 0 us -> 421 us
  other arithmetic: 108 us -> 18 us
  blocking collectives: 74.2 us -> 0 us
  local copies, waits for them, and re-layouts: 75.2 us -> 26.8 us
  matrix products: 141 us -> 93.6 us
    reduce_scatter x5 -> x0, waiting for transfers between devices: 947 us -> none  [the longest x1 618 us: body(): lax.psum_scatter(jnp.stack([jnp.einsum('sc,sn->cn', full_two, d_pre_low,...]
    pallas_call x0 -> x6, Pallas kernels: none -> 421 us  [the longest x1 189 us: gather(): pl.pallas_call(functools.partial(gather_kernel, m_size), out_shape=[jax.S...]
    all_gather x5 -> x0, waiting for transfers between devices: 210 us -> none  [the longest x1 139 us: body(): lax.all_gather(mlp_weight.astype(bf16_type), 'dp', axis=0, tiled=True)]
    all_gather x1 -> x0, blocking collectives: 74.2 us -> none  [body(): lax.all_gather(small_params, ('dp', 'tensor'), axis=1, tiled=True)]
    another operation x3 -> x4, other arithmetic: 69.9 us -> 3.15 us  [the longest x2 2.45 us: body(): jnp.stack([x_low, g_low])]
    unnamed x12 -> x0, waiting for transfers between devices: 61.5 us -> none
    dot_general x24 -> x21, matrix products: 141 us -> 93.6 us  [the longest x1 9.6 us: body(): grad_up = dot('sd,sn->dn', two_low, d_pre_low).astype(bf16)]
    unnamed x110 -> x72, local copies, waits for them, and re-layouts: 51.6 us -> 4.78 us
  transfers between devices with their start and end apart: 11 -> 0, of which waited for: 6 -> 0; matrix products, arithmetic and copies ran while one was open for 17% -> 0% of each run, Pallas kernels for 0% -> 0%
where the time goes in v1:
time: 565 us; the launch traced here: 561 us
  Pallas kernels  421 us (75%)
  matrix products  93.6 us (17%)
  local copies, waits for them, and re-layouts  26.8 us (5%)
  other arithmetic  18 us (3%)
    pallas_call x1, Pallas kernels, gather(): pl.pallas_call(functools.partial(gather_kernel, m_size), out_shape=[jax.S...  189 us
    pallas_call x1, Pallas kernels, scatter(): pl.pallas_call(functools.partial(scatter_kernel, m_size), out_shape=[jax....  182 us
    pallas_call x2, Pallas kernels, adam_update(): pl.pallas_call(functools.partial(adam_kernel, per), grid=(Z,), in_specs=[...  24.4 us
    pallas_call x1, Pallas kernels, place_outs(): pl.pallas_call(functools.partial(out_kernel, blocks), grid_spec=pltpu.Pre...  17.3 us

profile of v1, /device:TPU:0, one launch (start us, length us, event | category | flops | bytes accessed | tf_op | source)
XLA Modules:
  0.0 561.1 jit_solution(456989943998524243)
XLA Ops:
  9.0 8.6 %split_weights.1 = (bf16[4,128,512]{2,1,0:T(8,128)(2,1)}, bf16[4,128,512]{2,1,0:T(8,128)(2,1)}, bf16[4,128,1024]{2,1,0:T(8,128)(2,1)}, bf16[4,128,1024]{2,1,0:T(8,128)(2,1)}) custom-call(f32[128,4,1024]{2,1,0:T(4,128)} %refs_2_.2, f32[128,2,4096]{2,1,0:T(2,128)} %refs_2_.3), custom_call_target="tpu_custom_call" | custom-call | tf_op jit(solution)/shard_map/split_weights/pallas_call | solution.py:104
  17.6 188.8 %gather_all.1 = (bf16[2048,512]{1,0:T(8,128)(2,1)}, bf16[2048,512]{1,0:T(8,128)(2,1)}, bf16[2048,1024]{1,0:T(8,128)(2,1)}, bf16[2048,1024]{1,0:T(8,128)(2,1)}, b...) custom-call(bf16[4,128,512]{2,1,0:T(8,128)(2,1)} %get-tuple-element., ...), custom_call_target="tpu_custom_call" | custom-call | tf_op jit(solution)/shard_map/gather_all/pallas_call | solution.py:429
  210.2 3.9 fusion.56
  214.1 3.7 fusion.60
  219.9 4.5 fusion.45
  232.9 3.8 fusion.72
  236.7 3.9 fusion.73
  251.0 3.5 fusion.37
  254.5 3.5 fusion.34
  260.7 6.2 %convolution_convert_fusion.1 = bf16[2048,512]{1,0:T(8,128)(2,1)} fusion(f32[2048]{0:T(1024)S(1)} %add.213, f32[2048]{0:T(1024)S(1)} %mul.250, bf16[1024,256]{1,0:T(8,128)(2,1)} %bitcast.141, bf16[1024,256]{1,0:T(8,128)(2,1)} %bitcast.139, bf16[2,1024,2048]{2,1,0:T(8,128)(2,1)} %get-tuple-element.45), kind=kOutput, calls=%fused_computation.36 | convolution fusion | flops 2159017984 | bytes 7356416 | tf_op jit(solution)/shard_map/sd,sn->dn/dot_general | solution.py:970
  266.9 4.9 slice_bitcast_fusion.plain
  274.3 5.4 convolution_add_fusion.one
  280.4 6.1 %multiply_convert_fusion = (bf16[1024,1024]{1,0:T(8,128)(2,1)}, f32[1024,1024]{1,0:T(8,128)S(1)}) fusion(f32[1024]{0:T(1024)S(1)} %dynamic_slice.11, bf16[2048,1024]{1,0:T(8,128)(2,1)S(1)} %copy-done.20, f32[2048]{0:T(1024)S(1)} %add.241, f32[2048]{0:T(1024)S(1)} %mul.287, bf16[2,1024,2048]{2,1,0:T(8,128)(2,1)S(1)} %bitcast.125), kind=kOutput, calls=%fused_computation.27 | convolution fusion | flops 4309647360 | bytes 14700544 | tf_op jit(solution)/shard_map/sd,dn->sn/dot_general | solution.py:975
  286.5 7.0 %fusion.143 = (f32[1024]{0:T(1024)S(1)}, bf16[1024,1024]{1,0:T(8,128)(2,1)}) fusion(f32[1024,1024]{1,0:T(8,128)S(1)} %get-tuple-element.109, f32[1024]{0:T(1024)S(1)} %dynamic_slice.11, bf16[2048,1024]{1,0:T(8,128)(2,1)S(1)} %copy-done.22, bf16[2,1024,2048]{2,1,0:T(8,128)(2,1)S(1)} %bitcast.125), kind=kOutput, calls=%fused_computation.186 | convolution fusion | flops 4307549184 | bytes 14688256 | tf_op jit(solution)/shard_map/sd,dn->sn/dot_general | solution.py:977
  293.9 9.6 %convolution_convert_fusion = bf16[2048,1024]{1,0:T(8,128)(2,1)} fusion(f32[2048]{0:T(1024)S(1)} %add.241, f32[2048]{0:T(1024)S(1)} %mul.287, bf16[1024,1024]{1,0:T(8,128)(2,1)} %get-tuple-element.111, bf16[2,1024,2048]{2,1,0:T(8,128)(2,1)} %get-tuple-element.45), kind=kOutput, calls=%fused_computation.32 | convolution fusion | flops 4305453056 | bytes 10502144 | tf_op jit(solution)/shard_map/sd,sn->dn/dot_general | solution.py:981
  303.5 8.4 %fusion.23 = bf16[2048,1024]{1,0:T(8,128)(2,1)} fusion(bf16[1024,1024]{1,0:T(8,128)(2,1)S(1)} %copy-done.27, bf16[2,1024,2048]{2,1,0:T(8,128)(2,1)} %get-tuple-element.45), kind=kOutput, calls=%fused_computation.31 | convolution fusion | flops 4297064448 | bytes 10485760 | tf_op jit(solution)/shard_map/sd,sn->dn/dot_general | solution.py:982
  312.0 4.5 fusion.145
  316.6 4.7 convolution_add_fusion.1.y_ref
  321.3 6.9 %fusion.69.two = f32[1024,2048]{1,0:T(8,128)} fusion(bf16[2048,1024]{1,0:T(8,128)(2,1)S(1)} %copy-done.21, bf16[1024,1024]{1,0:T(8,128)(2,1)S(1)} %copy-done.26), kind=kOutput, calls=%fused_computation.73 | convolution fusion | flops 4294967296 | bytes 14680064 | tf_op jit(solution)/shard_map/sn,dn->sd/dot_general | solution.py:980
  328.2 17.3 %place_outs.1 = (bf16[1024,2048]{1,0:T(8,128)(2,1)}, bf16[1024,2048]{1,0:T(8,128)(2,1)}, f32[4,2048]{1,0:T(4,128)}) custom-call(s32[17]{0:T(128)} %pad_add_fusion.scalar, f32[1024,2048]{1,0:T(8,128)} %convolution_add_fusion.1.y_ref, f32[1024,2048]{1,0:T(8,128)} %convolution_add_fusion.one, f32[1024,2048]{1,0:T(8,128)} %fusion.69.two, ...), custom_call_target="tpu_custom_call" | custom-call | tf_op jit(solution)/shard_map/place_outs/pallas_call | solution.py:501
  347.4 182.0 %scatter_all.1 = (bf16[4,128,512]{2,1,0:T(8,128)(2,1)}, bf16[4,128,512]{2,1,0:T(8,128)(2,1)}, bf16[4,128,1024]{2,1,0:T(8,128)(2,1)}, bf16[4,128,1024]{2,1,0:T(8,...) custom-call(bf16[4,2,2,128,512]{4,3,2,1,0:T(8,128)(2,1)} %bitcast.123, ...), custom_call_target="tpu_custom_call" | custom-call | tf_op jit(solution)/shard_map/scatter_all/pallas_call | solution.py:813
  533.4 3.1 fusion.65
  536.4 10.2 %adam_update.2 = (f32[128,4,1024]{2,1,0:T(4,128)}, f32[128,4,1024]{2,1,0:T(4,128)}, f32[128,4,1024]{2,1,0:T(4,128)}, f32[128,4,1024]{2,1,0:T(4,128)}) custom-call(bf16[4,128,512]{2,1,0:T(8,128)(2,1)} %get-tuple-element.55.refs_0_, bf16[4,128,512]{2,1,0:T(8,128)(2,1)} %get-tuple-element.56.refs_1_, f32[128,4,1024]{2,1,0:T(4,128)} %refs_2_.2, ...), custom_call_target="tpu_custom_call" | custom-call | tf_op jit(solution)/shard_map/adam_update/pallas_call | solution.py:882
  546.6 14.2 %adam_update.3 = (f32[128,2,4096]{2,1,0:T(2,128)}, f32[128,2,4096]{2,1,0:T(2,128)}, f32[128,2,4096]{2,1,0:T(2,128)}, f32[128,2,4096]{2,1,0:T(2,128)}) custom-call(bf16[4,128,1024]{2,1,0:T(8,128)(2,1)} %get-tuple-element.58.refs_0_, bf16[4,128,1024]{2,1,0:T(8,128)(2,1)} %get-tuple-element.59.refs_1_, f32[128,2,4096]{2,1,0:T(2,128)} %refs_2_.3, ...), custom_call_target="tpu_custom_call" | custom-call | tf_op jit(solution)/shard_map/adam_update/pallas_call | solution.py:882
  (162 shorter events, 44.7 us)
Async XLA Ops:
  0.6 7.1 %copy-start.1 = (f32[128,2048]{1,0:T(8,128)S(1)}, f32[128,2048]{1,0:T(8,128)}, u32[]{:S(2)}) copy-start(f32[128,2048]{1,0:T(8,128)} %param.14) | copy-start | bytes 3145732
  210.2 3.9 copy-start.2
  214.1 5.8 %copy-start.24 = (bf16[2048,512]{1,0:T(8,128)(2,1)S(1)}, bf16[2048,512]{1,0:T(8,128)(2,1)}, u32[]{:S(2)}) copy-start(bf16[2048,512]{1,0:T(8,128)(2,1)} %get-tuple-element.47) | copy-start | bytes 6291460
  230.4 6.3 %copy-start.11 = (bf16[4,256,192]{2,1,0:T(8,128)(2,1)S(1)}, bf16[4,256,192]{2,1,0:T(8,128)(2,1)}, u32[]{:S(2)}) copy-start(bf16[4,256,192]{2,1,0:T(8,128)(2,1)} %slice.253) | copy-start | bytes 1179652
  232.7 7.9 %copy-start.10 = (bf16[1024,256]{1,0:T(8,128)(2,1)S(1)}, bf16[1024,256]{1,0:T(8,128)(2,1)}, u32[]{:S(2)}) copy-start(bf16[1024,256]{1,0:T(8,128)(2,1)} %copy-done.9) | copy-start | bytes 1572868
  241.0 13.5 %copy-start.4 = (bf16[4,256,256]{2,1,0:T(8,128)(2,1)}, bf16[4,256,256]{2,1,0:T(8,128)(2,1)S(1)}, u32[]{:S(2)}) copy-start(bf16[4,256,256]{2,1,0:T(8,128)(2,1)S(1)} %convolution_convert_fusion.2) | copy-start | bytes 1572868
  242.6 8.4 %copy-start.6 = (bf16[4,256,256]{2,1,0:T(8,128)(2,1)}, bf16[4,256,256]{2,1,0:T(8,128)(2,1)S(1)}, u32[]{:S(2)}) copy-start(bf16[4,256,256]{2,1,0:T(8,128)(2,1)S(1)} %get-tuple-element.90) | copy-start | bytes 1572868
  266.9 4.9 copy-start.12
  266.9 4.9 copy-start.13
  266.9 4.9 copy-start.25
  271.8 7.8 %slice-start = ((s8[8388608]{0:T(1024)(128)(4,1)}), s8[4194304]{0:T(1024)(128)(4,1)S(1)}, s32[]{:S(2)}) async-start(s8[8388608]{0:T(1024)(128)(4,1)} %bitcast.124), calls=%async_computation | async-start | bytes 8388608
  274.2 5.4 slice-start.1
  274.2 6.1 %copy-start.20 = (bf16[2048,1024]{1,0:T(8,128)(2,1)S(1)}, bf16[2048,1024]{1,0:T(8,128)(2,1)}, u32[]{:S(2)}) copy-start(bf16[2048,1024]{1,0:T(8,128)(2,1)} %get-tuple-element.50) | copy-start | bytes 12582916
  280.4 6.1 %copy-start.22 = (bf16[2048,1024]{1,0:T(8,128)(2,1)S(1)}, bf16[2048,1024]{1,0:T(8,128)(2,1)}, u32[]{:S(2)}) copy-start(bf16[2048,1024]{1,0:T(8,128)(2,1)} %get-tuple-element.49) | copy-start | bytes 12582916
  293.9 9.6 %copy-start.27 = (bf16[1024,1024]{1,0:T(8,128)(2,1)S(1)}, bf16[1024,1024]{1,0:T(8,128)(2,1)}, u32[]{:S(2)}) copy-start(bf16[1024,1024]{1,0:T(8,128)(2,1)} %get-tuple-element.108) | copy-start | bytes 6291460
  303.5 8.4 %copy-start.23 = (bf16[2048,1024]{1,0:T(8,128)(2,1)S(1)}, bf16[2048,1024]{1,0:T(8,128)(2,1)}, u32[]{:S(2)}) copy-start(bf16[2048,1024]{1,0:T(8,128)(2,1)} %get-tuple-element.49) | copy-start | bytes 12582916
  312.0 4.6 copy-start.5
  316.5 4.8 copy-start.21
  316.6 4.7 copy-start.26
  347.3 182.0 %copy-start = (f32[128,2048]{1,0:T(8,128)S(1)}, f32[128,2048]{1,0:T(8,128)}, u32[]{:S(2)}) copy-start(f32[128,2048]{1,0:T(8,128)} %param.12) | copy-start | bytes 3145732
  347.3 185.4 %copy-start.16 = (f32[12,64]{1,0:T(8,128)S(1)}, f32[12,64]{1,0:T(8,128)}, u32[]{:S(2)}) copy-start(f32[12,64]{1,0:T(8,128)} %param.17) | copy-start | bytes 9220
  347.3 185.4 %copy-start.18 = (f32[12,64]{1,0:T(8,128)S(1)}, f32[12,64]{1,0:T(8,128)}, u32[]{:S(2)}) copy-start(f32[12,64]{1,0:T(8,128)} %param.22) | copy-start | bytes 9220
  347.4 185.4 %copy-start.19 = (f32[12,64]{1,0:T(8,128)S(1)}, f32[12,64]{1,0:T(8,128)}, u32[]{:S(2)}) copy-start(f32[12,64]{1,0:T(8,128)} %param.23) | copy-start | bytes 9220
  532.7 13.9 %copy-start.17 = (f32[12,64]{1,0:T(8,128)}, f32[12,64]{1,0:T(8,128)S(1)}, u32[]{:S(2)}) copy-start(f32[12,64]{1,0:T(8,128)S(1)} %reshape.277) | copy-start | bytes 9220
  (6 other events, 11.2 us)

commit v2 on v1

--- a/solution.py
+++ b/solution.py
@@ -27,38 +27,6 @@
     center = row_data - jnp.mean(row_data, axis=-1, keepdims=True)
     inverse = lax.rsqrt(jnp.mean(center * center, axis=-1, keepdims=True) + norm_epsilon)
     return (center * inverse, inverse)
-
-
-def angle_tables(places):
-    half_dims = ROT // 2
-    frequency = 10000.0 ** (-(jnp.arange(half_dims).astype(f32) * (2.0 / ROT)))
-    angles = places[..., None] * frequency
-    return (jnp.cos(angles), jnp.sin(angles))
-
-
-def rotate(values, cos_table, sin_table):
-    half_dims = ROT // 2
-    low_half = values[..., :half_dims]
-    high_half = values[..., half_dims:ROT]
-    return jnp.concatenate(
-        [
-            low_half * cos_table - high_half * sin_table,
-            high_half * cos_table + low_half * sin_table,
-            values[..., ROT:],
-        ],
-        axis=-1,
-    )
-
-
-def gelu_exact(pre_act):
-    return 0.5 * pre_act * (1.0 + lax.erf(pre_act * 0.7071067811865476))
-
-
-def gelu_slope(pre_act):
-    return (
-        0.5 * (1.0 + lax.erf(pre_act * 0.7071067811865476))
-        + pre_act * jnp.exp(-0.5 * pre_act * pre_act) * 0.3989422804014327
-    )
 
 
 def adam_step(weight, gradient, moment_one, moment_two):
@@ -115,7 +83,34 @@
 
 
 MESH = pl.DeviceIdType.MESH
-M_FIRST = (True, False, True, False)
+PARTS = (1, 1, 2, 2)
+CHUNKS = ((0, 0, True), (1, 0, False), (2, 0, True), (2, 1, False), (3, 0, True), (3, 1, False))
+GATHER_ORDER = {
+    (False, False): (
+        0, 10, 500, 510, 520, 530, 540, 550, 700, 600, 501, 900, 620, 511, 910, 640, 601, 801, 502, 710, 20, 30, 40,
+        50, 512, 602, 610, 920, 630, 811, 521, 650, 531, 621, 541, 551, 641, 611, 930, 802, 940, 503, 612, 513, 603,
+        631, 651, 812, 522, 532, 622, 542, 552, 632, 642, 613, 652, 803, 813, 523, 533, 623, 543, 553, 633, 643, 653,
+    ),
+    (False, True): (
+        0, 10, 700, 500, 510, 520, 530, 540, 550, 610, 630, 650, 600, 501, 900, 620, 511, 611, 640, 710, 20, 30, 40,
+        50, 801, 910, 601, 502, 602, 811, 521, 930, 531, 621, 541, 940, 551, 641, 631, 512, 612, 651, 920, 802, 503,
+        603, 812, 522, 532, 622, 542, 552, 642, 632, 513, 613, 652, 803, 813, 523, 533, 623, 543, 633, 553, 643, 653,
+    ),
+    (True, False): (
+        0, 10, 500, 510, 520, 530, 540, 550, 900, 700, 600, 200, 503, 620, 100, 300, 640, 501, 513, 603, 210, 310,
+        601, 110, 511, 710, 20, 30, 40, 50, 803, 400, 610, 801, 502, 910, 410, 630, 512, 602, 650, 811, 220, 813,
+        120, 920, 523, 521, 320, 230, 623, 533, 130, 613, 621, 330, 531, 543, 240, 340, 140, 611, 553, 541, 643, 350,
+        250, 930, 150, 551, 641, 940, 802, 612, 633, 631, 812, 653, 420, 651, 522, 430, 532, 622, 440, 542, 632, 450,
+        642, 552, 652,
+    ),
+    (True, True): (
+        0, 10, 700, 500, 510, 520, 530, 540, 550, 900, 610, 630, 650, 600, 200, 503, 620, 100, 300, 640, 501, 513,
+        613, 710, 20, 30, 40, 50, 210, 310, 110, 511, 611, 603, 601, 803, 400, 801, 502, 910, 602, 813, 811, 523,
+        220, 320, 120, 623, 533, 930, 521, 330, 230, 940, 543, 130, 621, 633, 340, 531, 643, 631, 553, 240, 350, 140,
+        410, 541, 653, 512, 612, 250, 920, 641, 150, 551, 651, 802, 812, 420, 522, 430, 622, 532, 632, 440, 542, 450,
+        642, 552, 652,
+    ),
+}
 
 
 class Links:
@@ -146,6 +141,7 @@
     def drain(self):
         for one in self.sends:
             one.wait_send()
+        self.sends = []
 
     def partners(self):
         other = 1 - self.t
@@ -154,6 +150,17 @@
         out += [self.to(c=1 - self.c), self.to(t=other), self.to(c=1 - self.c, t=other)]
         return out
 
+    def doubling(self):
+        high = self.z // 2
+        place = ((self.m * 2 + self.c) * 2 + self.t) * 4 + lax.rem(self.z + high, 2) * 2 + high
+        steps = [(1, self.to(z=self.z ^ 3)), (2, self.to(z=self.z ^ 1)), (4, self.to(t=1 - self.t))]
+        steps.append((8, self.to(c=1 - self.c)))
+        j = 1
+        while j < self.m_size:
+            steps.append((16 * j, self.to(m=self.m ^ j)))
+            j *= 2
+        return place, steps
+
     def meet(self):
         barrier = pltpu.get_barrier_semaphore()
         everyone = self.partners()
@@ -165,256 +172,209 @@
 def gather_kernel(m_size, *refs):
     pieces, low, mine_small = refs[:4], refs[4], refs[5]
     full, act, table = refs[6:10], refs[10], refs[11]
-    stage, stage_m = refs[12:16], refs[16:20]
-    (zs, zr, ps, pr, ms, mr, near_s, far_s, xr, as_, ar, ws, wr, ss, sr) = refs[20:35]
-    bounce, bounce_low, lin, lout = refs[35:39], refs[39], refs[40], refs[41]
+    count = len(CHUNKS)
+    stage, stage_m, relay = (refs[12 + i * count : 12 + (i + 1) * count] for i in range(3))
+    refs = refs[12 + 3 * count :]
+    (zs, zr, gs, gr, ps, pr, ms, mr, near_s, far_s, xr, as_, ar, ws, wr, ss, sr, lin, lout) = refs[:19]
+    bounce, bounce_low = refs[19 : 19 + count], refs[19 + count]
     net = Links(m_size)
     z, m, c, t = net.z, net.m, net.c, net.t
     rows = pieces[0].shape[1]
     half = low.shape[1]
     role = lax.rem(c + t, 2)
-
-    def by_role(do):
-        @pl.when(role == 0)
-        def _():
-            do(True)
-
-        @pl.when(role == 1)
-        def _():
-            do(False)
-
-    def block(zz, mm, cc, count=1):
+    inner_z = lax.rem(z + z // 2, 2)
+
+    def columns(ch):
+        array, part, _ = CHUNKS[ch]
+        wide = pieces[array].shape[2] // PARTS[array]
+        return array, slice(part * wide, (part + 1) * wide)
+
+    def piece(ch, zz):
+        array, cols = columns(ch)
+        return pieces[array].at[zz, :, cols]
+
+    def whole(ch, zz, mm, cc, size=1):
+        array, cols = columns(ch)
         start = ((zz * m_size + mm) * 2 + cc) * rows
-        return pl.ds(pl.multiple_of(start, rows), count * rows)
+        return full[array].at[pl.ds(pl.multiple_of(start, rows), size * rows), cols]
 
     own_place = pl.ds(pl.multiple_of(z * 2 * half + t * half, half), half)
     place = lambda zz, h: pl.ds(pl.multiple_of(zz * 2 * half + (t ^ h) * half, half), half)
 
-    loads = [pltpu.make_async_copy(pieces[ch].at[z], bounce[ch], lin.at[ch]) for ch in range(4)]
-    loads.append(pltpu.make_async_copy(low.at[0], bounce_low, lin.at[4]))
-    stores = [pltpu.make_async_copy(bounce[ch], full[ch].at[block(z, m, c)], lout.at[ch]) for ch in range(4)]
-    stores.append(pltpu.make_async_copy(bounce_low, act.at[0, own_place], lout.at[4]))
-
-    def load_own(diag):
-        if diag:
-            for one in loads:
-                one.start()
-
-    by_role(load_own)
+    loads = [pltpu.make_async_copy(piece(ch, z), bounce[ch], lin.at[ch]) for ch in range(count)]
+    loads.append(pltpu.make_async_copy(low.at[0], bounce_low, lin.at[count]))
+    stores = [pltpu.make_async_copy(bounce[ch], whole(ch, z, m, c), lout.at[ch]) for ch in range(count)]
+    stores.append(pltpu.make_async_copy(bounce_low, act.at[0, own_place], lout.at[count]))
+
+    @pl.when(role == 0)
+    def _():
+        for one in loads:
+            one.start()
+
     net.meet()
-
-    near = net.copy(low.at[1], act.at[1, own_place], near_s, xr.at[0], net.to(c=1 - c))
-    far = [
-        net.copy(low.at[0], act.at[0, own_place], near_s, xr.at[1], net.to(t=1 - t)),
-        net.copy(low.at[1], act.at[1, own_place], far_s, xr.at[1], net.to(c=1 - c, t=1 - t)),
-    ]
-
-    def rows_out(diag):
-        if diag:
-            near.start()
-        else:
-            for one in far:
-                one.start()
-
-    by_role(rows_out)
-
-    steps = [(1, net.to(t=1 - t)), (2, net.to(c=1 - c))]
-    j = 1
-    while j < m_size:
-        steps.append((4 * j, net.to(m=m ^ j)))
-        j *= 2
-    steps += [(4 * m_size, net.to(z=z ^ 1)), (8 * m_size, net.to(z=z ^ 3))]
-    flat = ((z * m_size + m) * 2 + c) * 2 + t
+    flat, steps = net.doubling()
     small_own = pltpu.make_async_copy(mine_small, table.at[flat], ss.at[len(steps)])
     small_own.start()
-    state = {"small": 0}
-
-    def small_send():
-        i = state["small"]
-        if i < len(steps):
-            size, target = steps[i]
-            span = table.at[pl.ds(flat // size * size, size)]
-            net.send(span, span, ss.at[i], sr.at[i], target)
-
-    def small_next():
-        i = state["small"]
-        if i < len(steps):
-            size = steps[i][0]
-            net.landed(table.at[pl.ds((flat // size ^ 1) * size, size)], sr.at[i])
-            state["small"] += 1
-            small_send()
-
-    def spot(diag, ch, zz, j):
+
+    def program(inner, diag):
+        state = {"small": 0}
+
+        def small_send():
+            i = state["small"]
+            if i < len(steps):
+                size, target = steps[i]
+                span = table.at[pl.ds(flat // size * size, size)]
+                net.send(span, span, ss.at[i], sr.at[i], target)
+
+        def small_next():
+            i = state["small"]
+            if i < len(steps):
+                size = steps[i][0]
+                net.landed(table.at[pl.ds((flat // size ^ 1) * size, size)], sr.at[i])
+                state["small"] += 1
+                small_send()
+
+        def spot(ch, zz, j):
+            if diag:
+                return whole(ch, zz, m ^ j, c)
+            return stage_m[ch].at[m ^ j, zz] if j else stage[ch].at[zz]
+
+        def source(ch, k, j):
+            return piece(ch, z) if k == 0 and j == 0 else spot(ch, z ^ k, j)
+
+        def spread(ch, k, j):
+            src, dst = source(ch, k, j), whole(ch, z ^ k, m ^ j, c)
+            net.send(src, dst, ps.at[ch, j, k, 1], pr.at[ch, j, k, c], net.to(c=t, t=1 - t))
+            if not diag:
+                net.send(src, dst, ps.at[ch, j, k, 0], pr.at[ch, j, k, c], net.to(c=1 - c))
+
+        def spread_landed(ch, k, j):
+            for cc in (1 - c,) if diag else (1 - c, c):
+                net.landed(whole(ch, z ^ k, m ^ j, cc), pr.at[ch, j, k, cc])
+
+        def swap(h, k):
+            src = act.at[role, place(z ^ k, h)]
+            net.send(src, src, ws.at[k, h], wr.at[k, h], net.to(c=1 - c))
+
+        def rows_on(h, block, i, hop, k):
+            src = act.at[role, place(block, h)]
+            net.send(src, src, as_.at[h, i], ar.at[h, k], net.to(z=z ^ hop))
+
+        def quarters(ch, _):
+            for i, (k, hop, through) in enumerate(
+                ((3, 3, None), (2, 3, 2), (1, 1, None)) if inner else ((3, 1, 1), (2, 1, 0), (1, 1, None))
+            ):
+                target = net.to(z=z ^ hop)
+                if through is None:
+                    net.send(piece(ch, z ^ k), spot(ch, z, 0), zs.at[ch, i], zr.at[ch, k], target)
+                else:
+                    net.send(piece(ch, z ^ k), relay[ch].at[through], zs.at[ch, i], gr.at[ch, through], target)
+
+        def pass_on(through):
+            hop, k = ((3, 2), (3, None), (1, 2), (1, 3))[through]
+
+            def run(ch, _):
+                src = relay[ch].at[through]
+                net.landed(src, gr.at[ch, through])
+                if k is None:
+                    net.send(src, relay[ch].at[3], gs.at[ch, through], gr.at[ch, 3], net.to(z=z ^ hop))
+                else:
+                    dst = spot(ch, z ^ hop ^ k, 0)
+                    net.send(src, dst, gs.at[ch, through], zr.at[ch, k], net.to(z=z ^ hop))
+
+            return run
+
+        def first(ch, k):
+            if k:
+                net.landed(spot(ch, z ^ k, 0), zr.at[ch, k])
+            if CHUNKS[ch][2]:
+                for j in range(1, m_size):
+                    dst = whole(ch, z ^ k, m, c) if diag else stage_m[ch].at[m, z ^ k]
+                    net.send(source(ch, k, 0), dst, ms.at[ch, j, k], mr.at[ch, j, k], net.to(m=m ^ j))
+            spread(ch, k, 0)
+
+        def second(ch, k):
+            if CHUNKS[ch][2]:
+                for j in range(1, m_size):
+                    net.landed(spot(ch, z ^ k, j), mr.at[ch, j, k])
+                    spread(ch, k, j)
+            else:
+                if diag and k == 0:
+                    stores[ch].wait()
+                spread_landed(ch, k, 0)
+                both = whole(ch, z ^ k, m, 0, 2)
+                for j in range(1, m_size):
+                    net.send(both, both, ms.at[ch, j, k], mr.at[ch, j, k], net.to(m=m ^ j))
+
+        def rows_start(h, _):
+            if h:
+                net.landed(act.at[0 if diag else 1, place(z, 1)], xr.at[1])
+            elif diag:
+                stores[count].wait()
+            else:
+                net.landed(act.at[1, place(z, 0)], xr.at[0])
+            if inner:
+                rows_on(h, z, 0, 3, 3)
+            rows_on(h, z, 1, 1, 1)
+            swap(h, 0)
+
+        def rows_next(h, k):
+            net.landed(act.at[role, place(z ^ k, h)], ar.at[h, k])
+            if inner:
+                hop, there = {1: (3, 2), 3: (1, 2), 2: (1, 3)}[k]
+                rows_on(h, z ^ k, 1 + k, hop, there)
+            swap(h, k)
+
+        small_own.wait()
+        small_send()
         if diag:
-            return full[ch].at[block(zz, m ^ j, c)]
-        return stage_m[ch].at[m ^ j, zz] if j else stage[ch].at[zz]
-
-    order = [(ch, k) for ch in range(4) for k in (0, 1, 3, 2)]
-
-    def quarters_out(diag):
-        for ch, k in order:
-            if k:
-                net.copy(
-                    pieces[ch].at[z ^ k], spot(diag, ch, z, 0), zs.at[ch, k], zr.at[ch, k], net.to(z=z ^ k)
-                ).start()
-
-    by_role(quarters_out)
-    small_own.wait()
-    small_send()
-
-    def store_own(diag):
+            net.send(low.at[1], act.at[1, own_place], near_s, xr.at[0], net.to(c=1 - c))
+        else:
+            net.send(low.at[0], act.at[0, own_place], near_s, xr.at[1], net.to(t=1 - t))
+            net.send(low.at[1], act.at[1, own_place], far_s, xr.at[1], net.to(c=1 - c, t=1 - t))
         if diag:
             for load, store in zip(loads, stores):
                 load.wait()
                 store.start()
-
-    by_role(store_own)
-
-    def source(diag, ch, k, j):
-        return pieces[ch].at[z] if k == 0 and j == 0 else spot(diag, ch, z ^ k, j)
-
-    def spread(diag, ch, k, j):
-        src = source(diag, ch, k, j)
-        dst = full[ch].at[block(z ^ k, m ^ j, c)]
-        net.copy(src, dst, ps.at[ch, j, k, 1], pr.at[ch, j, k, c], net.to(c=t, t=1 - t)).start()
-        if not diag:
-            net.copy(src, dst, ps.at[ch, j, k, 0], pr.at[ch, j, k, c], net.to(c=1 - c)).start()
-
-    def spread_landed(diag, ch, k, j):
-        for cc in (1 - c,) if diag else (1 - c, c):
-            net.landed(full[ch].at[block(z ^ k, m ^ j, cc)], pr.at[ch, j, k, cc])
-
-    def first(ch, k):
-        def do(diag):
-            if k:
-                net.landed(spot(diag, ch, z ^ k, 0), zr.at[ch, k])
-            if M_FIRST[ch]:
-                for j in range(1, m_size):
-                    dst = full[ch].at[block(z ^ k, m, c)] if diag else stage_m[ch].at[m, z ^ k]
-                    net.copy(
-                        source(diag, ch, k, 0), dst, ms.at[ch, j, k], mr.at[ch, j, k], net.to(m=m ^ j)
-                    ).start()
-            spread(diag, ch, k, 0)
-
-        by_role(do)
-
-    def second(ch, k):
-        def do(diag):
-            if M_FIRST[ch]:
-                for j in range(1, m_size):
-                    net.landed(spot(diag, ch, z ^ k, j), mr.at[ch, j, k])
-                    spread(diag, ch, k, j)
-            else:
-                if diag and k == 0:
-                    stores[ch].wait()
-                spread_landed(diag, ch, k, 0)
-                both = full[ch].at[block(z ^ k, m, 0, 2)]
-                for j in range(1, m_size):
-                    net.copy(both, both, ms.at[ch, j, k], mr.at[ch, j, k], net.to(m=m ^ j)).start()
-
-        by_role(do)
-
-    def third(ch, k):
-        def do(diag):
-            if M_FIRST[ch]:
-                for j in range(m_size):
-                    spread_landed(diag, ch, k, j)
-                if diag and k == 0:
-                    stores[ch].wait()
-            else:
-                for j in range(1, m_size):
-                    net.landed(full[ch].at[block(z ^ k, m ^ j, 0, 2)], mr.at[ch, j, k])
-
-        by_role(do)
-
-    def drain(ch, k):
-        def do(diag):
-            if k:
-                src = pieces[ch].at[z ^ k]
-                net.copy(src, src, zs.at[ch, k], zr.at[ch, k], net.to(z=z ^ k)).wait_send()
-            if M_FIRST[ch]:
-                src = source(diag, ch, k, 0)
-            else:
-                src = full[ch].at[block(z ^ k, m, 0, 2)]
-            for j in range(1, m_size):
-                net.copy(src, src, ms.at[ch, j, k], mr.at[ch, j, k], net.to(m=m ^ j)).wait_send()
-            for j in range(m_size if M_FIRST[ch] else 1):
-                src = source(diag, ch, k, j)
-                for side in (1,) if diag else (1, 0):
-                    net.copy(src, src, ps.at[ch, j, k, side], pr.at[ch, j, k, 0], net.to(c=1 - c)).wait_send()
-
-        by_role(do)
-
-    own_first = [p for p in order if p[1] == 0] + [p for p in order if p[1]]
-
-    def rows_start(h):
-        def do(diag):
-            if h:
-                net.landed(act.at[0 if diag else 1, place(z, 1)], xr.at[1])
-            elif diag:
-                stores[4].wait()
-            else:
-                net.landed(act.at[1, place(z, 0)], xr.at[0])
-
-        by_role(do)
-        src = act.at[role, place(z, h)]
-        net.send(src, src, as_.at[h, 0], ar.at[h, 0], net.to(z=z ^ 3))
-        net.send(src, src, as_.at[h, 1], ar.at[h, 1], net.to(z=z ^ 1))
-        net.send(src, src, ws.at[0, h], wr.at[0, h], net.to(c=1 - c))
-
-    def rows_far(h):
-        src = act.at[role, place(z ^ 3, h)]
-        net.landed(src, ar.at[h, 0])
-        net.send(src, src, as_.at[h, 2], ar.at[h, 2], net.to(z=z ^ 1))
-        net.send(src, src, ws.at[3, h], wr.at[3, h], net.to(c=1 - c))
-
-    def rows_last(h, k):
-        src = act.at[role, place(z ^ k, h)]
-        net.landed(src, ar.at[h, k])
-        net.send(src, src, ws.at[k, h], wr.at[k, h], net.to(c=1 - c))
-
-    for ch, k in own_first[:4]:
-        first(ch, k)
-    small_next()
-    rows_start(0)
-    small_next()
-    rows_start(1)
-    small_next()
-    pending = list(own_first[:4])
-    for i, (ch, k) in enumerate(own_first[4:]):
-        first(ch, k)
-        pending.append((ch, k))
-        if len(pending) > 3:
-            second(*pending.pop(0))
-        if i % 3 == 2:
+        runs = [quarters] + [pass_on(i) for i in range(4)] + [first, second, rows_start, rows_next]
+        runs.append(lambda *_: small_next())
+        for code in GATHER_ORDER[inner, diag]:
+            runs[code // 100](code // 10 % 10, code % 10)
+        while state["small"] < len(steps):
             small_next()
-    rows_far(0)
-    while pending:
-        second(*pending.pop(0))
-    while state["small"] < len(steps):
-        small_next()
-    rows_far(1)
-    for h in range(2):
-        rows_last(h, 1)
-    for ch, k in own_first:
-        third(ch, k)
-    for h in range(2):
-        rows_last(h, 2)
-    for k in (0, 3, 1, 2):
-        for h in range(2):
-            net.landed(act.at[1 - role, place(z ^ k, h)], wr.at[k, h])
-    net.drain()
-    for ch, k in order:
-        drain(ch, k)
-
-    def rows_drain(diag):
-        if diag:
-            near.wait_send()
-        else:
-            for one in far:
-                one.wait_send()
-
-    by_role(rows_drain)
+        for ch in range(count):
+            for k in range(Z):
+                if CHUNKS[ch][2]:
+                    for j in range(m_size):
+                        spread_landed(ch, k, j)
+                    if diag and k == 0:
+                        stores[ch].wait()
+                else:
+                    for j in range(1, m_size):
+                        net.landed(whole(ch, z ^ k, m ^ j, 0, 2), mr.at[ch, j, k])
+        for k in range(Z):
+            for h in range(2):
+                net.landed(act.at[1 - role, place(z ^ k, h)], wr.at[k, h])
+        net.drain()
+
+    by_class(inner_z, role, program)
+
+
+def table_order(m_size):
+    order = []
+    for z in range(Z):
+        for rest in range(4 * m_size):
+            order.append(rest * 4 + (z + z // 2) % 2 * 2 + z // 2)
+    return order
+
+
+def by_class(inner_z, role, program):
+    for inner in (False, True):
+        for diag in (False, True):
+
+            @pl.when((inner_z == int(inner)) & (role == int(not diag)))
+            def _(inner=inner, diag=diag):
+                program(inner, diag)
 
 
 def gather(pieces, low, small, m_size):
@@ -422,101 +382,230 @@
     width = low.shape[2]
     devices = m_size * 4 * Z
     cols = [p.shape[2] for p in pieces]
-    stages = [jax.ShapeDtypeStruct((Z, rows, n), bf16) for n in cols]
-    stages_m = [jax.ShapeDtypeStruct((m_size, Z, rows, n), bf16) for n in cols]
+    count = len(CHUNKS)
+    parts = [cols[array] // PARTS[array] for array, _, _ in CHUNKS]
     sem = pltpu.SemaphoreType.DMA
     doubling = m_size.bit_length() - 1 + 4
+    in_place = pl.BlockSpec(memory_space=pl.ANY)
+    shape = lambda *dims: jax.ShapeDtypeStruct(dims, bf16)
     outs = pl.pallas_call(
         functools.partial(gather_kernel, m_size),
-        out_shape=[jax.ShapeDtypeStruct((width, n), bf16) for n in cols]
-        + [
-            jax.ShapeDtypeStruct((2, Z * 2 * low.shape[1], width), bf16),
-            jax.ShapeDtypeStruct((devices,) + small.shape, f32),
-        ]
-        + stages
-        + stages_m,
-        in_specs=[pl.BlockSpec(memory_space=pl.ANY)] * 6,
-        out_specs=[pl.BlockSpec(memory_space=pl.ANY)] * 14,
+        out_shape=[shape(width, n) for n in cols]
+        + [shape(2, Z * 2 * low.shape[1], width), jax.ShapeDtypeStruct((devices,) + small.shape, f32)]
+        + [shape(Z, rows, n) for n in parts]
+        + [shape(m_size, Z, rows, n) for n in parts]
+        + [shape(4, rows, n) for n in parts],
+        in_specs=[in_place] * 6,
+        out_specs=[in_place] * (6 + 3 * count),
         scratch_shapes=[
-            sem((4, Z)),
-            sem((4, Z)),
-            sem((4, m_size, Z, 2)),
-            sem((4, m_size, Z, 2)),
-            sem((4, m_size, Z)),
-            sem((4, m_size, Z)),
+            sem((count, 3)),
+            sem((count, Z)),
+            sem((count, 4)),
+            sem((count, 4)),
+            sem((count, m_size, Z, 2)),
+            sem((count, m_size, Z, 2)),
+            sem((count, m_size, Z)),
+            sem((count, m_size, Z)),
             sem,
             sem,
             sem((2,)),
-            sem((2, 3)),
-            sem((2, 3)),
+            sem((2, 5)),
+            sem((2, Z)),
             sem((Z, 2)),
             sem((Z, 2)),
             sem((doubling + 1,)),
             sem((doubling,)),
+            sem((count + 1,)),
+            sem((count + 1,)),
         ]
-        + [pltpu.VMEM((rows, n), bf16) for n in cols]
-        + [pltpu.VMEM(low.shape[1:], bf16), sem((5,)), sem((5,))],
+        + [pltpu.VMEM((rows, n), bf16) for n in parts]
+        + [pltpu.VMEM(low.shape[1:], bf16)],
         compiler_params=pltpu.CompilerParams(collective_id=0, has_side_effects=True),
         name="gather_all",
     )(*pieces, low, small)
     return outs[:4], outs[4], outs[5]
 
 
-def out_kernel(blocks, scalar, y_ref, one, two, plain, par, keep, send, sums):
-    diag = scalar[blocks] == 1
+VMEM_BYTES = 60 * 1024 * 1024
+
+
+def dot(a, b, over_a=1, over_b=0):
+    return lax.dot_general(a, b, (((over_a,), (over_b,)), ((), ())), preferred_element_type=f32)
+
+
+def turn(value, tables, sign):
+    cos, low, high = (table[...] for table in tables)
+    part = value[:, :128]
+    turned = part * cos + sign * (
+        pltpu.roll(part, 128 - ROT // 2, 1) * low + pltpu.roll(part, ROT // 2, 1) * high
+    )
+    return jnp.concatenate([turned, value[:, 128:]], axis=1)
+
+
+def turn_tables(places):
+    half = ROT // 2
+    column = jnp.arange(128)
+    frequency = 10000.0 ** (-((column % half).astype(f32) * (2.0 / ROT)))
+    angles = places.reshape(-1, 1) * frequency
+    cos = jnp.where(column < ROT, jnp.cos(angles), 1.0)
+    sin = jnp.sin(angles)
+    return cos, jnp.where(column < half, -sin, 0.0), jnp.where((column >= half) & (column < ROT), sin, 0.0)
+
+
+def attn_kernel(x, g, w_qk, w_vo, par, bias, cos, low, high, across, down, one_out, att_out, d_out, sums):
+    tables = (cos, low, high)
+    n = HEAD_DIM
+    scale = HEAD_DIM ** (-0.5)
+    one = (x[...].astype(f32) * par[0:1, :] + par[1:2, :]).astype(bf16)
+    one_out[...] = one
+    qk = dot(one, w_qk[...])
+    q = turn(qk[:, :n] + bias[0:1, :], tables, 1.0).astype(bf16)
+    k = turn(qk[:, n:], tables, 1.0).astype(bf16)
+    v = (dot(one, w_vo[:, :n]) + bias[1:2, :]).astype(bf16)
+    d_att = dot(g[...], w_vo[:, n:]).astype(bf16)
+    scores = jnp.where(across[0] <= down[0], dot(q, k, 1, 1) * scale, -jnp.inf)
+    top = jnp.max(scores, axis=-1, keepdims=True)
+    log_total = top + jnp.log(jnp.sum(jnp.exp(scores - top), axis=-1, keepdims=True))
+    probs = jnp.exp(scores - log_total)
+    low_probs = probs.astype(bf16)
+    att_out[...] = dot(low_probs, v).astype(bf16)
+    d_probs = dot(d_att, v, 1, 1)
+    d_scores = (probs * (d_probs - jnp.sum(probs * d_probs, axis=-1, keepdims=True)) * scale).astype(bf16)
+    d_q = turn(dot(d_scores, k), tables, -1.0)
+    d_k = turn(dot(d_scores, q, 0, 0), tables, -1.0)
+    d_v = dot(low_probs, d_att, 0, 0)
+    d_out[:, :n] = d_q.astype(bf16)
+    d_out[:, n : 2 * n] = d_k.astype(bf16)
+    d_out[:, 2 * n :] = d_v.astype(bf16)
 
     @pl.when(pl.program_id(0) == 0)
     def _():
         sums[...] = jnp.zeros_like(sums)
 
-    for p in range(blocks):
-        dst = pl.ds(pl.multiple_of(scalar[p] * 128, 128), 128)
-        src = slice(p * 128, (p + 1) * 128)
-        y, d_one, d_two = y_ref[:, src], one[:, src], two[:, src]
-        x = plain[:, src].astype(f32)
-        u = d_one * par[0:1, dst] + d_two * par[2:3, dst]
-        keep[:, dst] = jnp.where(diag, y, u).astype(bf16)
-        send[:, dst] = jnp.where(diag, u, y).astype(bf16)
-        rows = [jnp.sum(v, axis=0, keepdims=True) for v in (d_one * x, d_one, d_two * x, d_two)]
-        for i, row in enumerate(rows):
-            sums[i : i + 1, dst] += row
-
-
-def place_outs(y, d_one, d_two, plain, par, order, diag):
-    rows, width = y.shape
-    blocks = order.shape[0]
-    if (width // blocks) % 128:
-        back = jnp.argsort(order)
-        take = lambda v: jnp.take(v.reshape(v.shape[0], blocks, -1), back, axis=1).reshape(v.shape)
-        y, d_one, d_two, x = take(y), take(d_one), take(d_two), take(plain).astype(f32)
-        u = d_one * par[0] + d_two * par[2]
-        sums = jnp.stack([jnp.sum(v, axis=0) for v in (d_one * x, d_one, d_two * x, d_two)])
-        return jnp.where(diag, y, u).astype(bf16), jnp.where(diag, u, y).astype(bf16), sums
-    per = width // 128 // blocks
-    order = (order[:, None] * per + jnp.arange(per)[None]).reshape(-1)
-    blocks = blocks * per
+    sums[0:1, :] += jnp.sum(d_q, axis=0, keepdims=True)
+    sums[1:2, :] += jnp.sum(d_v, axis=0, keepdims=True)
+
+
+def fixed(*shape):
+    return pl.BlockSpec(shape, lambda i: (0,) * len(shape))
+
+
+def run_attention(acts, w_qk, w_vo, par, bias, places):
+    _, rows, width = acts.shape
+    seq, n = rows // Z, HEAD_DIM
+    by_rows = lambda cols: pl.BlockSpec((seq, cols), lambda i: (i, 0))
+    act = lambda which: pl.BlockSpec((None, seq, width), lambda i: (which, i, 0))
+    return pl.pallas_call(
+        attn_kernel,
+        grid=(Z,),
+        in_specs=[act(0), act(1), fixed(width, 2 * n), fixed(width, 2 * n), fixed(*par.shape), fixed(2, n)]
+        + [by_rows(128)] * 3
+        + [pl.BlockSpec((1, 1, seq), lambda i: (i, 0, 0)), pl.BlockSpec((1, seq, 1), lambda i: (i, 0, 0))],
+        out_specs=[by_rows(width), by_rows(n), by_rows(3 * n), fixed(2, n)],
+        out_shape=[jax.ShapeDtypeStruct((rows, cols), bf16) for cols in (width, n, 3 * n)]
+        + [jax.ShapeDtypeStruct((2, n), f32)],
+        compiler_params=pltpu.CompilerParams(vmem_limit_bytes=VMEM_BYTES),
+        name="attention",
+    )(acts, acts, w_qk, w_vo, par, bias, *turn_tables(places), places[:, None, :], places[:, :, None])
+
+
+def hidden_kernel(x, g, up, down, par, bias, two_out, act_out, d_out, sums):
+    @pl.when(pl.program_id(0) == 0)
+    def _():
+        two_out[...] = (x[...].astype(f32) * par[2:3, :] + par[3:4, :]).astype(bf16)
+
+    pre = dot(two_out[...], up[...]) + bias[...]
+    erf = 1.0 + lax.erf(pre * 0.7071067811865476)
+    act_out[...] = (0.5 * pre * erf).astype(bf16)
+    slope = 0.5 * erf + pre * jnp.exp(-0.5 * pre * pre) * 0.3989422804014327
+    d_pre = dot(g[...], down[...]) * slope
+    d_out[...] = d_pre.astype(bf16)
+    sums[...] = jnp.sum(d_pre, axis=0, keepdims=True)
+
+
+def run_hidden(acts, w_up, w_dn, par, bias):
+    _, rows, width = acts.shape
+    hidden = w_up.shape[1]
     step = 256
-    spec = pl.BlockSpec((step, width), lambda i, s: (i, 0))
-    whole = pl.BlockSpec((4, width), lambda i, s: (0, 0))
+    act = lambda which: pl.BlockSpec((None, rows, width), lambda i: (which, 0, 0), pipeline_mode=pl.Buffered(1))
+    tile = lambda height: pl.BlockSpec((height, step), lambda i: (0, i))
     return pl.pallas_call(
-        functools.partial(out_kernel, blocks),
+        hidden_kernel,
+        grid=(hidden // step,),
+        in_specs=[act(0), act(1), tile(width), tile(width), fixed(*par.shape), tile(1)],
+        out_specs=[fixed(rows, width), tile(rows), tile(rows), tile(1)],
+        out_shape=[jax.ShapeDtypeStruct((rows, n), bf16) for n in (width, hidden, hidden)]
+        + [jax.ShapeDtypeStruct((1, hidden), f32)],
+        compiler_params=pltpu.CompilerParams(vmem_limit_bytes=VMEM_BYTES),
+        name="hidden_units",
+    )(acts, acts, w_up, w_dn, par, bias)
+
+
+def outs_kernel(flag, att, d_attn, act, d_pre, x, w_qk, w_vo, w_up, w_dn, par, keep, give, sums):
+    diag = flag[0] == 1
+    n = HEAD_DIM
+    y = dot(att[...], w_vo[:, n:], 1, 1) + dot(act[...], w_dn[...], 1, 1)
+    d_one = dot(d_attn[:, : 2 * n], w_qk[...], 1, 1) + dot(d_attn[:, 2 * n :], w_vo[:, :n], 1, 1)
+    d_two = dot(d_pre[...], w_up[...], 1, 1)
+    u = d_one * par[0:1, :] + d_two * par[2:3, :]
+    keep[...] = jnp.where(diag, y, u).astype(bf16)
+    give[...] = jnp.where(diag, u, y).astype(bf16)
+    plain = x[...].astype(f32)
+    for i, value in enumerate((d_one * plain, d_one, d_two * plain, d_two)):
+        sums[i : i + 1, :] = jnp.sum(value, axis=0, keepdims=True)
+
+
+def run_outs(diag, att, d_attn, act, d_pre, acts, weights, par):
+    _, rows, width = acts.shape
+    step = 256
+    fix = lambda v: pl.BlockSpec(v.shape, lambda i, s: (0, 0), pipeline_mode=pl.Buffered(1))
+    tile = lambda height: pl.BlockSpec((height, step), lambda i, s: (0, i))
+    return pl.pallas_call(
+        outs_kernel,
         grid_spec=pltpu.PrefetchScalarGridSpec(
             num_scalar_prefetch=1,
-            grid=(rows // step,),
-            in_specs=[spec] * 4 + [whole],
-            out_specs=[spec, spec, whole],
+            grid=(width // step,),
+            in_specs=[fix(v) for v in (att, d_attn, act, d_pre)]
+            + [pl.BlockSpec((None, rows, step), lambda i, s: (0, 0, i))]
+            + [pl.BlockSpec((step, v.shape[1]), lambda i, s: (i, 0)) for v in weights]
+            + [tile(4)],
+            out_specs=[tile(rows), tile(rows), tile(4)],
         ),
-        out_shape=[jax.ShapeDtypeStruct((rows, width), bf16)] * 2
-        + [jax.ShapeDtypeStruct((4, width), f32)],
-        name="place_outs",
-    )(
-        jnp.concatenate([order, diag.astype(jnp.int32).reshape(1)]).astype(jnp.int32),
-        y,
-        d_one,
-        d_two,
-        plain,
-        par,
-    )
+        out_shape=[jax.ShapeDtypeStruct((rows, width), bf16)] * 2 + [jax.ShapeDtypeStruct((4, width), f32)],
+        compiler_params=pltpu.CompilerParams(vmem_limit_bytes=VMEM_BYTES),
+        name="outputs",
+    )(diag.astype(jnp.int32).reshape(1), att, d_attn, act, d_pre, acts, *weights, par)
+
+
+def grads_kernel(one, two, g, att, d_attn, act, d_pre, qk, vo, up, dn):
+    n = HEAD_DIM
+    first = dot(one[...], d_attn[...], 0, 0)
+    qk[...] = first[:, : 2 * n].astype(bf16)
+    vo[:, :n] = first[:, 2 * n :].astype(bf16)
+    vo[:, n:] = dot(g[...], att[...], 0, 0).astype(bf16)
+    up[...] = dot(two[...], d_pre[...], 0, 0).astype(bf16)
+    dn[...] = dot(g[...], act[...], 0, 0).astype(bf16)
+
+
+def run_grads(one, two, acts, att, d_attn, act, d_pre):
+    rows, width = one.shape
+    step = 256
+    tile = pl.BlockSpec((rows, step), lambda i: (0, i))
+    fix = lambda v: pl.BlockSpec(v.shape, lambda i: (0, 0), pipeline_mode=pl.Buffered(1))
+    cols = [2 * HEAD_DIM, 2 * HEAD_DIM, act.shape[1], act.shape[1]]
+    return pl.pallas_call(
+        grads_kernel,
+        grid=(width // step,),
+        in_specs=[tile, tile, pl.BlockSpec((None, rows, step), lambda i: (1, 0, i))]
+        + [fix(v) for v in (att, d_attn, act, d_pre)],
+        out_specs=[pl.BlockSpec((step, n), lambda i: (i, 0)) for n in cols],
+        out_shape=[jax.ShapeDtypeStruct((width, n), bf16) for n in cols],
+        compiler_params=pltpu.CompilerParams(vmem_limit_bytes=VMEM_BYTES),
+        name="weight_grads",
+    )(one, two, acts, att, d_attn, act, d_pre)
+
+
+M_FIRST = (True, False, True, False)
 
 
 def add_rows(dst, sources):
@@ -583,13 +672,7 @@
     current[...] = terms[...]
     net.meet()
 
-    flat = ((z * m_size + m) * 2 + c) * 2 + t
-    steps = [(1, net.to(t=1 - t)), (2, net.to(c=1 - c))]
-    j = 1
-    while j < m_size:
-        steps.append((4 * j, net.to(m=m ^ j)))
-        j *= 2
-    steps += [(4 * m_size, net.to(z=z ^ 1)), (8 * m_size, net.to(z=z ^ 3))]
+    flat, steps = net.doubling()
     steps = steps[::-1]
     state = {"small": 0}
 
@@ -921,67 +1004,21 @@
     ).reshape(-1, 128)
     weights, acts, table = gather(pieces, jnp.stack([x_low, g_low]), small_tile, grid.m)
     w_qk, w_vo, w_up, w_dn = weights
-    everyone = table.reshape(devices, -1)
+    everyone = jnp.take(table.reshape(devices, -1), jnp.array(table_order(grid.m)), axis=0)
     small_all = jnp.transpose(everyone[:, : 12 * part].reshape(devices, 12, part), (1, 0, 2)).reshape(12, width)
     group = (jnp.arange(Z) * grid.m + m) * 4 + t * 2
     places = jnp.take(everyone[:, tile : tile + seq], group, axis=0)
-    plain, grads = acts[0], acts[1]
-    x_group = plain.astype(f32)
-    one_low = (x_group * small_all[0] + small_all[1]).astype(bf16)
-    two_low = (x_group * small_all[2] + small_all[3]).astype(bf16)
-    order = jnp.arange(grid.dp)
-
+    par = small_all[:4]
     head = c * Z + z
     hidden = w_up.shape[1]
-    query_bias = lax.dynamic_slice_in_dim(small_all[4], head * HEAD_DIM, HEAD_DIM)
-    value_bias = lax.dynamic_slice_in_dim(small_all[5], head * HEAD_DIM, HEAD_DIM)
-    up_bias = lax.dynamic_slice_in_dim(small_all[8:12].reshape(-1), head * hidden, hidden)
-
-    dot = functools.partial(jnp.einsum, preferred_element_type=f32)
-
-    cos_table, sin_table = angle_tables(places)
-    score_scale = HEAD_DIM ** (-0.5)
-    visible = places[:, None, :] <= places[:, :, None]
-    qk = dot("sd,dn->sn", one_low, w_qk)
-    w_v, w_o = w_vo[:, :HEAD_DIM], w_vo[:, HEAD_DIM:]
-    per_seq = lambda v: v.reshape(Z, seq, HEAD_DIM)
-    queries = rotate(per_seq(qk[:, :HEAD_DIM] + query_bias), cos_table, sin_table).astype(bf16)
-    key_rows = rotate(per_seq(qk[:, HEAD_DIM:]), cos_table, sin_table).astype(bf16)
-    values = per_seq((dot("sd,dn->sn", one_low, w_v) + value_bias).astype(bf16))
-    scores = dot("nqd,nkd->nqk", queries, key_rows) * score_scale
-    scores = jnp.where(visible, scores, -jnp.inf)
-    row_max = jnp.max(scores, axis=-1, keepdims=True)
-    log_total = row_max + jnp.log(jnp.sum(jnp.exp(scores - row_max), axis=-1, keepdims=True))
-    probs = jnp.exp(scores - log_total)
-    probs_low = probs.astype(bf16)
-    attended = dot("nqk,nkd->nqd", probs_low, values).astype(bf16)
-    d_attended = per_seq(dot("sd,dn->sn", grads, w_o).astype(bf16))
-    d_probs = dot("nqd,nkd->nqk", d_attended, values)
-    d_scores = (probs * (d_probs - jnp.sum(probs * d_probs, axis=-1, keepdims=True)) * score_scale).astype(bf16)
-    d_query = rotate(dot("nqk,nkd->nqd", d_scores, key_rows), cos_table, -sin_table)
-    d_key = rotate(dot("nqk,nqd->nkd", d_scores, queries), cos_table, -sin_table)
-    d_value = dot("nqk,nqd->nkd", probs_low, d_attended)
-    flat = lambda v: v.reshape(Z * seq, HEAD_DIM)
-    attended, d_query, d_key, d_value = flat(attended), flat(d_query), flat(d_key), flat(d_value)
-    dqk_low = jnp.concatenate([d_query, d_key], axis=1).astype(bf16)
-    dv_low = d_value.astype(bf16)
-    d_one = dot("sn,dn->sd", dqk_low, w_qk) + dot("sn,dn->sd", dv_low, w_v)
-    y_attn = dot("sn,dn->sd", attended, w_o)
-    grad_qk = dot("sd,sn->dn", one_low, dqk_low).astype(bf16)
-    grad_vo = jnp.concatenate(
-        [dot("sd,sn->dn", one_low, dv_low).astype(bf16), dot("sd,sn->dn", grads, attended).astype(bf16)], axis=1
-    )
-
-    pre_act = dot("sd,dn->sn", two_low, w_up) + up_bias
-    activation = gelu_exact(pre_act).astype(bf16)
-    d_pre = dot("sd,dn->sn", grads, w_dn) * gelu_slope(pre_act)
-    d_pre_low = d_pre.astype(bf16)
-    y_part = dot("sn,dn->sd", activation, w_dn) + y_attn
-    d_two = dot("sn,dn->sd", d_pre_low, w_up)
-    grad_up = dot("sd,sn->dn", two_low, d_pre_low).astype(bf16)
-    grad_dn = dot("sd,sn->dn", grads, activation).astype(bf16)
-
-    keep, give, norm_sums = place_outs(y_part, d_one, d_two, plain, small_all[:4], order, diag)
+    head_bias = lax.dynamic_slice_in_dim(small_all[4:6], head * HEAD_DIM, HEAD_DIM, axis=1)
+    up_bias = lax.dynamic_slice_in_dim(small_all[8:12].reshape(1, -1), head * hidden, hidden, axis=1)
+
+    one_low, attended, d_attn, head_sums = run_attention(acts, w_qk, w_vo, par, head_bias, places)
+    two_low, activation, d_pre, up_sums = run_hidden(acts, w_up, w_dn, par, up_bias)
+    keep, give, norm_sums = run_outs(diag, attended, d_attn, activation, d_pre, acts, weights, par)
+    weight_grads = run_grads(one_low, two_low, acts, attended, d_attn, activation, d_pre)
+
     spread_cols = lambda v, n: lax.dynamic_update_slice_in_dim(
         jnp.zeros((n,), f32), v, head * v.shape[0], 0
     )
@@ -989,17 +1026,19 @@
     small_terms = jnp.concatenate(
         [
             norm_sums,
-            spread_cols(jnp.sum(d_query, axis=0), width)[None],
-            spread_cols(jnp.sum(d_value, axis=0), width)[None],
+            spread_cols(head_sums[0], width)[None],
+            spread_cols(head_sums[1], width)[None],
             out_sum[None],
             out_sum[None],
-            spread_cols(jnp.sum(d_pre, axis=0), 4 * width).reshape(4, width),
+            spread_cols(up_sums[0], 4 * width).reshape(4, width),
         ],
         axis=0,
     )
     terms = jnp.transpose(small_terms.reshape(12, devices, part), (1, 0, 2)).reshape(devices, 12 * part)
+    places_of = table_order(grid.m)
+    terms = jnp.take(terms, jnp.array([places_of.index(i) for i in range(devices)]), axis=0)
     terms = jnp.pad(terms, ((0, 0), (0, tile - 12 * part))).reshape(devices, -1, 128)
-    own, own_rows, own_small = scatter([grad_qk, grad_vo, grad_up, grad_dn], keep, give, terms, grid.m, rows)
+    own, own_rows, own_small = scatter(weight_grads, keep, give, terms, grid.m, rows)
     y_rows, u_rows = own_rows[0].astype(f32), own_rows[1].astype(f32)
     block_out = block_in + y_rows + small_all[6] + small_all[7]
     input_grad = out_grad + inverse * (

time: 565 us -> 466 us (0.82)
  matrix products: 93.6 us -> 0 us
  local copies, waits for them, and re-layouts: 26.8 us -> 10.7 us
  Pallas kernels: 421 us -> 433 us
    dot_general x21 -> x0, matrix products: 93.6 us -> none  [the longest x1 9.6 us: body(): grad_up = dot('sd,sn->dn', two_low, d_pre_low).astype(bf16)]
    pallas_call x2 -> x5, Pallas kernels: 206 us -> 212 us  [the longest x1 142 us: gather(): pl.pallas_call(functools.partial(gather_kernel, m_size), out_shape=[shape...]
    pallas_call x1, Pallas kernels: 182 us -> 188 us  [scatter(): pl.pallas_call(functools.partial(scatter_kernel, m_size), out_shape=[jax....]
where the time goes in v2:
time: 466 us; the launch traced here: 465 us
  Pallas kernels  433 us (93%)
  other arithmetic  20.5 us (4%)
  local copies, waits for them, and re-layouts  10.7 us (2%)
    pallas_call x1, Pallas kernels, scatter(): pl.pallas_call(functools.partial(scatter_kernel, m_size), out_shape=[jax....  188 us
    pallas_call x1, Pallas kernels, gather(): pl.pallas_call(functools.partial(gather_kernel, m_size), out_shape=[shape...  142 us
    pallas_call x2, Pallas kernels, adam_update(): pl.pallas_call(functools.partial(adam_kernel, per), grid=(Z,), in_specs=[...  24.1 us
    pallas_call x1, Pallas kernels, run_outs(): pl.pallas_call(outs_kernel, grid_spec=pltpu.PrefetchScalarGridSpec(num_sc...  21.6 us
    pallas_call x1, Pallas kernels, run_grads(): pl.pallas_call(grads_kernel, grid=(width // step,), in_specs=[tile, tile,...  19.2 us
    pallas_call x1, Pallas kernels, run_hidden(): pl.pallas_call(hidden_kernel, grid=(hidden // step,), in_specs=[act(0), a...  17.1 us
    pallas_call x1, Pallas kernels, run_attention(): pl.pallas_call(attn_kernel, grid=(Z,), in_specs=[act(0), act(1), fixed(wi...  12.7 us

profile of v2, /device:TPU:0, one launch (start us, length us, event | category | flops | bytes accessed | tf_op | source)
XLA Modules:
  0.0 465.3 jit_solution(7646073703930164130)
XLA Ops:
  0.7 1.4 reduce_sum.45
  2.2 1.5 multiply_reduce_fusion
  5.1 0.8 reshape.245
  7.1 1.4 fusion.13
  8.7 1.1 pad_maximum_fusion.refs_4_
  9.7 8.6 %split_weights.1 = (bf16[4,128,512]{2,1,0:T(8,128)(2,1)}, bf16[4,128,512]{2,1,0:T(8,128)(2,1)}, bf16[4,128,1024]{2,1,0:T(8,128)(2,1)}, bf16[4,128,1024]{2,1,0:T(8,128)(2,1)}) custom-call(f32[128,4,1024]{2,1,0:T(4,128)} %refs_2_.2, f32[128,2,4096]{2,1,0:T(2,128)} %refs_2_.3), custom_call_target="tpu_custom_call" | custom-call | tf_op jit(solution)/shard_map/split_weights/pallas_call | solution.py:72
  18.4 141.7 %gather_all.1 = (bf16[2048,512]{1,0:T(8,128)(2,1)}, bf16[2048,512]{1,0:T(8,128)(2,1)}, bf16[2048,1024]{1,0:T(8,128)(2,1)}, bf16[2048,1024]{1,0:T(8,128)(2,1)}, b...) custom-call(bf16[4,128,512]{2,1,0:T(8,128)(2,1)} %get-tuple-element., ...), custom_call_target="tpu_custom_call" | custom-call | tf_op jit(solution)/shard_map/gather_all/pallas_call | solution.py:391
  160.1 1.0 copy.44
  165.0 0.7 slice.48.par
  165.9 0.9 broadcast_select_fusion.down
  166.8 3.2 fusion.9
  170.0 12.7 %attention.1 = (bf16[1024,2048]{1,0:T(8,128)(2,1)}, bf16[1024,256]{1,0:T(8,128)(2,1)}, bf16[1024,768]{1,0:T(8,128)(2,1)}, f32[2,256]{1,0:T(2,128)}) custom-call(bf16[2,1024,2048]{2,1,0:T(8,128)(2,1)} %get-tuple-element.57.x.g, bf16[2,1024,2048]{2,1,0:T(8,128)(2,1)} %get-tuple-element.57.x.g, bf16[2048,512]{1,0:T(8,128)(2,1)} %get-tuple-element.58.w_qk, ...), custom_call_target="tpu_custom_call" | custom-call | tf_op jit(solution)/shard_map/attention/pallas_call | solution.py:498
  182.7 0.7 slice_dynamic-update-slice_fusion
  183.4 0.7 slice_dynamic-update-slice_fusion.1
  186.1 17.1 %hidden_units.1 = (bf16[1024,2048]{1,0:T(8,128)(2,1)}, bf16[1024,1024]{1,0:T(8,128)(2,1)}, bf16[1024,1024]{1,0:T(8,128)(2,1)}, f32[1,1024]{1,0:T(1,128)}) custom-call(bf16[2,1024,2048]{2,1,0:T(8,128)(2,1)} %get-tuple-element.57.x.g, bf16[2,1024,2048]{2,1,0:T(8,128)(2,1)} %get-tuple-element.57.x.g, bf16[2048,1024]{1,0:T(8,128)(2,1)} %get-tuple-element.62.up.w_up, ...), custom_call_target="tpu_custom_call" | custom-call | tf_op jit(solution)/shard_map/hidden_units/pallas_call | solution.py:532
  203.2 21.6 %outputs.1 = (bf16[1024,2048]{1,0:T(8,128)(2,1)}, bf16[1024,2048]{1,0:T(8,128)(2,1)}, f32[4,2048]{1,0:T(4,128)}) custom-call(s32[1]{0:T(128)} %bitcast.11.flag, bf16[1024,256]{1,0:T(8,128)(2,1)} %get-tuple-element.65.att, bf16[1024,768]{1,0:T(8,128)(2,1)} %get-tuple-element.66.d_attn, bf16[1024,1024]{1,0:T(8,128)(2,1)} %get-tuple-element.67.act, ...), custom_call_target="tpu_custom_call" | custom-call | tf_op jit(solution)/shard_map/outputs/pallas_call | solution.py:563
  224.9 19.2 %weight_grads.1 = (bf16[2048,512]{1,0:T(8,128)(2,1)}, bf16[2048,512]{1,0:T(8,128)(2,1)}, bf16[2048,1024]{1,0:T(8,128)(2,1)}, bf16[2048,1024]{1,0:T(8,128)(2,1)}) custom-call(bf16[1024,2048]{1,0:T(8,128)(2,1)} %get-tuple-element.61.one, bf16[1024,2048]{1,0:T(8,128)(2,1)} %get-tuple-element.64.two, bf16[2,1024,2048]{2,1,0:T(8,128)(2,1)} %get-tuple-element.57.x.g, ...), custom_call_target="tpu_custom_call" | custom-call | tf_op jit(solution)/shard_map/weight_grads/pallas_call | solution.py:596
  246.2 187.8 %scatter_all.1 = (bf16[4,128,512]{2,1,0:T(8,128)(2,1)}, bf16[4,128,512]{2,1,0:T(8,128)(2,1)}, bf16[4,128,1024]{2,1,0:T(8,128)(2,1)}, bf16[4,128,1024]{2,1,0:T(8,...) custom-call(bf16[4,2,2,128,512]{4,3,2,1,0:T(8,128)(2,1)} %bitcast.53, bf16[4,2,2,128,512]{4,3,2,1,0:T(8,128)(2,1)} %bitcast.54, ...), custom_call_target="tpu_custom_call" | custom-call | tf_op jit(solution)/shard_map/scatter_all/pallas_call | solution.py:896
  434.1 1.4 fusion.5
  435.4 1.2 convert_reduce_fusion
  436.6 0.8 reshape.260
  438.0 3.1 fusion.4
  441.1 10.0 %adam_update.2 = (f32[128,4,1024]{2,1,0:T(4,128)}, f32[128,4,1024]{2,1,0:T(4,128)}, f32[128,4,1024]{2,1,0:T(4,128)}, f32[128,4,1024]{2,1,0:T(4,128)}) custom-call(bf16[4,128,512]{2,1,0:T(8,128)(2,1)} %get-tuple-element.79.refs_0_, bf16[4,128,512]{2,1,0:T(8,128)(2,1)} %get-tuple-element.80.refs_1_, f32[128,4,1024]{2,1,0:T(4,128)} %refs_2_.2, ...), custom_call_target="tpu_custom_call" | custom-call | tf_op jit(solution)/shard_map/adam_update/pallas_call | solution.py:965
  451.1 14.2 %adam_update.3 = (f32[128,2,4096]{2,1,0:T(2,128)}, f32[128,2,4096]{2,1,0:T(2,128)}, f32[128,2,4096]{2,1,0:T(2,128)}, f32[128,2,4096]{2,1,0:T(2,128)}) custom-call(bf16[4,128,1024]{2,1,0:T(8,128)(2,1)} %get-tuple-element.82.refs_0_, bf16[4,128,1024]{2,1,0:T(8,128)(2,1)} %get-tuple-element.83.refs_1_, f32[128,2,4096]{2,1,0:T(2,128)} %refs_2_.3, ...), custom_call_target="tpu_custom_call" | custom-call | tf_op jit(solution)/shard_map/adam_update/pallas_call | solution.py:965
  (77 shorter events, 11.5 us)
Async XLA Ops:
  0.6 7.8 %copy-start.1 = (f32[128,2048]{1,0:T(8,128)S(1)}, f32[128,2048]{1,0:T(8,128)}, u32[]{:S(2)}) copy-start(f32[128,2048]{1,0:T(8,128)} %param.16) | copy-start | bytes 3145732
  224.8 19.2 %copy-start.7 = (f32[1,1024]{1,0:T(1,128)S(1)}, f32[1,1024]{1,0:T(1,128)}, u32[]{:S(2)}) copy-start(f32[1,1024]{1,0:T(1,128)} %get-tuple-element.77) | copy-start | bytes 12292
  224.9 19.6 %copy-start.2 = (f32[4,2048]{1,0:T(4,128)S(1)}, f32[4,2048]{1,0:T(4,128)}, u32[]{:S(2)}) copy-start(f32[4,2048]{1,0:T(4,128)} %get-tuple-element.75) | copy-start | bytes 98308
  246.2 187.9 %copy-start = (f32[128,2048]{1,0:T(8,128)S(1)}, f32[128,2048]{1,0:T(8,128)}, u32[]{:S(2)}) copy-start(f32[128,2048]{1,0:T(8,128)} %param.14) | copy-start | bytes 3145732
  246.2 191.2 %copy-start.3 = (f32[12,64]{1,0:T(8,128)S(1)}, f32[12,64]{1,0:T(8,128)}, u32[]{:S(2)}) copy-start(f32[12,64]{1,0:T(8,128)} %param.19) | copy-start | bytes 9220
  246.2 191.2 %copy-start.5 = (f32[12,64]{1,0:T(8,128)S(1)}, f32[12,64]{1,0:T(8,128)}, u32[]{:S(2)}) copy-start(f32[12,64]{1,0:T(8,128)} %param.24) | copy-start | bytes 9220
  246.2 191.2 %copy-start.6 = (f32[12,64]{1,0:T(8,128)S(1)}, f32[12,64]{1,0:T(8,128)}, u32[]{:S(2)}) copy-start(f32[12,64]{1,0:T(8,128)} %param.25) | copy-start | bytes 9220
  437.4 13.7 %copy-start.4 = (f32[12,64]{1,0:T(8,128)}, f32[12,64]{1,0:T(8,128)S(1)}, u32[]{:S(2)}) copy-start(f32[12,64]{1,0:T(8,128)S(1)} %reshape.260) | copy-start | bytes 9220

commit v3 on v2

--- a/solution.py
+++ b/solution.py
@@ -109,6 +109,44 @@
         220, 320, 120, 623, 533, 930, 521, 330, 230, 940, 543, 130, 621, 633, 340, 531, 643, 631, 553, 240, 350, 140,
         410, 541, 653, 512, 612, 250, 920, 641, 150, 551, 651, 802, 812, 420, 522, 430, 622, 532, 632, 440, 542, 450,
         642, 552, 652,
+    ),
+}
+SCATTER_ORDER = {
+    (False, False): (
+        30, 31, 20, 21, 10, 11, 0, 1, 131, 530, 531, 520, 521, 510, 511, 500, 501, 1600, 203, 413, 223, 433, 243,
+        453, 121, 1610, 202, 412, 222, 432, 242, 452, 111, 903, 1620, 201, 411, 221, 431, 241, 451, 101, 923, 943,
+        1630, 200, 410, 220, 430, 240, 450, 130, 902, 1013, 1033, 303, 323, 922, 343, 120, 942, 1053, 302, 322, 342,
+        110, 901, 1012, 921, 301, 321, 341, 100, 941, 300, 320, 340, 1032, 900, 920, 800, 1052, 940, 1113, 1133,
+        1011, 1103, 810, 1031, 1051, 1153, 1123, 1143, 1640, 1010, 1112, 1030, 1050, 1102, 1122, 1142, 1101, 1132,
+        1121, 1152, 1141, 1111, 1100, 1120, 1140, 1131, 1151, 1110, 1130, 1150,
+    ),
+    (False, True): (
+        30, 31, 20, 21, 10, 11, 0, 1, 131, 530, 531, 520, 521, 510, 511, 500, 501, 1600, 203, 413, 223, 433, 243,
+        453, 121, 1610, 903, 202, 412, 222, 432, 242, 452, 111, 923, 201, 411, 221, 431, 241, 451, 101, 943, 1620,
+        200, 410, 220, 430, 240, 450, 130, 902, 1013, 922, 1033, 1630, 303, 323, 343, 120, 942, 1053, 901, 302, 322,
+        342, 110, 921, 301, 321, 341, 100, 1012, 941, 300, 320, 340, 900, 920, 1032, 940, 800, 1113, 1052, 1133,
+        1103, 1123, 810, 1011, 1031, 1153, 1051, 1143, 1640, 1010, 1112, 1030, 1050, 1102, 1122, 1142, 1132, 1101,
+        1152, 1121, 1111, 1141, 1100, 1120, 1131, 1140, 1151, 1110, 1130, 1150,
+    ),
+    (True, False): (
+        30, 31, 20, 21, 10, 11, 0, 1, 131, 530, 531, 520, 521, 510, 511, 500, 501, 1600, 203, 413, 223, 433, 243,
+        453, 121, 1610, 202, 412, 222, 432, 242, 452, 111, 620, 903, 923, 1620, 201, 411, 221, 431, 241, 451, 101,
+        943, 200, 410, 220, 430, 240, 450, 130, 902, 1013, 621, 922, 1033, 303, 323, 343, 1053, 120, 700, 901, 942,
+        302, 322, 342, 110, 1012, 630, 921, 941, 301, 321, 341, 100, 710, 900, 920, 1032, 300, 320, 340, 1052, 940,
+        631, 1113, 1133, 1103, 1011, 1123, 800, 1031, 1153, 1051, 1143, 810, 1630, 1310, 1112, 1010, 1330, 1300,
+        1640, 1030, 1350, 1510, 1320, 1410, 1050, 1340, 1530, 1102, 1132, 1210, 1500, 1122, 1550, 1200, 1101, 1520,
+        1220, 1142, 1540, 1240, 1121, 1152, 1400, 1141, 1111, 1430, 1230, 1100, 1131, 1120, 1151, 1420, 1250, 1140,
+        1110, 1440, 1130, 1150, 1450,
+    ),
+    (True, True): (
+        30, 31, 20, 21, 10, 11, 0, 1, 131, 530, 531, 520, 521, 510, 511, 500, 501, 1600, 203, 413, 223, 433, 243,
+        453, 121, 1610, 903, 202, 412, 222, 432, 242, 452, 111, 620, 923, 201, 411, 221, 431, 241, 451, 101, 943,
+        1620, 902, 200, 410, 220, 430, 240, 450, 130, 1013, 621, 922, 1033, 942, 1053, 303, 323, 343, 120, 700, 901,
+        921, 302, 322, 342, 110, 630, 1012, 941, 900, 301, 321, 341, 100, 710, 920, 1032, 940, 300, 320, 340, 1113,
+        1052, 631, 1133, 1103, 1123, 1011, 800, 1153, 1031, 1051, 1143, 810, 1630, 1112, 1102, 1310, 1330, 1010,
+        1300, 1640, 1320, 1410, 1030, 1350, 1400, 1340, 1510, 1132, 1050, 1210, 1530, 1122, 1500, 1200, 1142, 1520,
+        1220, 1101, 1550, 1240, 1152, 1121, 1540, 1230, 1111, 1141, 1430, 1131, 1100, 1250, 1151, 1120, 1420, 1140,
+        1440, 1110, 1130, 1150, 1450,
     ),
 }
 
@@ -605,9 +643,6 @@
     )(one, two, acts, att, d_attn, act, d_pre)
 
 
-M_FIRST = (True, False, True, False)
-
-
 def add_rows(dst, sources):
     step = min(dst.shape[0], 32)
 
@@ -620,331 +655,446 @@
         dst[span, :] = total.astype(dst.dtype)
 
 
-def scatter_kernel(m_size, *refs):
-    grads, keep, give, terms = refs[:4], refs[4], refs[5], refs[6]
-    own, rows_out, small_out = refs[7:11], refs[11], refs[12]
-    home_first, x_first, mid_first, far_first, sum_first = (refs[13 + 2 * i : 15 + 2 * i] for i in range(5))
-    own_last, far_last, sum_last, home_last, x_last, sum_far = (refs[23 + 2 * i : 25 + 2 * i] for i in range(6))
-    got, kept, total, got_z, three, final, current, got_small = refs[35:43]
-    (cl, cs, cr, fs, fr, zs, zr, zl, dl, ds_, dr, es, er, kl, gs, gr, ys, yr, rs, rr, rl, ss, sr) = refs[43:]
+def scatter_kernel(m_size, fused, *refs):
+    if fused:
+        ones, twos, acts, att, d_attn, act, d_pre = refs[:7]
+        keep, give, terms = refs[7:10]
+        grads, refs = refs[10:14], refs[14:]
+    else:
+        grads, (keep, give, terms), refs = refs[:4], refs[4:7], refs[7:]
+    own, rows_out, small_out, refs = refs[:4], refs[4], refs[5], refs[6:]
+    count = len(CHUNKS)
+    buffers = []
+    for _, _, m_first in CHUNKS:
+        size = 5 if m_first else 6
+        buffers.append(refs[:size])
+        refs = refs[size:]
+    relay, refs = refs[:count], refs[count:]
+    got, kept, got_z, final, current, got_small = refs[:6]
+    (gs, gr, kl, as_, ar, ys, yr, yl, ws, wr, wl, fs, fr, xs, xr, zs, zr, zl, ps, pr, ss, sr) = refs[6:28]
+    if fused:
+        tiles, made, tl, ml = refs[28:]
     net = Links(m_size)
     z, m, c, t = net.z, net.m, net.c, net.t
     half = rows_out.shape[1]
     role = lax.rem(c + t, 2)
-    first_chunks = [ch for ch in range(4) if M_FIRST[ch]]
-    last_chunks = [ch for ch in range(4) if not M_FIRST[ch]]
-    pairs_first = [(i, ch) for i, ch in enumerate(first_chunks)]
-    pairs_last = [(i, ch) for i, ch in enumerate(last_chunks)]
-    ks = (3, 2, 1, 0)
-
-    def by_role(do):
-        @pl.when(role == 0)
-        def _():
-            do(True)
-
-        @pl.when(role == 1)
-        def _():
-            do(False)
-
+    inner_z = lax.rem(z + z // 2, 2)
+    flat, steps = net.doubling()
+    steps = steps[::-1]
+
+    def columns(ch):
+        array, part, _ = CHUNKS[ch]
+        wide = own[array].shape[2] // PARTS[array]
+        return array, slice(part * wide, (part + 1) * wide)
+
+    def rows_of(ch, k, j, cc=None):
+        array, cols = columns(ch)
+        if cc is None:
+            return grads[array].at[z ^ k, m ^ j, :, :, cols]
+        return grads[array].at[z ^ k, m ^ j, cc, :, cols]
+
+    def owned(ch, zz):
+        array, cols = columns(ch)
+        return own[array].at[zz, :, cols]
+
+    span = lambda h: pl.ds(pl.multiple_of((t ^ h) * half, half), half)
     loads_keep = [pltpu.make_async_copy(keep.at[z ^ k], kept.at[k], kl.at[k]) for k in range(Z)]
-    loads_last = {
-        (i, k): pltpu.make_async_copy(grads[ch].at[z ^ k, m], own_last[i].at[k], dl.at[i, k])
-        for i, ch in pairs_last
-        for k in ks
-    }
-    loads_first = {
-        (i, j, k): pltpu.make_async_copy(grads[ch].at[z ^ k, m ^ j, c], home_first[i].at[j, k], cl.at[i, j, k])
-        for i, ch in pairs_first
-        for j in range(m_size)
-        for k in ks
-    }
     for one in loads_keep:
         one.start()
-    for one in loads_last.values():
-        one.start()
-
-    def load_first(diag):
-        if diag:
-            for one in loads_first.values():
+    current[...] = terms[...]
+
+    def tile_loads(i, slot):
+        block = (z ^ (Z - 1 - lax.rem(i, Z))) * m_size + (m ^ (1 - i // Z))
+        wide = tiles.shape[3]
+        cols = pl.ds(pl.multiple_of(block * wide, wide), wide)
+        sources = (ones.at[:, cols], twos.at[:, cols], acts.at[1, :, cols])
+        return [pltpu.make_async_copy(src, tiles.at[slot, n], tl.at[slot, n]) for n, src in enumerate(sources)]
+
+    def make(i):
+        slot = lax.rem(i, 2)
+
+        @pl.when(i < 2 * Z - 1)
+        def _():
+            for one in tile_loads(i + 1, 1 - slot):
                 one.start()
 
-    by_role(load_first)
-    current[...] = terms[...]
+        for one in tile_loads(i, slot):
+            one.wait()
+        n = HEAD_DIM
+        high = made[0].shape[1]
+        for array, at, left, right, lo, hi in (
+            (0, 0, 0, d_attn, 0, 2 * n),
+            (1, 0, 0, d_attn, 2 * n, 3 * n),
+            (1, n, 2, att, 0, n),
+            (2, 0, 1, d_pre, 0, d_pre.shape[1]),
+            (3, 0, 2, act, 0, act.shape[1]),
+        ):
+            value = dot(tiles[slot, left], right[:, lo:hi], 0, 0).astype(bf16)
+            for cc in range(2):
+                made[array][cc, :, at : at + hi - lo] = value[cc * high : (cc + 1) * high]
+        stores = [
+            pltpu.make_async_copy(
+                made[array], grads[array].at[z ^ (Z - 1 - lax.rem(i, Z)), m ^ (1 - i // Z)], ml.at[array]
+            )
+            for array in range(4)
+        ]
+        for one in stores:
+            one.start()
+        for one in stores:
+            one.wait()
+
+    if fused:
+        for one in tile_loads(0, 0):
+            one.start()
     net.meet()
 
-    flat, steps = net.doubling()
-    steps = steps[::-1]
-    state = {"small": 0}
-
-    def small_send():
-        i = state["small"]
-        if i < len(steps):
-            size, target = steps[i]
-            net.send(
-                current.at[pl.ds((flat // size ^ 1) * size, size)],
-                got_small.at[pl.ds(size, size)],
-                ss.at[i],
-                sr.at[i],
-                target,
+    def program(inner, diag):
+        state = {"small": 0}
+        sent = []
+
+        def send(*parts):
+            (parts,) = parts
+            net.copy(*parts()).start()
+            sent.append(parts)
+
+        def small_send():
+            i = state["small"]
+            if i < len(steps):
+                size, target = steps[i]
+                send(
+                    lambda: (
+                        current.at[pl.ds((flat // size ^ 1) * size, size)],
+                        got_small.at[pl.ds(size, size)],
+                        ss.at[i],
+                        sr.at[i],
+                        target,
+                    )
+                )
+
+        def small_next(*_):
+            i = state["small"]
+            if i < len(steps):
+                size = steps[i][0]
+                net.landed(got_small.at[pl.ds(size, size)], sr.at[i])
+                block = pl.ds(flat // size * size, size)
+                current[block] = current[block] + got_small[pl.ds(size, size)]
+                state["small"] += 1
+                small_send()
+
+        def swap(k, h):
+            send(
+                lambda: (give.at[z ^ k, span(h)], got.at[k, span(h)], gs.at[k, h], gr.at[k, h], net.to(c=1 - c))
             )
 
-    def small_next():
-        i = state["small"]
-        if i < len(steps):
-            size = steps[i][0]
-            net.landed(got_small.at[pl.ds(size, size)], sr.at[i])
-            span = pl.ds(flat // size * size, size)
-            current[span] = current[span] + got_small[pl.ds(size, size)]
-            state["small"] += 1
-            small_send()
-
-    for k in (1, 2, 3, 0):
-        net.send(give.at[z ^ k], got.at[k], gs.at[k], gr.at[k], net.to(c=1 - c))
-    small_send()
-
-    def to_owner(diag, source, home, far, sems, i, jk):
-        send_sem, recv_sem = sems
-        if diag:
-            net.copy(source(1 - c), home, send_sem.at[i, *jk, 0], recv_sem.at[i, *jk, 0], net.to(c=1 - c)).start()
-        else:
-            net.copy(source(c), far, send_sem.at[i, *jk, 0], recv_sem.at[i, *jk, 1], net.to(t=1 - t)).start()
-            net.copy(
-                source(1 - c), far, send_sem.at[i, *jk, 1], recv_sem.at[i, *jk, 1], net.to(c=1 - c, t=1 - t)
-            ).start()
-
-    def collect_first(i, ch, j, k):
-        def do(diag):
-            to_owner(
-                diag,
-                lambda cc: grads[ch].at[z ^ k, m ^ j, cc],
-                home_first[i].at[j, k],
-                x_first[i].at[j, k],
-                (cs, cr),
-                i,
-                (j, k),
+        def load_mine(ch, j, k):
+            if CHUNKS[ch][2]:
+                return pltpu.make_async_copy(rows_of(ch, k, j, c), buffers[ch][0].at[j, k], wl.at[ch, j, k])
+            return pltpu.make_async_copy(rows_of(ch, k, 0), buffers[ch][0].at[k], wl.at[ch, 0, k])
+
+        def load_made(k, own_m):
+            for j in (0,) if own_m == 0 else range(1, m_size):
+                for ch in range(count):
+                    if (diag and CHUNKS[ch][2]) or (j == 0 and not CHUNKS[ch][2]):
+                        load_mine(ch, j, k).start()
+
+        def to_owner(source, home, far, ch, j, k):
+            if diag:
+                send(lambda: (source(1 - c), home(), ws.at[ch, j, k, 0], wr.at[ch, j, k, 0], net.to(c=1 - c)))
+            else:
+                send(lambda: (source(c), far(), ws.at[ch, j, k, 0], wr.at[ch, j, k, 1], net.to(t=1 - t)))
+                send(
+                    lambda: (source(1 - c), far(), ws.at[ch, j, k, 1], wr.at[ch, j, k, 1], net.to(c=1 - c, t=1 - t))
+                )
+
+        def owners_part(ch, j, k):
+            home, far = buffers[ch][0], buffers[ch][1]
+            to_owner(lambda cc: rows_of(ch, k, j, cc), lambda: home.at[j, k], lambda: far.at[j, k], ch, j, k)
+
+        def others(ch, k):
+            for j in range(1, m_size):
+                owners_part(ch, j, k)
+
+        def same(ch, k):
+            owners_part(ch, 0, k)
+
+        def across(ch, k):
+            for j in range(1, m_size):
+                send(
+                    lambda j=j: (
+                        rows_of(ch, k, j),
+                        buffers[ch][1].at[j - 1, k],
+                        fs.at[ch, j, k],
+                        fr.at[ch, j, k],
+                        net.to(m=m ^ j),
+                    )
+                )
+
+        def collected(home, far, ch, j, k):
+            if not diag:
+                net.landed(home, wr.at[ch, j, k, 0])
+            elif CHUNKS[ch][2]:
+                load_mine(ch, j, k).wait()
+            net.landed(far, wr.at[ch, j, k, 1])
+
+        def middle(ch, k):
+            home, far, mid, far_m, _ = buffers[ch]
+            for j in range(1, m_size):
+                collected(home.at[j, k], far.at[j, k], ch, j, k)
+                add_rows(mid.at[j - 1, k], [home.at[j, k], far.at[j, k]])
+                send(
+                    lambda j=j: (
+                        mid.at[j - 1, k],
+                        far_m.at[j - 1, k],
+                        xs.at[ch, j, k],
+                        xr.at[ch, j, k],
+                        net.to(m=m ^ j),
+                    )
+                )
+
+        def summed(ch, k):
+            mine, far_m, both, home, far, _ = buffers[ch]
+            load_mine(ch, 0, k).wait()
+            for j in range(1, m_size):
+                net.landed(far_m.at[j - 1, k], fr.at[ch, j, k])
+            for cc in range(2):
+                add_rows(both.at[k, cc], [mine.at[k, cc]] + [far_m.at[j - 1, k, cc] for j in range(1, m_size)])
+            to_owner(lambda cc: both.at[k, cc], lambda: home.at[k], lambda: far.at[k], ch, 0, k)
+
+        def finish(ch, k):
+            if CHUNKS[ch][2]:
+                home, far, _, far_m, result = buffers[ch]
+                collected(home.at[0, k], far.at[0, k], ch, 0, k)
+                for j in range(1, m_size):
+                    net.landed(far_m.at[j - 1, k], xr.at[ch, j, k])
+                sources = [home.at[0, k], far.at[0, k]] + [far_m.at[j - 1, k] for j in range(1, m_size)]
+            else:
+                _, _, both, home, far, result = buffers[ch]
+                collected(home.at[k], far.at[k], ch, 0, k)
+                sources = [both.at[k, c] if diag else home.at[k], far.at[k]]
+            add_rows(result.at[k], sources)
+            if k == 0:
+                pltpu.make_async_copy(result.at[k], owned(ch, z), zl.at[ch]).start()
+                return
+            hop, through = {1: (1, None), 2: (3, 2), 3: (3, None)}[k] if inner else {1: (1, None), 2: (1, 0), 3: (1, 1)}[k]
+            if through is None:
+                send(lambda: (result.at[k], owned(ch, z), zs.at[ch, k], zr.at[ch, k], net.to(z=z ^ hop)))
+            else:
+                send(
+                    lambda: (
+                        result.at[k],
+                        relay[ch].at[through],
+                        zs.at[ch, k],
+                        pr.at[ch, through],
+                        net.to(z=z ^ hop),
+                    )
+                )
+
+        def pass_on(through):
+            hop, k = ((3, 2), (3, None), (1, 2), (1, 3))[through]
+
+            def run(ch, _):
+                net.landed(relay[ch].at[through], pr.at[ch, through])
+
+                def parts():
+                    if k is None:
+                        dst, recv_sem = relay[ch].at[3], pr.at[ch, 3]
+                    else:
+                        dst, recv_sem = owned(ch, z ^ hop ^ k), zr.at[ch, k]
+                    return relay[ch].at[through], dst, ps.at[ch, through], recv_sem, net.to(z=z ^ hop)
+
+                send(parts)
+
+            return run
+
+        def rows_first(k, h):
+            if h == 0:
+                pltpu.make_async_copy(keep.at[z ^ k], kept.at[k], kl.at[k]).wait()
+            net.landed(got.at[k, span(h)], gr.at[k, h])
+            add_rows(kept.at[k, span(h)], [kept.at[k, span(h)], got.at[k, span(h)]])
+            if k and not inner:
+                slot = {1: 0, 2: 1, 3: 2}[k]
+                send(
+                    lambda: (
+                        kept.at[k, span(h)],
+                        got_z.at[slot, span(h)],
+                        as_.at[k, h],
+                        ar.at[slot, h],
+                        net.to(z=z ^ 1),
+                    )
+                )
+
+        def rows_through(k, h, slot, there, hop):
+            net.landed(got_z.at[slot, span(h)], ar.at[slot, h])
+            add_rows(kept.at[k, span(h)], [kept.at[k, span(h)], got_z.at[slot, span(h)]])
+            send(
+                lambda: (
+                    kept.at[k, span(h)],
+                    got_z.at[there, span(h)],
+                    as_.at[k, h],
+                    ar.at[there, h],
+                    net.to(z=z ^ hop),
+                )
             )
 
-        by_role(do)
-
-    for k in ks:
-        for i, ch in pairs_last:
-            for j in range(1, m_size):
-                net.send(grads[ch].at[z ^ k, m ^ j], far_last[i].at[j - 1, k], ds_.at[i, j, k], dr.at[i, j, k], net.to(m=m ^ j))
-        for i, ch in pairs_first:
-            for j in range(1, m_size):
-                collect_first(i, ch, j, k)
-    for k in ks:
-        for i, ch in pairs_first:
-            collect_first(i, ch, 0, k)
-
-    def collected_first(i, j, k):
-        def do(diag):
+        def rows_inner(k, h):
+            rows_through(k, h, {3: 1, 2: 2}[k], {3: 3, 2: 4}[k], 3)
+
+        def rows_outer(h, _):
+            rows_through(1, h, 4, 0, 1)
+
+        def rows_back(h, _):
+            slots = (0, 3) if inner else (0,)
+            for slot in slots:
+                net.landed(got_z.at[slot, span(h)], ar.at[slot, h])
+            add_rows(final.at[h], [kept.at[0, span(h)]] + [got_z.at[slot, span(h)] for slot in slots])
+            if diag and h == 0:
+                pltpu.make_async_copy(final.at[h], rows_out.at[0], yl).start()
+            elif diag:
+                send(lambda: (final.at[h], rows_out.at[0], ys.at[h], yr.at[0], net.to(t=1 - t)))
+            elif h == 0:
+                send(lambda: (final.at[h], rows_out.at[1], ys.at[h], yr.at[1], net.to(c=1 - c)))
+            else:
+                send(lambda: (final.at[h], rows_out.at[1], ys.at[h], yr.at[1], net.to(c=1 - c, t=1 - t)))
+
+        runs = [swap, load_made, others, same, across, rows_first, rows_inner, rows_outer, rows_back]
+        runs += [middle, summed, finish] + [pass_on(i) for i in range(4)] + [small_next]
+
+        def run(codes):
+            for code in codes:
+                runs[code // 100](code // 10 % 10, code % 10)
+
+        def end():
+            while state["small"] < len(steps):
+                small_next()
+            small_out[...] = current[flat]
+            for ch in range(count):
+                for k in range(1, Z):
+                    net.landed(owned(ch, z ^ k), zr.at[ch, k])
+                pltpu.make_async_copy(owned(ch, z), owned(ch, z), zl.at[ch]).wait()
+            net.landed(rows_out.at[1], yr.at[1])
             if diag:
-                loads_first[i, j, k].wait()
+                pltpu.make_async_copy(final.at[0], rows_out.at[0], yl).wait()
             else:
-                net.landed(home_first[i].at[j, k], cr.at[i, j, k, 0])
-
-        by_role(do)
-        net.landed(x_first[i].at[j, k], cr.at[i, j, k, 1])
-
-    for one in loads_keep:
-        one.wait()
-    for k in (1, 2, 3, 0):
-        net.landed(got.at[k], gr.at[k])
-        add_rows(total.at[k], [kept.at[k], got.at[k]])
-        if k in (1, 2):
-            net.send(total.at[k], got_z.at[k - 1], ys.at[k], yr.at[k], net.to(z=z ^ 1))
-    small_next()
-
-    def to_z(ch, tile, k):
-        if k:
-            net.send(tile, own[ch].at[z], zs.at[ch, k], zr.at[ch, k], net.to(z=z ^ k))
-        else:
-            pltpu.make_async_copy(tile, own[ch].at[z], zl.at[ch]).start()
-
-    def middle(k):
-        for i, ch in pairs_first:
-            for j in range(1, m_size):
-                collected_first(i, j, k)
-                add_rows(mid_first[i].at[j - 1, k], [home_first[i].at[j, k], x_first[i].at[j, k]])
-                net.send(mid_first[i].at[j - 1, k], far_first[i].at[j - 1, k], fs.at[i, j, k], fr.at[i, j, k], net.to(m=m ^ j))
-        for i, ch in pairs_last:
-            loads_last[i, k].wait()
-            for j in range(1, m_size):
-                net.landed(far_last[i].at[j - 1, k], dr.at[i, j, k])
-            for cc in range(2):
-                add_rows(
-                    sum_last[i].at[k, cc],
-                    [own_last[i].at[k, cc]] + [far_last[i].at[j - 1, k, cc] for j in range(1, m_size)],
-                )
-
-            def do(diag):
-                to_owner(
-                    diag,
-                    lambda cc: sum_last[i].at[k, cc],
-                    home_last[i].at[k],
-                    x_last[i].at[k],
-                    (es, er),
-                    i,
-                    (k,),
-                )
-
-            by_role(do)
-
-    def finish(k):
-        for i, ch in pairs_first:
-            collected_first(i, 0, k)
-            for j in range(1, m_size):
-                net.landed(far_first[i].at[j - 1, k], fr.at[i, j, k])
-            add_rows(
-                sum_first[i].at[k],
-                [home_first[i].at[0, k], x_first[i].at[0, k]] + [far_first[i].at[j - 1, k] for j in range(1, m_size)],
-            )
-            to_z(ch, sum_first[i].at[k], k)
-        for i, ch in pairs_last:
-
-            def do(diag):
-                net.landed(x_last[i].at[k], er.at[i, k, 1])
-                if diag:
-                    add_rows(sum_far[i].at[k], [sum_last[i].at[k, c], x_last[i].at[k]])
-                else:
-                    net.landed(home_last[i].at[k], er.at[i, k, 0])
-                    add_rows(sum_far[i].at[k], [home_last[i].at[k], x_last[i].at[k]])
-
-            by_role(do)
-            to_z(ch, sum_far[i].at[k], k)
-
-    middle(3)
-    small_next()
-    middle(2)
-    net.landed(got_z.at[1], yr.at[2])
-    add_rows(three, [total.at[3], got_z.at[1]])
-    net.send(three, got_z.at[2], ys.at[3], yr.at[3], net.to(z=z ^ 3))
-    small_next()
-    middle(1)
-    finish(3)
-    small_next()
-    middle(0)
-    finish(2)
-    while state["small"] < len(steps):
-        small_next()
-    small_out[...] = current[flat]
-    finish(1)
-    net.landed(got_z.at[0], yr.at[1])
-    net.landed(got_z.at[2], yr.at[3])
-    add_rows(final, [total.at[0], got_z.at[0], got_z.at[2]])
-    mine = final.at[pl.ds(pl.multiple_of(t * half, half), half)]
-    other = final.at[pl.ds(pl.multiple_of((1 - t) * half, half), half)]
-    keep_rows = pltpu.make_async_copy(mine, rows_out.at[0], rl)
-
-    def rows_back(diag):
-        if diag:
-            keep_rows.start()
-            net.copy(other, rows_out.at[0], rs.at[0], rr.at[0], net.to(t=1 - t)).start()
-        else:
-            net.copy(mine, rows_out.at[1], rs.at[0], rr.at[1], net.to(c=1 - c)).start()
-            net.copy(other, rows_out.at[1], rs.at[1], rr.at[1], net.to(c=1 - c, t=1 - t)).start()
-
-    by_role(rows_back)
-    finish(0)
-    for ch in range(4):
-        for k in range(1, Z):
-            net.landed(own[ch].at[z ^ k], zr.at[ch, k])
-        pltpu.make_async_copy(own[ch].at[z], own[ch].at[z], zl.at[ch]).wait()
-
-    def rows_done(diag):
-        net.landed(rows_out.at[1], rr.at[1])
-        if diag:
-            keep_rows.wait()
-            net.copy(other, rows_out.at[0], rs.at[0], rr.at[0], net.to(t=1 - t)).wait_send()
-        else:
-            net.landed(rows_out.at[0], rr.at[0])
-            net.copy(mine, rows_out.at[1], rs.at[0], rr.at[1], net.to(c=1 - c)).wait_send()
-            net.copy(other, rows_out.at[1], rs.at[1], rr.at[1], net.to(c=1 - c, t=1 - t)).wait_send()
-
-    by_role(rows_done)
-
-    def owners_done(diag):
-        for k in ks:
-            for side in range(1 if diag else 2):
-                for i, ch in pairs_first:
-                    for j in range(m_size):
-                        src = grads[ch].at[z ^ k, m ^ j, 0]
-                        net.copy(src, src, cs.at[i, j, k, side], cr.at[i, j, k, 0], net.to(c=1 - c)).wait_send()
-                for i, ch in pairs_last:
-                    src = sum_last[i].at[k, 0]
-                    net.copy(src, src, es.at[i, k, side], er.at[i, k, 0], net.to(c=1 - c)).wait_send()
-
-    by_role(owners_done)
-    net.drain()
-
-
-def scatter(grads, keep, give, terms, m_size, rows):
-    cols = [g.shape[1] for g in grads]
+                net.landed(rows_out.at[0], yr.at[0])
+            for parts in sent:
+                net.copy(*parts()).wait_send()
+
+        return small_send, run, end
+
+    programs = {key: program(*key) for key in SCATTER_ORDER}
+    cuts = {
+        key: [i for i, code in enumerate(codes) if code // 100 == 1] + [len(codes)]
+        for key, codes in SCATTER_ORDER.items()
+    }
+
+    def begin(inner, diag):
+        small_send, run, _ = programs[inner, diag]
+        small_send()
+        run(SCATTER_ORDER[inner, diag][: cuts[inner, diag][0]])
+
+    def part(i, inner, diag):
+        lo, hi = cuts[inner, diag][i : i + 2]
+        programs[inner, diag][1](SCATTER_ORDER[inner, diag][lo:hi])
+
+    by_class(inner_z, role, begin)
+    if fused:
+
+        @pl.loop(0, 2 * Z)
+        def _(i):
+            make(i)
+            for n in range(2 * Z):
+
+                @pl.when(i == n)
+                def _(n=n):
+                    by_class(inner_z, role, functools.partial(part, n))
+
+    else:
+        for n in range(2 * Z):
+            by_class(inner_z, role, functools.partial(part, n))
+    by_class(inner_z, role, lambda inner, diag: programs[inner, diag][2]())
+
+
+def scatter(factors, keep, give, terms, m_size, rows):
+    one, two, acts, att, d_attn, act, d_pre = factors
     width = keep.shape[1]
     block = width // (2 * Z * m_size)
     seq = keep.shape[0] // Z
-    first = [n for ch, n in enumerate(cols) if M_FIRST[ch]]
-    last = [n for ch, n in enumerate(cols) if not M_FIRST[ch]]
-    nf, nl = len(first), len(last)
+    cols = [2 * HEAD_DIM, 2 * HEAD_DIM, act.shape[1], act.shape[1]]
+    parts = [cols[array] // PARTS[array] for array, _, _ in CHUNKS]
+    count = len(CHUNKS)
+    fused = m_size == 2 and 2 * block % 256 == 0
     sem = pltpu.SemaphoreType.DMA
     vmem = lambda *shape: pltpu.VMEM(shape, bf16)
     doubling = m_size.bit_length() - 1 + 4
-    any_spec = pl.BlockSpec(memory_space=pl.ANY)
+    in_place = pl.BlockSpec(memory_space=pl.ANY)
     in_vmem = pl.BlockSpec(memory_space=pltpu.VMEM)
     far = m_size - 1
+    term_shapes = [jax.ShapeDtypeStruct((Z, m_size, 2, block, n), bf16) for n in cols]
+    out_shape = [jax.ShapeDtypeStruct((Z, block, n), bf16) for n in cols]
+    out_shape += [jax.ShapeDtypeStruct((2, rows, width), bf16), jax.ShapeDtypeStruct(terms.shape[1:], f32)]
+    out_specs = [in_place] * 5 + [in_vmem]
+    if fused:
+        inputs = [one, two, acts, att, d_attn, act, d_pre]
+        in_specs = [in_place] * 3 + [in_vmem] * 4
+        out_shape, out_specs = term_shapes + out_shape, [in_place] * 4 + out_specs
+    else:
+        inputs = [g.reshape(s.shape) for g, s in zip(run_grads(*factors), term_shapes)]
+        in_specs = [in_place] * 4
+    scratch = []
+    for n, (_, _, m_first) in zip(parts, CHUNKS):
+        if m_first:
+            scratch += [vmem(m_size, Z, block, n)] * 2 + [vmem(far, Z, block, n)] * 2 + [vmem(Z, block, n)]
+        else:
+            scratch += [vmem(Z, 2, block, n), vmem(far, Z, 2, block, n), vmem(Z, 2, block, n)]
+            scratch += [vmem(Z, block, n)] * 3
+    scratch += [vmem(4, block, n) for n in parts]
+    scratch += [vmem(Z, seq, width)] * 2 + [vmem(5, seq, width), vmem(2, rows, width)]
+    scratch += [pltpu.VMEM(terms.shape, f32)] * 2
+    scratch += [
+        sem((Z, 2)),
+        sem((Z, 2)),
+        sem((Z,)),
+        sem((Z, 2)),
+        sem((5, 2)),
+        sem((2,)),
+        sem((2,)),
+        sem,
+        sem((count, m_size, Z, 2)),
+        sem((count, m_size, Z, 2)),
+        sem((count, m_size, Z)),
+        sem((count, m_size, Z)),
+        sem((count, m_size, Z)),
+        sem((count, m_size, Z)),
+        sem((count, m_size, Z)),
+        sem((count, Z)),
+        sem((count, Z)),
+        sem((count,)),
+        sem((count, 4)),
+        sem((count, 4)),
+        sem((doubling,)),
+        sem((doubling,)),
+    ]
+    if fused:
+        scratch.append(vmem(2, 3, keep.shape[0], 2 * block))
+        made = [vmem(2, block, n) for n in cols]
+        scratch_made = [sem((2, 3)), sem((4,))]
     outs = pl.pallas_call(
-        functools.partial(scatter_kernel, m_size),
-        out_shape=[jax.ShapeDtypeStruct((Z, block, n), bf16) for n in cols]
-        + [jax.ShapeDtypeStruct((2, rows, width), bf16), jax.ShapeDtypeStruct(terms.shape[1:], f32)],
-        in_specs=[any_spec] * 6 + [in_vmem],
-        out_specs=[any_spec] * 5 + [in_vmem],
-        scratch_shapes=[vmem(m_size, Z, block, n) for n in first] * 2
-        + [vmem(far, Z, block, n) for n in first] * 2
-        + [vmem(Z, block, n) for n in first]
-        + [vmem(Z, 2, block, n) for n in last]
-        + [vmem(far, Z, 2, block, n) for n in last]
-        + [vmem(Z, 2, block, n) for n in last]
-        + [vmem(Z, block, n) for n in last] * 3
-        + [vmem(Z, seq, width)] * 3
-        + [vmem(3, seq, width), vmem(seq, width), vmem(seq, width)]
-        + [pltpu.VMEM(terms.shape, f32)] * 2
-        + [
-            sem((nf, m_size, Z)),
-            sem((nf, m_size, Z, 2)),
-            sem((nf, m_size, Z, 2)),
-            sem((nf, m_size, Z)),
-            sem((nf, m_size, Z)),
-            sem((4, Z)),
-            sem((4, Z)),
-            sem((4,)),
-            sem((nl, Z)),
-            sem((nl, m_size, Z)),
-            sem((nl, m_size, Z)),
-            sem((nl, Z, 2)),
-            sem((nl, Z, 2)),
-            sem((Z,)),
-            sem((Z,)),
-            sem((Z,)),
-            sem((Z,)),
-            sem((Z,)),
-            sem((2,)),
-            sem((2,)),
-            sem,
-            sem((doubling,)),
-            sem((doubling,)),
-        ],
-        compiler_params=pltpu.CompilerParams(
-            collective_id=1, has_side_effects=True, vmem_limit_bytes=60 * 1024 * 1024
-        ),
+        functools.partial(scatter_entry, m_size, fused),
+        out_shape=out_shape,
+        in_specs=in_specs + [in_place] * 2 + [in_vmem],
+        out_specs=out_specs,
+        scratch_shapes=scratch + (made + scratch_made if fused else []),
+        compiler_params=pltpu.CompilerParams(collective_id=1, has_side_effects=True, vmem_limit_bytes=67043328),
         name="scatter_all",
-    )(
-        *[g.reshape(Z, m_size, 2, block, -1) for g in grads],
-        keep.reshape(Z, seq, width),
-        give.reshape(Z, seq, width),
-        terms,
-    )
+    )(*inputs, keep.reshape(Z, seq, width), give.reshape(Z, seq, width), terms)
+    outs = outs[4:] if fused else outs
     return outs[:4], outs[4], outs[5]
+
+
+def scatter_entry(m_size, fused, *refs):
+    if fused:
+        refs = refs[:-6] + (refs[-6:-2],) + refs[-2:]
+    scatter_kernel(m_size, fused, *refs)
 
 
 def adam_kernel(per, *refs):
@@ -1017,7 +1167,7 @@
     one_low, attended, d_attn, head_sums = run_attention(acts, w_qk, w_vo, par, head_bias, places)
     two_low, activation, d_pre, up_sums = run_hidden(acts, w_up, w_dn, par, up_bias)
     keep, give, norm_sums = run_outs(diag, attended, d_attn, activation, d_pre, acts, weights, par)
-    weight_grads = run_grads(one_low, two_low, acts, attended, d_attn, activation, d_pre)
+    factors = (one_low, two_low, acts, attended, d_attn, activation, d_pre)
 
     spread_cols = lambda v, n: lax.dynamic_update_slice_in_dim(
         jnp.zeros((n,), f32), v, head * v.shape[0], 0
@@ -1038,7 +1188,7 @@
     places_of = table_order(grid.m)
     terms = jnp.take(terms, jnp.array([places_of.index(i) for i in range(devices)]), axis=0)
     terms = jnp.pad(terms, ((0, 0), (0, tile - 12 * part))).reshape(devices, -1, 128)
-    own, own_rows, own_small = scatter(weight_grads, keep, give, terms, grid.m, rows)
+    own, own_rows, own_small = scatter(factors, keep, give, terms, grid.m, rows)
     y_rows, u_rows = own_rows[0].astype(f32), own_rows[1].astype(f32)
     block_out = block_in + y_rows + small_all[6] + small_all[7]
     input_grad = out_grad + inverse * (

time: 466 us -> 419 us (0.90); the launches traced: 465 us -> 412 us
  Pallas kernels: 433 us -> 376 us
    pallas_call x2 -> x1, Pallas kernels: 207 us -> 149 us  [scatter(): pl.pallas_call(functools.partial(scatter_entry, m_size, fused), out_shape...]
where the time goes in v3:
time: 419 us; the launch traced here: 412 us
  Pallas kernels  376 us (90%)
  other arithmetic  22.2 us (5%)
  local copies, waits for them, and re-layouts  12.6 us (3%)
    pallas_call x1, Pallas kernels, scatter(): pl.pallas_call(functools.partial(scatter_entry, m_size, fused), out_shape...  149 us
    pallas_call x1, Pallas kernels, gather(): pl.pallas_call(functools.partial(gather_kernel, m_size), out_shape=[shape...  142 us
    pallas_call x2, Pallas kernels, adam_update(): pl.pallas_call(functools.partial(adam_kernel, per), grid=(Z,), in_specs=[...  24.1 us
    pallas_call x1, Pallas kernels, run_outs(): pl.pallas_call(outs_kernel, grid_spec=pltpu.PrefetchScalarGridSpec(num_sc...  21.6 us
    pallas_call x1, Pallas kernels, run_hidden(): pl.pallas_call(hidden_kernel, grid=(hidden // step,), in_specs=[act(0), a...  17.1 us
    pallas_call x1, Pallas kernels, run_attention(): pl.pallas_call(attn_kernel, grid=(Z,), in_specs=[act(0), act(1), fixed(wi...  12.7 us
    pallas_call x1, Pallas kernels, split_weights(): pl.pallas_call(split_kernel, grid=(rows // step,), in_specs=[pl.BlockSpec...  8.65 us

profile of v3, /device:TPU:0, one launch (start us, length us, event | category | flops | bytes accessed | tf_op | source)
XLA Modules:
  0.0 411.8 jit_solution(13529056201393676272)
XLA Ops:
  0.7 1.4 reduce_sum.45
  2.2 1.5 multiply_reduce_fusion
  5.1 0.8 reshape.233
  7.1 1.4 fusion.13
  8.7 1.1 pad_maximum_fusion.refs_4_
  9.8 8.6 %split_weights.1 = (bf16[4,128,512]{2,1,0:T(8,128)(2,1)}, bf16[4,128,512]{2,1,0:T(8,128)(2,1)}, bf16[4,128,1024]{2,1,0:T(8,128)(2,1)}, bf16[4,128,1024]{2,1,0:T(8,128)(2,1)}) custom-call(f32[128,4,1024]{2,1,0:T(4,128)} %refs_2_.2, f32[128,2,4096]{2,1,0:T(2,128)} %refs_2_.3), custom_call_target="tpu_custom_call" | custom-call | tf_op jit(solution)/shard_map/split_weights/pallas_call | solution.py:72
  18.4 141.9 %gather_all.1 = (bf16[2048,512]{1,0:T(8,128)(2,1)}, bf16[2048,512]{1,0:T(8,128)(2,1)}, bf16[2048,1024]{1,0:T(8,128)(2,1)}, bf16[2048,1024]{1,0:T(8,128)(2,1)}, b...) custom-call(bf16[4,128,512]{2,1,0:T(8,128)(2,1)} %get-tuple-element., ...), custom_call_target="tpu_custom_call" | custom-call | tf_op jit(solution)/shard_map/gather_all/pallas_call | solution.py:429
  160.3 1.0 copy.44
  166.4 0.7 slice.48.par
  167.3 0.9 broadcast_select_fusion.down
  168.2 3.2 fusion.9
  171.3 12.7 %attention.1 = (bf16[1024,2048]{1,0:T(8,128)(2,1)}, bf16[1024,256]{1,0:T(8,128)(2,1)}, bf16[1024,768]{1,0:T(8,128)(2,1)}, f32[2,256]{1,0:T(2,128)}) custom-call(bf16[2,1024,2048]{2,1,0:T(8,128)(2,1)} %get-tuple-element.53.x.g.refs_2_, bf16[2,1024,2048]{2,1,0:T(8,128)(2,1)} %get-tuple-element.53.x.g.refs_2_, bf16[2048,512]{1,0:T(8,128)(2,1)} %get-tuple-element.54.w_qk, ...), custom_call_target="tpu_custom_call" | custom-call | tf_op jit(solution)/shard_map/attention/pallas_call | solution.py:536
  184.0 0.7 slice_dynamic-update-slice_fusion
  187.4 17.1 %hidden_units.1 = (bf16[1024,2048]{1,0:T(8,128)(2,1)}, bf16[1024,1024]{1,0:T(8,128)(2,1)}, bf16[1024,1024]{1,0:T(8,128)(2,1)}, f32[1,1024]{1,0:T(1,128)}) custom-call(bf16[2,1024,2048]{2,1,0:T(8,128)(2,1)} %get-tuple-element.53.x.g.refs_2_, bf16[2,1024,2048]{2,1,0:T(8,128)(2,1)} %get-tuple-element.53.x.g.refs_2_, ...), custom_call_target="tpu_custom_call" | custom-call | tf_op jit(solution)/shard_map/hidden_units/pallas_call | solution.py:570
  204.6 21.6 %outputs.1 = (bf16[1024,2048]{1,0:T(8,128)(2,1)}, bf16[1024,2048]{1,0:T(8,128)(2,1)}, f32[4,2048]{1,0:T(4,128)}) custom-call(s32[1]{0:T(128)} %bitcast.7.flag, bf16[1024,256]{1,0:T(8,128)(2,1)} %get-tuple-element.61.att.refs_3_, bf16[1024,768]{1,0:T(8,128)(2,1)} %get-tuple-element.62.d_attn.refs_4_, bf16[1024,1024]{1,0:T(8,128)(2,1)} %get-tuple-element.63.act.refs_5_, ...), custom_call_target="tpu_custom_call" | custom-call | tf_op jit(solution)/shard_map/outputs/pallas_call | solution.py:601
  226.6 0.9 concatenate.18
  229.0 149.4 %scatter_all.1 = (bf16[4,2,2,128,512]{4,3,2,1,0:T(8,128)(2,1)}, bf16[4,2,2,128,512]{4,3,2,1,0:T(8,128)(2,1)}, bf16[4,2,2,128,1024]{4,3,2,1,0:T(8,128)(2,1)}, bf1...) custom-call(bf16[1024,2048]{1,0:T(8,128)(2,1)} %get-tuple-element.57, ...), custom_call_target="tpu_custom_call" | custom-call | tf_op jit(solution)/shard_map/scatter_all/pallas_call | solution.py:1081
  378.5 1.7 fusion.5
  380.2 1.2 convert_reduce_fusion
  381.4 0.7 reshape.244
  382.1 1.4 multiply_subtract_fusion
  383.5 3.7 fusion.4
  387.2 10.0 %adam_update.2 = (f32[128,4,1024]{2,1,0:T(4,128)}, f32[128,4,1024]{2,1,0:T(4,128)}, f32[128,4,1024]{2,1,0:T(4,128)}, f32[128,4,1024]{2,1,0:T(4,128)}) custom-call(bf16[4,128,512]{2,1,0:T(8,128)(2,1)} %get-tuple-element.71.refs_0_, bf16[4,128,512]{2,1,0:T(8,128)(2,1)} %get-tuple-element.72.refs_1_, f32[128,4,1024]{2,1,0:T(4,128)} %refs_2_.2, ...), custom_call_target="tpu_custom_call" | custom-call | tf_op jit(solution)/shard_map/adam_update/pallas_call | solution.py:1115
  397.1 14.2 %adam_update.3 = (f32[128,2,4096]{2,1,0:T(2,128)}, f32[128,2,4096]{2,1,0:T(2,128)}, f32[128,2,4096]{2,1,0:T(2,128)}, f32[128,2,4096]{2,1,0:T(2,128)}) custom-call(bf16[4,128,1024]{2,1,0:T(8,128)(2,1)} %get-tuple-element.74.refs_0_, bf16[4,128,1024]{2,1,0:T(8,128)(2,1)} %get-tuple-element.75.refs_1_, f32[128,2,4096]{2,1,0:T(2,128)} %refs_2_.3, ...), custom_call_target="tpu_custom_call" | custom-call | tf_op jit(solution)/shard_map/adam_update/pallas_call | solution.py:1115
  (70 shorter events, 12.6 us)
Async XLA Ops:
  0.6 7.9 %copy-start = (f32[128,2048]{1,0:T(8,128)S(1)}, f32[128,2048]{1,0:T(8,128)}, u32[]{:S(2)}) copy-start(f32[128,2048]{1,0:T(8,128)} %param.16) | copy-start | bytes 3145732
  2.2 5.0 %copy-start.2 = (f32[128]{0:T(128)}, f32[128]{0:T(128)S(1)}, u32[]{:S(2)}) copy-start(f32[128]{0:T(128)S(1)} %broadcast_multiply_fusion.2) | copy-start | bytes 1540
  3.7 3.4 copy-start.3
  204.6 21.6 %copy-start.4 = (f32[1,1024]{1,0:T(1,128)S(1)}, f32[1,1024]{1,0:T(1,128)}, u32[]{:S(2)}) copy-start(f32[1,1024]{1,0:T(1,128)} %get-tuple-element.69) | copy-start | bytes 12292
  382.1 15.0 %copy-start.1 = (f32[12,64]{1,0:T(8,128)}, f32[12,64]{1,0:T(8,128)S(1)}, u32[]{:S(2)}) copy-start(f32[12,64]{1,0:T(8,128)S(1)} %reshape.244) | copy-start | bytes 9220

commit v4 on v3

--- a/solution.py
+++ b/solution.py
@@ -53,7 +53,10 @@
         self.diag = self.c_now == self.t_now
 
 
-def split_kernel(attn, mlp, qk, vo, up, dn):
+def prepare_kernel(rows, cotangent, attn, mlp, qk, vo, up, dn, low):
+    normed, _ = layer_stats(rows[...])
+    low[0] = normed.astype(bf16)
+    low[1] = cotangent[...].astype(bf16)
     quarter_a = attn.shape[2] // Z
     quarter_m = mlp.shape[2] // Z
     for q in range(Z):
@@ -64,22 +67,30 @@
             (up, dn)[j][q] = mlp[:, j, q * quarter_m : (q + 1) * quarter_m].astype(bf16)
 
 
-def split_weights(attn_weight, mlp_weight):
-    rows, _, width = attn_weight.shape
+def prepare(block_in, out_grad, attn_weight, mlp_weight):
+    own, width = block_in.shape
+    rows, _, half = attn_weight.shape
     hidden = mlp_weight.shape[2]
-    step = min(rows, 32)
-    shapes = [2 * width // Z] * 2 + [hidden // Z] * 2
-    return pl.pallas_call(
-        split_kernel,
-        grid=(rows // step,),
+    step = min(rows, 16)
+    steps = rows // step
+    shapes = [2 * half // Z] * 2 + [hidden // Z] * 2
+    by_rows = pl.BlockSpec((own // steps, width), lambda i: (i, 0))
+    outs = pl.pallas_call(
+        prepare_kernel,
+        grid=(steps,),
         in_specs=[
-            pl.BlockSpec((step, 4, width), lambda i: (i, 0, 0)),
+            by_rows,
+            by_rows,
+            pl.BlockSpec((step, 4, half), lambda i: (i, 0, 0)),
             pl.BlockSpec((step, 2, hidden), lambda i: (i, 0, 0)),
         ],
-        out_specs=[pl.BlockSpec((Z, step, n), lambda i: (0, i, 0)) for n in shapes],
-        out_shape=[jax.ShapeDtypeStruct((Z, rows, n), bf16) for n in shapes],
-        name="split_weights",
-    )(attn_weight, mlp_weight)
+        out_specs=[pl.BlockSpec((Z, step, n), lambda i: (0, i, 0)) for n in shapes]
+        + [pl.BlockSpec((2, own // steps, width), lambda i: (0, i, 0))],
+        out_shape=[jax.ShapeDtypeStruct((Z, rows, n), bf16) for n in shapes]
+        + [jax.ShapeDtypeStruct((2, own, width), bf16)],
+        name="prepare",
+    )(block_in, out_grad, attn_weight, mlp_weight)
+    return outs[:4], outs[4]
 
 
 MESH = pl.DeviceIdType.MESH
@@ -87,28 +98,38 @@
 CHUNKS = ((0, 0, True), (1, 0, False), (2, 0, True), (2, 1, False), (3, 0, True), (3, 1, False))
 GATHER_ORDER = {
     (False, False): (
-        0, 10, 500, 510, 520, 530, 540, 550, 700, 600, 501, 900, 620, 511, 910, 640, 601, 801, 502, 710, 20, 30, 40,
-        50, 512, 602, 610, 920, 630, 811, 521, 650, 531, 621, 541, 551, 641, 611, 930, 802, 940, 503, 612, 513, 603,
-        631, 651, 812, 522, 532, 622, 542, 552, 632, 642, 613, 652, 803, 813, 523, 533, 623, 543, 553, 633, 643, 653,
+        0, 10, 500, 510, 520, 530, 540, 550, 700, 20, 1100, 600, 501, 900, 620, 511, 910, 640, 601, 1101, 801, 1110,
+        521, 710, 30, 40, 50, 502, 621, 512, 602, 610, 1010, 630, 811, 1111, 920, 1030, 650, 531, 1000, 541, 551,
+        1050, 1020, 641, 611, 930, 1040, 1001, 802, 1011, 522, 1120, 940, 503, 1021, 622, 513, 612, 603, 1002, 1012,
+        631, 651, 812, 1121, 1041, 1031, 532, 1051, 542, 1022, 552, 642, 1003, 632, 613, 652, 803, 1042, 1032, 523,
+        1013, 1200, 1052, 1130, 1201, 623, 1202, 1023, 813, 1131, 1203, 533, 1204, 543, 1205, 553, 633, 643, 653,
+        1043, 1033, 1206, 1207, 1053, 1208, 1209, 1210, 1211,
     ),
     (False, True): (
-        0, 10, 700, 500, 510, 520, 530, 540, 550, 610, 630, 650, 600, 501, 900, 620, 511, 611, 640, 710, 20, 30, 40,
-        50, 801, 910, 601, 502, 602, 811, 521, 930, 531, 621, 541, 940, 551, 641, 631, 512, 612, 651, 920, 802, 503,
-        603, 812, 522, 532, 622, 542, 552, 642, 632, 513, 613, 652, 803, 813, 523, 533, 623, 543, 633, 553, 643, 653,
+        0, 10, 700, 20, 500, 510, 520, 530, 540, 550, 610, 630, 650, 501, 600, 1100, 900, 1000, 511, 620, 1020, 611,
+        640, 1040, 710, 30, 40, 50, 1010, 1030, 801, 1050, 601, 1001, 521, 910, 1110, 1011, 502, 1101, 621, 1021,
+        602, 1002, 811, 531, 541, 1111, 930, 631, 551, 641, 512, 612, 940, 651, 1031, 1041, 920, 1012, 802, 522,
+        1120, 1051, 503, 622, 1022, 603, 1003, 812, 532, 542, 1121, 632, 552, 642, 513, 613, 652, 1032, 1042, 1013,
+        1200, 1052, 1201, 803, 1202, 523, 1130, 623, 1023, 813, 533, 1131, 1203, 543, 1204, 633, 553, 1205, 643, 653,
+        1043, 1033, 1206, 1207, 1208, 1053, 1209, 1210, 1211,
     ),
     (True, False): (
-        0, 10, 500, 510, 520, 530, 540, 550, 900, 700, 600, 200, 503, 620, 100, 300, 640, 501, 513, 603, 210, 310,
-        601, 110, 511, 710, 20, 30, 40, 50, 803, 400, 610, 801, 502, 910, 410, 630, 512, 602, 650, 811, 220, 813,
-        120, 920, 523, 521, 320, 230, 623, 533, 130, 613, 621, 330, 531, 543, 240, 340, 140, 611, 553, 541, 643, 350,
-        250, 930, 150, 551, 641, 940, 802, 612, 633, 631, 812, 653, 420, 651, 522, 430, 532, 622, 440, 542, 632, 450,
-        642, 552, 652,
+        0, 10, 500, 510, 520, 530, 540, 550, 900, 700, 20, 1100, 600, 200, 503, 620, 100, 300, 640, 501, 513, 603,
+        210, 310, 1101, 601, 110, 511, 710, 30, 40, 50, 803, 523, 1130, 610, 801, 320, 623, 220, 400, 1110, 630,
+        1010, 120, 502, 521, 410, 910, 650, 512, 1030, 1000, 602, 621, 1050, 1020, 1131, 811, 1040, 813, 230, 1111,
+        533, 130, 920, 613, 330, 531, 1003, 543, 240, 1001, 1013, 340, 140, 611, 553, 643, 541, 350, 250, 1023, 150,
+        1011, 551, 641, 930, 802, 612, 420, 1120, 1002, 940, 522, 1021, 1012, 1200, 633, 622, 631, 1201, 1202, 653,
+        1043, 1033, 1031, 812, 651, 430, 1121, 1203, 532, 1022, 1041, 1053, 1204, 1051, 440, 1205, 542, 632, 450,
+        552, 642, 1032, 1206, 652, 1207, 1042, 1208, 1052, 1209, 1210, 1211,
     ),
     (True, True): (
-        0, 10, 700, 500, 510, 520, 530, 540, 550, 900, 610, 630, 650, 600, 200, 503, 620, 100, 300, 640, 501, 513,
-        613, 710, 20, 30, 40, 50, 210, 310, 110, 511, 611, 603, 601, 803, 400, 801, 502, 910, 602, 813, 811, 523,
-        220, 320, 120, 623, 533, 930, 521, 330, 230, 940, 543, 130, 621, 633, 340, 531, 643, 631, 553, 240, 350, 140,
-        410, 541, 653, 512, 612, 250, 920, 641, 150, 551, 651, 802, 812, 420, 522, 430, 622, 532, 632, 440, 542, 450,
-        642, 552, 652,
+        0, 10, 700, 20, 500, 510, 520, 530, 540, 550, 900, 610, 630, 650, 600, 200, 503, 1100, 1000, 620, 100, 300,
+        1020, 640, 501, 513, 1040, 710, 30, 613, 40, 50, 210, 310, 1010, 110, 1030, 511, 611, 1050, 603, 1003, 601,
+        1001, 803, 1101, 1013, 523, 1130, 801, 320, 1011, 220, 400, 1110, 623, 1023, 120, 502, 521, 910, 602, 621,
+        1002, 813, 1021, 533, 811, 330, 230, 1111, 543, 1131, 130, 633, 930, 340, 531, 643, 631, 553, 240, 350, 140,
+        1033, 410, 541, 940, 653, 1043, 512, 612, 250, 1031, 150, 641, 551, 651, 920, 1053, 1041, 802, 1012, 1200,
+        420, 1120, 1201, 522, 1051, 1202, 622, 1022, 812, 430, 1121, 1203, 532, 1204, 632, 440, 1205, 542, 450, 1032,
+        1206, 552, 642, 1207, 652, 1042, 1208, 1209, 1052, 1210, 1211,
     ),
 }
 SCATTER_ORDER = {
@@ -208,17 +229,22 @@
 
 
 def gather_kernel(m_size, *refs):
-    pieces, low, mine_small = refs[:4], refs[4], refs[5]
-    full, act, table = refs[6:10], refs[10], refs[11]
+    pieces, low, mine_small, base = refs[:4], refs[4], refs[5], refs[6]
+    full, act_out, one_out, two_out = refs[7:11], refs[11], refs[12], refs[13]
+    att, d_attn, hidden_out, d_pre, head_sums, up_sums, table = refs[14:21]
     count = len(CHUNKS)
-    stage, stage_m, relay = (refs[12 + i * count : 12 + (i + 1) * count] for i in range(3))
-    refs = refs[12 + 3 * count :]
-    (zs, zr, gs, gr, ps, pr, ms, mr, near_s, far_s, xr, as_, ar, ws, wr, ss, sr, lin, lout) = refs[:19]
-    bounce, bounce_low = refs[19 : 19 + count], refs[19 + count]
+    stage, stage_m, relay = (refs[21 + i * count : 21 + (i + 1) * count] for i in range(3))
+    refs = refs[21 + 3 * count :]
+    (zs, zr, gs, gr, ps, pr, ms, mr, near_s, far_s, xr, as_, ar, ws, wr, ss, sr, lin, lout, ls, os_) = refs[:21]
+    bounce, refs = refs[21 : 21 + count], refs[21 + count :]
+    act, w_qk, w_vo, one_v, two_v, tile_v, slope, par, bias, up_bias = refs
     net = Links(m_size)
     z, m, c, t = net.z, net.m, net.c, net.t
     rows = pieces[0].shape[1]
     half = low.shape[1]
+    seq = 2 * half
+    width = low.shape[2]
+    n = HEAD_DIM
     role = lax.rem(c + t, 2)
     inner_z = lax.rem(z + z // 2, 2)
 
@@ -236,35 +262,49 @@
         start = ((zz * m_size + mm) * 2 + cc) * rows
         return full[array].at[pl.ds(pl.multiple_of(start, rows), size * rows), cols]
 
-    own_place = pl.ds(pl.multiple_of(z * 2 * half + t * half, half), half)
-    place = lambda zz, h: pl.ds(pl.multiple_of(zz * 2 * half + (t ^ h) * half, half), half)
-
-    loads = [pltpu.make_async_copy(piece(ch, z), bounce[ch], lin.at[ch]) for ch in range(count)]
-    loads.append(pltpu.make_async_copy(low.at[0], bounce_low, lin.at[count]))
-    stores = [pltpu.make_async_copy(bounce[ch], whole(ch, z, m, c), lout.at[ch]) for ch in range(count)]
-    stores.append(pltpu.make_async_copy(bounce_low, act.at[0, own_place], lout.at[count]))
+    own_place = pl.ds(pl.multiple_of(z * seq + t * half, half), half)
+    place = lambda zz, h: pl.ds(pl.multiple_of(zz * seq + (t ^ h) * half, half), half)
+
+    def load_own(ch):
+        return pltpu.make_async_copy(piece(ch, z), bounce[ch], lin.at[ch])
+
+    def store_own(ch):
+        return pltpu.make_async_copy(bounce[ch], whole(ch, z, m, c), lout.at[ch])
+
+    def low_own():
+        return pltpu.make_async_copy(low.at[0], act.at[0, own_place], lin.at[count])
 
     @pl.when(role == 0)
     def _():
-        for one in loads:
-            one.start()
-
+        for ch in range(count):
+            load_own(ch).start()
+        low_own().start()
+
+    flat, steps = net.doubling()
+    pltpu.make_async_copy(mine_small, table.at[flat], ss.at[len(steps)]).start()
     net.meet()
-    flat, steps = net.doubling()
-    small_own = pltpu.make_async_copy(mine_small, table.at[flat], ss.at[len(steps)])
-    small_own.start()
+    pltpu.make_async_copy(mine_small, table.at[flat], ss.at[len(steps)]).wait()
 
     def program(inner, diag):
         state = {"small": 0}
+        sent = []
+
+        def send(parts):
+            net.copy(*parts()).start()
+            sent.append(parts)
 
         def small_send():
             i = state["small"]
             if i < len(steps):
                 size, target = steps[i]
-                span = table.at[pl.ds(flat // size * size, size)]
-                net.send(span, span, ss.at[i], sr.at[i], target)
-
-        def small_next():
+
+                def parts():
+                    span = table.at[pl.ds(flat // size * size, size)]
+                    return span, span, ss.at[i], sr.at[i], target
+
+                send(parts)
+
+        def small_next(*_):
             i = state["small"]
             if i < len(steps):
                 size = steps[i][0]
@@ -272,6 +312,10 @@
                 state["small"] += 1
                 small_send()
 
+        def small_last():
+            while state["small"] < len(steps):
+                small_next()
+
         def spot(ch, zz, j):
             if diag:
                 return whole(ch, zz, m ^ j, c)
@@ -281,44 +325,67 @@
             return piece(ch, z) if k == 0 and j == 0 else spot(ch, z ^ k, j)
 
         def spread(ch, k, j):
-            src, dst = source(ch, k, j), whole(ch, z ^ k, m ^ j, c)
-            net.send(src, dst, ps.at[ch, j, k, 1], pr.at[ch, j, k, c], net.to(c=t, t=1 - t))
+            block = lambda: whole(ch, z ^ k, m ^ j, c)
+            send(
+                lambda: (
+                    source(ch, k, j),
+                    block(),
+                    ps.at[ch, j, k, 1],
+                    pr.at[ch, j, k, c],
+                    net.to(c=t, t=1 - t),
+                )
+            )
             if not diag:
-                net.send(src, dst, ps.at[ch, j, k, 0], pr.at[ch, j, k, c], net.to(c=1 - c))
+                send(
+                    lambda: (source(ch, k, j), block(), ps.at[ch, j, k, 0], pr.at[ch, j, k, c], net.to(c=1 - c))
+                )
 
         def spread_landed(ch, k, j):
             for cc in (1 - c,) if diag else (1 - c, c):
                 net.landed(whole(ch, z ^ k, m ^ j, cc), pr.at[ch, j, k, cc])
 
         def swap(h, k):
-            src = act.at[role, place(z ^ k, h)]
-            net.send(src, src, ws.at[k, h], wr.at[k, h], net.to(c=1 - c))
-
-        def rows_on(h, block, i, hop, k):
-            src = act.at[role, place(block, h)]
-            net.send(src, src, as_.at[h, i], ar.at[h, k], net.to(z=z ^ hop))
+            def parts():
+                src = act.at[role, place(z ^ k, h)]
+                return src, src, ws.at[k, h], wr.at[k, h], net.to(c=1 - c)
+
+            send(parts)
+
+        def rows_on(h, flip, i, hop, k):
+            def parts():
+                src = act.at[role, place(z ^ flip, h)]
+                return src, src, as_.at[h, i], ar.at[h, k], net.to(z=z ^ hop)
+
+            send(parts)
 
         def quarters(ch, _):
             for i, (k, hop, through) in enumerate(
                 ((3, 3, None), (2, 3, 2), (1, 1, None)) if inner else ((3, 1, 1), (2, 1, 0), (1, 1, None))
             ):
-                target = net.to(z=z ^ hop)
-                if through is None:
-                    net.send(piece(ch, z ^ k), spot(ch, z, 0), zs.at[ch, i], zr.at[ch, k], target)
-                else:
-                    net.send(piece(ch, z ^ k), relay[ch].at[through], zs.at[ch, i], gr.at[ch, through], target)
+
+                def parts(i=i, k=k, hop=hop, through=through):
+                    if through is None:
+                        dst, recv_sem = spot(ch, z, 0), zr.at[ch, k]
+                    else:
+                        dst, recv_sem = relay[ch].at[through], gr.at[ch, through]
+                    return piece(ch, z ^ k), dst, zs.at[ch, i], recv_sem, net.to(z=z ^ hop)
+
+                send(parts)
 
         def pass_on(through):
             hop, k = ((3, 2), (3, None), (1, 2), (1, 3))[through]
 
             def run(ch, _):
-                src = relay[ch].at[through]
-                net.landed(src, gr.at[ch, through])
-                if k is None:
-                    net.send(src, relay[ch].at[3], gs.at[ch, through], gr.at[ch, 3], net.to(z=z ^ hop))
-                else:
-                    dst = spot(ch, z ^ hop ^ k, 0)
-                    net.send(src, dst, gs.at[ch, through], zr.at[ch, k], net.to(z=z ^ hop))
+                net.landed(relay[ch].at[through], gr.at[ch, through])
+
+                def parts():
+                    if k is None:
+                        dst, recv_sem = relay[ch].at[3], gr.at[ch, 3]
+                    else:
+                        dst, recv_sem = spot(ch, z ^ hop ^ k, 0), zr.at[ch, k]
+                    return relay[ch].at[through], dst, gs.at[ch, through], recv_sem, net.to(z=z ^ hop)
+
+                send(parts)
 
             return run
 
@@ -327,8 +394,12 @@
                 net.landed(spot(ch, z ^ k, 0), zr.at[ch, k])
             if CHUNKS[ch][2]:
                 for j in range(1, m_size):
-                    dst = whole(ch, z ^ k, m, c) if diag else stage_m[ch].at[m, z ^ k]
-                    net.send(source(ch, k, 0), dst, ms.at[ch, j, k], mr.at[ch, j, k], net.to(m=m ^ j))
+
+                    def parts(j=j):
+                        dst = whole(ch, z ^ k, m, c) if diag else stage_m[ch].at[m, z ^ k]
+                        return source(ch, k, 0), dst, ms.at[ch, j, k], mr.at[ch, j, k], net.to(m=m ^ j)
+
+                    send(parts)
             spread(ch, k, 0)
 
         def second(ch, k):
@@ -338,64 +409,238 @@
                     spread(ch, k, j)
             else:
                 if diag and k == 0:
-                    stores[ch].wait()
+                    store_own(ch).wait()
                 spread_landed(ch, k, 0)
-                both = whole(ch, z ^ k, m, 0, 2)
                 for j in range(1, m_size):
-                    net.send(both, both, ms.at[ch, j, k], mr.at[ch, j, k], net.to(m=m ^ j))
+
+                    def parts(j=j):
+                        both = whole(ch, z ^ k, m, 0, 2)
+                        return both, both, ms.at[ch, j, k], mr.at[ch, j, k], net.to(m=m ^ j)
+
+                    send(parts)
+
+        def third(ch, k):
+            if CHUNKS[ch][2]:
+                for j in range(m_size):
+                    spread_landed(ch, k, j)
+                if diag and k == 0:
+                    store_own(ch).wait()
+            else:
+                for j in range(1, m_size):
+                    net.landed(whole(ch, z ^ k, m ^ j, 0, 2), mr.at[ch, j, k])
 
         def rows_start(h, _):
             if h:
                 net.landed(act.at[0 if diag else 1, place(z, 1)], xr.at[1])
             elif diag:
-                stores[count].wait()
+                low_own().wait()
             else:
                 net.landed(act.at[1, place(z, 0)], xr.at[0])
             if inner:
-                rows_on(h, z, 0, 3, 3)
-            rows_on(h, z, 1, 1, 1)
+                rows_on(h, 0, 0, 3, 3)
+            rows_on(h, 0, 1, 1, 1)
             swap(h, 0)
 
         def rows_next(h, k):
             net.landed(act.at[role, place(z ^ k, h)], ar.at[h, k])
             if inner:
                 hop, there = {1: (3, 2), 3: (1, 2), 2: (1, 3)}[k]
-                rows_on(h, z ^ k, 1 + k, hop, there)
+                rows_on(h, k, 1 + k, hop, there)
             swap(h, k)
 
-        small_own.wait()
-        small_send()
-        if diag:
-            net.send(low.at[1], act.at[1, own_place], near_s, xr.at[0], net.to(c=1 - c))
-        else:
-            net.send(low.at[0], act.at[0, own_place], near_s, xr.at[1], net.to(t=1 - t))
-            net.send(low.at[1], act.at[1, own_place], far_s, xr.at[1], net.to(c=1 - c, t=1 - t))
-        if diag:
-            for load, store in zip(loads, stores):
-                load.wait()
-                store.start()
-        runs = [quarters] + [pass_on(i) for i in range(4)] + [first, second, rows_start, rows_next]
-        runs.append(lambda *_: small_next())
-        for code in GATHER_ORDER[inner, diag]:
-            runs[code // 100](code // 10 % 10, code % 10)
-        while state["small"] < len(steps):
-            small_next()
-        for ch in range(count):
-            for k in range(Z):
-                if CHUNKS[ch][2]:
-                    for j in range(m_size):
-                        spread_landed(ch, k, j)
-                    if diag and k == 0:
-                        stores[ch].wait()
-                else:
-                    for j in range(1, m_size):
-                        net.landed(whole(ch, z ^ k, m ^ j, 0, 2), mr.at[ch, j, k])
-        for k in range(Z):
-            for h in range(2):
-                net.landed(act.at[1 - role, place(z ^ k, h)], wr.at[k, h])
-        net.drain()
-
-    by_class(inner_z, role, program)
+        def swapped(k, h):
+            net.landed(act.at[1 - role, place(z ^ k, h)], wr.at[k, h])
+
+        def begin():
+            small_send()
+            if diag:
+                send(lambda: (low.at[1], act.at[1, own_place], near_s, xr.at[0], net.to(c=1 - c)))
+                for ch in range(count):
+                    load_own(ch).wait()
+                    store_own(ch).start()
+            else:
+                send(lambda: (low.at[0], act.at[0, own_place], near_s, xr.at[1], net.to(t=1 - t)))
+                send(lambda: (low.at[1], act.at[1, own_place], far_s, xr.at[1], net.to(c=1 - c, t=1 - t)))
+
+        runs = [quarters] + [pass_on(i) for i in range(4)]
+        runs += [first, second, rows_start, rows_next, small_next, third, swapped]
+
+        def run(codes):
+            for code in codes:
+                runs[code // 100](code // 10 % 10, code % 10)
+
+        def end():
+            for parts in sent:
+                net.copy(*parts()).wait_send()
+
+        return begin, run, small_last, end
+
+    programs = {key: program(*key) for key in GATHER_ORDER}
+    work = len(runs_before(GATHER_ORDER[True, True]))
+
+    def device_rows(index):
+        zz, rest = index // (4 * m_size), lax.rem(index, 4 * m_size)
+        return rest * 4 + lax.rem(zz + zz // 2, 2) * 2 + zz // 2
+
+    def parameters():
+        part = width // (8 * m_size * 2)
+        per = 128 // part
+        static = table_order(m_size)
+        for b in range(width // 128):
+            got = [table[static[b * per + e], 0:4, 0:part] for e in range(per)]
+            par[:, b * 128 : (b + 1) * 128] = jnp.concatenate(got, axis=1)
+        head = c * Z + z
+        for b in range(n // 128):
+            start = (head * n + b * 128) // part
+            got = [table[device_rows(start + e), 4:6, 0:part] for e in range(per)]
+            bias[:, b * 128 : (b + 1) * 128] = jnp.concatenate(got, axis=1)
+        wide = up_bias.shape[1]
+        row = 8 + head * wide // width
+        for b in range(wide // 128):
+            start = (lax.rem(head * wide, width) + b * 128) // part
+            got = [table[device_rows(start + e), pl.ds(row, 1), 0:part] for e in range(per)]
+            up_bias[:, b * 128 : (b + 1) * 128] = jnp.concatenate(got, axis=1)
+
+    def weights_in():
+        return [
+            pltpu.make_async_copy(full[0], w_qk, ls.at[0]),
+            pltpu.make_async_copy(full[1], w_vo, ls.at[1]),
+        ]
+
+    def rows_saved(i):
+        k = i ^ (inner_z & (i // 2))
+        span = pl.ds(pl.multiple_of((z ^ k) * seq, seq), seq)
+        return [
+            pltpu.make_async_copy(one_v.at[lax.rem(i, 2)], one_out.at[span], os_.at[0, i]),
+            pltpu.make_async_copy(two_v.at[span], two_out.at[span], os_.at[1, i]),
+            pltpu.make_async_copy(act.at[:, span], act_out.at[:, span], os_.at[2, i]),
+        ]
+
+    def attention(i):
+        @pl.when(i == 0)
+        def _():
+            for one in weights_in():
+                one.start()
+            parameters()
+            head_sums[...] = jnp.zeros_like(head_sums)
+            for one in weights_in():
+                one.wait()
+
+        @pl.when(i >= 2)
+        def _():
+            rows_saved(i - 2)[0].wait()
+
+        k = i ^ (inner_z & (i // 2))
+        span = pl.ds(pl.multiple_of((z ^ k) * seq, seq), seq)
+        x = act[0, span, :].astype(f32)
+        one = (x * par[0:1, :] + par[1:2, :]).astype(bf16)
+        one_v[lax.rem(i, 2)] = one
+        two_v[span, :] = (x * par[2:3, :] + par[3:4, :]).astype(bf16)
+        for copy in rows_saved(i):
+            copy.start()
+        source = device_rows((((z ^ k) * m_size + m) * 2 + t) * 2)
+        across = jnp.concatenate([table[source, 12 + e : 13 + e, :] for e in range(seq // 128)], axis=1)
+        spots = lax.broadcasted_iota(jnp.int32, (seq, seq), 0).astype(f32)
+        hit = jnp.where(spots == across, 1.0, 0.0).astype(bf16)
+        down = dot(hit, spots.astype(bf16), 0, 0)
+        turns = dot(hit, base[...], 0, 0)
+        tables = [sum(turns[:, (3 * a + e) * 128 : (3 * a + e + 1) * 128] for e in range(3)) for a in range(3)]
+        scale = HEAD_DIM ** (-0.5)
+        qk = dot(one, w_qk[...])
+        q = turn(qk[:, :n] + bias[0:1, :], tables, 1.0).astype(bf16)
+        k_rows = turn(qk[:, n:], tables, 1.0).astype(bf16)
+        v = (dot(one, w_vo[:, :n]) + bias[1:2, :]).astype(bf16)
+        d_att = dot(act[1, span, :], w_vo[:, n:]).astype(bf16)
+        scores = jnp.where(across <= down, dot(q, k_rows, 1, 1) * scale, -jnp.inf)
+        top = jnp.max(scores, axis=-1, keepdims=True)
+        log_total = top + jnp.log(jnp.sum(jnp.exp(scores - top), axis=-1, keepdims=True))
+        probs = jnp.exp(scores - log_total)
+        low_probs = probs.astype(bf16)
+        att[span, :] = dot(low_probs, v).astype(bf16)
+        d_probs = dot(d_att, v, 1, 1)
+        d_scores = (probs * (d_probs - jnp.sum(probs * d_probs, axis=-1, keepdims=True)) * scale).astype(bf16)
+        d_q = turn(dot(d_scores, k_rows), tables, -1.0)
+        d_k = turn(dot(d_scores, q, 0, 0), tables, -1.0)
+        d_v = dot(low_probs, d_att, 0, 0)
+        d_attn[span, 0:n] = d_q.astype(bf16)
+        d_attn[span, n : 2 * n] = d_k.astype(bf16)
+        d_attn[span, 2 * n :] = d_v.astype(bf16)
+        head_sums[0:1, :] += jnp.sum(d_q, axis=0, keepdims=True)
+        head_sums[1:2, :] += jnp.sum(d_v, axis=0, keepdims=True)
+
+    wide = pieces[2].shape[2] // Z
+
+    def tile_in(array, j):
+        cols = pl.ds(pl.multiple_of(j * wide, wide), wide)
+        return pltpu.make_async_copy(full[array].at[:, cols], tile_v.at[lax.rem(j, 2)], ls.at[lax.rem(j, 2)])
+
+    def tile_ready(array, j):
+        @pl.when(lax.rem(j, 2) == 0)
+        def _():
+            tile_in(array, j).start()
+            tile_in(array, j + 1).start()
+
+        tile_in(array, j).wait()
+
+    def hidden(i):
+        j = i - Z
+        tile_ready(2, j)
+        cols = pl.ds(pl.multiple_of(j * wide, wide), wide)
+        pre = dot(two_v[...], tile_v[lax.rem(j, 2)]) + up_bias[:, cols]
+        erf = 1.0 + lax.erf(pre * 0.7071067811865476)
+        hidden_out[:, cols] = (0.5 * pre * erf).astype(bf16)
+        slope[j] = 0.5 * erf + pre * jnp.exp(-0.5 * pre * pre) * 0.3989422804014327
+
+    def hidden_back(i):
+        j = i - 2 * Z
+        tile_ready(3, j)
+        cols = pl.ds(pl.multiple_of(j * wide, wide), wide)
+        value = dot(act[1], tile_v[lax.rem(j, 2)]) * slope[j]
+        d_pre[:, cols] = value.astype(bf16)
+        up_sums[:, cols] = jnp.sum(value, axis=0, keepdims=True)
+
+    def begin(inner, diag):
+        start, run, small_last, _ = programs[inner, diag]
+        start()
+        run(runs_before(GATHER_ORDER[inner, diag])[0])
+        small_last()
+
+    def part(i, inner, diag):
+        programs[inner, diag][1](runs_before(GATHER_ORDER[inner, diag])[i + 1])
+
+    by_class(inner_z, role, begin)
+
+    @pl.loop(0, work - 1)
+    def _(i):
+        pl.when(i < Z)(lambda: attention(i))
+        pl.when((i >= Z) & (i < 2 * Z))(lambda: hidden(i))
+        pl.when(i >= 2 * Z)(lambda: hidden_back(i))
+        for e in range(work - 1):
+
+            @pl.when(i == e)
+            def _(e=e):
+                by_class(inner_z, role, functools.partial(part, e))
+
+    by_class(inner_z, role, lambda inner, diag: programs[inner, diag][3]())
+    for i in range(Z):
+        saved = rows_saved(i)
+        for copy in saved[1:] if i < 2 else saved:
+            copy.wait()
+
+
+def runs_before(order):
+    cuts = [i for i, code in enumerate(order) if code // 100 == 12]
+    return [order[lo:hi] for lo, hi in zip([0] + [i + 1 for i in cuts], cuts + [len(order)])]
+
+
+def turn_base(seq):
+    terms = []
+    for value in turn_tables(jnp.arange(seq).astype(f32)):
+        for _ in range(3):
+            low = lax.reduce_precision(value, 8, 7)
+            terms.append(low.astype(bf16))
+            value = value - low
+    return jnp.concatenate(terms, axis=1)
 
 
 def table_order(m_size):
@@ -417,7 +662,8 @@
 
 def gather(pieces, low, small, m_size):
     rows = pieces[0].shape[1]
-    width = low.shape[2]
+    own, width = low.shape[1:]
+    tokens = Z * 2 * own
     devices = m_size * 4 * Z
     cols = [p.shape[2] for p in pieces]
     count = len(CHUNKS)
@@ -425,16 +671,22 @@
     sem = pltpu.SemaphoreType.DMA
     doubling = m_size.bit_length() - 1 + 4
     in_place = pl.BlockSpec(memory_space=pl.ANY)
+    in_vmem = pl.BlockSpec(memory_space=pltpu.VMEM)
     shape = lambda *dims: jax.ShapeDtypeStruct(dims, bf16)
+    exact = lambda *dims: jax.ShapeDtypeStruct(dims, f32)
+    hidden, n = cols[2], HEAD_DIM
+    vmem = lambda *dims: pltpu.VMEM(dims, bf16)
     outs = pl.pallas_call(
         functools.partial(gather_kernel, m_size),
         out_shape=[shape(width, n) for n in cols]
-        + [shape(2, Z * 2 * low.shape[1], width), jax.ShapeDtypeStruct((devices,) + small.shape, f32)]
+        + [shape(2, tokens, width), shape(tokens, width), shape(tokens, width)]
+        + [shape(tokens, n), shape(tokens, 3 * n), shape(tokens, hidden), shape(tokens, hidden)]
+        + [exact(2, n), exact(1, hidden), exact(devices, *small.shape)]
         + [shape(Z, rows, n) for n in parts]
         + [shape(m_size, Z, rows, n) for n in parts]
         + [shape(4, rows, n) for n in parts],
-        in_specs=[in_place] * 6,
-        out_specs=[in_place] * (6 + 3 * count),
+        in_specs=[in_place] * 6 + [in_vmem],
+        out_specs=[in_place] * 7 + [in_vmem] * 7 + [in_place] * (3 * count),
         scratch_shapes=[
             sem((count, 3)),
             sem((count, Z)),
@@ -454,14 +706,18 @@
             sem((doubling + 1,)),
             sem((doubling,)),
             sem((count + 1,)),
-            sem((count + 1,)),
+            sem((count,)),
+            sem((2,)),
+            sem((3, Z)),
         ]
-        + [pltpu.VMEM((rows, n), bf16) for n in parts]
-        + [pltpu.VMEM(low.shape[1:], bf16)],
-        compiler_params=pltpu.CompilerParams(collective_id=0, has_side_effects=True),
+        + [vmem(rows, n) for n in parts]
+        + [vmem(2, tokens, width), vmem(width, 2 * n), vmem(width, 2 * n), vmem(2, 2 * own, width)]
+        + [vmem(tokens, width), vmem(2, width, hidden // Z), pltpu.VMEM((Z, tokens, hidden // Z), f32)]
+        + [pltpu.VMEM((4, width), f32), pltpu.VMEM((2, n), f32), pltpu.VMEM((1, hidden), f32)],
+        compiler_params=pltpu.CompilerParams(collective_id=0, has_side_effects=True, vmem_limit_bytes=67043328),
         name="gather_all",
-    )(*pieces, low, small)
-    return outs[:4], outs[4], outs[5]
+    )(*pieces, low, small, turn_base(2 * own))
+    return outs[:4], outs[4], outs[5:7], outs[7:11], outs[11:13], outs[13]
 
 
 VMEM_BYTES = 60 * 1024 * 1024
@@ -472,7 +728,7 @@
 
 
 def turn(value, tables, sign):
-    cos, low, high = (table[...] for table in tables)
+    cos, low, high = tables
     part = value[:, :128]
     turned = part * cos + sign * (
         pltpu.roll(part, 128 - ROT // 2, 1) * low + pltpu.roll(part, ROT // 2, 1) * high
@@ -490,93 +746,8 @@
     return cos, jnp.where(column < half, -sin, 0.0), jnp.where((column >= half) & (column < ROT), sin, 0.0)
 
 
-def attn_kernel(x, g, w_qk, w_vo, par, bias, cos, low, high, across, down, one_out, att_out, d_out, sums):
-    tables = (cos, low, high)
-    n = HEAD_DIM
-    scale = HEAD_DIM ** (-0.5)
-    one = (x[...].astype(f32) * par[0:1, :] + par[1:2, :]).astype(bf16)
-    one_out[...] = one
-    qk = dot(one, w_qk[...])
-    q = turn(qk[:, :n] + bias[0:1, :], tables, 1.0).astype(bf16)
-    k = turn(qk[:, n:], tables, 1.0).astype(bf16)
-    v = (dot(one, w_vo[:, :n]) + bias[1:2, :]).astype(bf16)
-    d_att = dot(g[...], w_vo[:, n:]).astype(bf16)
-    scores = jnp.where(across[0] <= down[0], dot(q, k, 1, 1) * scale, -jnp.inf)
-    top = jnp.max(scores, axis=-1, keepdims=True)
-    log_total = top + jnp.log(jnp.sum(jnp.exp(scores - top), axis=-1, keepdims=True))
-    probs = jnp.exp(scores - log_total)
-    low_probs = probs.astype(bf16)
-    att_out[...] = dot(low_probs, v).astype(bf16)
-    d_probs = dot(d_att, v, 1, 1)
-    d_scores = (probs * (d_probs - jnp.sum(probs * d_probs, axis=-1, keepdims=True)) * scale).astype(bf16)
-    d_q = turn(dot(d_scores, k), tables, -1.0)
-    d_k = turn(dot(d_scores, q, 0, 0), tables, -1.0)
-    d_v = dot(low_probs, d_att, 0, 0)
-    d_out[:, :n] = d_q.astype(bf16)
-    d_out[:, n : 2 * n] = d_k.astype(bf16)
-    d_out[:, 2 * n :] = d_v.astype(bf16)
-
-    @pl.when(pl.program_id(0) == 0)
-    def _():
-        sums[...] = jnp.zeros_like(sums)
-
-    sums[0:1, :] += jnp.sum(d_q, axis=0, keepdims=True)
-    sums[1:2, :] += jnp.sum(d_v, axis=0, keepdims=True)
-
-
 def fixed(*shape):
     return pl.BlockSpec(shape, lambda i: (0,) * len(shape))
-
-
-def run_attention(acts, w_qk, w_vo, par, bias, places):
-    _, rows, width = acts.shape
-    seq, n = rows // Z, HEAD_DIM
-    by_rows = lambda cols: pl.BlockSpec((seq, cols), lambda i: (i, 0))
-    act = lambda which: pl.BlockSpec((None, seq, width), lambda i: (which, i, 0))
-    return pl.pallas_call(
-        attn_kernel,
-        grid=(Z,),
-        in_specs=[act(0), act(1), fixed(width, 2 * n), fixed(width, 2 * n), fixed(*par.shape), fixed(2, n)]
-        + [by_rows(128)] * 3
-        + [pl.BlockSpec((1, 1, seq), lambda i: (i, 0, 0)), pl.BlockSpec((1, seq, 1), lambda i: (i, 0, 0))],
-        out_specs=[by_rows(width), by_rows(n), by_rows(3 * n), fixed(2, n)],
-        out_shape=[jax.ShapeDtypeStruct((rows, cols), bf16) for cols in (width, n, 3 * n)]
-        + [jax.ShapeDtypeStruct((2, n), f32)],
-        compiler_params=pltpu.CompilerParams(vmem_limit_bytes=VMEM_BYTES),
-        name="attention",
-    )(acts, acts, w_qk, w_vo, par, bias, *turn_tables(places), places[:, None, :], places[:, :, None])
-
-
-def hidden_kernel(x, g, up, down, par, bias, two_out, act_out, d_out, sums):
-    @pl.when(pl.program_id(0) == 0)
-    def _():
-        two_out[...] = (x[...].astype(f32) * par[2:3, :] + par[3:4, :]).astype(bf16)
-
-    pre = dot(two_out[...], up[...]) + bias[...]
-    erf = 1.0 + lax.erf(pre * 0.7071067811865476)
-    act_out[...] = (0.5 * pre * erf).astype(bf16)
-    slope = 0.5 * erf + pre * jnp.exp(-0.5 * pre * pre) * 0.3989422804014327
-    d_pre = dot(g[...], down[...]) * slope
-    d_out[...] = d_pre.astype(bf16)
-    sums[...] = jnp.sum(d_pre, axis=0, keepdims=True)
-
-
-def run_hidden(acts, w_up, w_dn, par, bias):
-    _, rows, width = acts.shape
-    hidden = w_up.shape[1]
-    step = 256
-    act = lambda which: pl.BlockSpec((None, rows, width), lambda i: (which, 0, 0), pipeline_mode=pl.Buffered(1))
-    tile = lambda height: pl.BlockSpec((height, step), lambda i: (0, i))
-    return pl.pallas_call(
-        hidden_kernel,
-        grid=(hidden // step,),
-        in_specs=[act(0), act(1), tile(width), tile(width), fixed(*par.shape), tile(1)],
-        out_specs=[fixed(rows, width), tile(rows), tile(rows), tile(1)],
-        out_shape=[jax.ShapeDtypeStruct((rows, n), bf16) for n in (width, hidden, hidden)]
-        + [jax.ShapeDtypeStruct((1, hidden), f32)],
-        compiler_params=pltpu.CompilerParams(vmem_limit_bytes=VMEM_BYTES),
-        name="hidden_units",
-    )(acts, acts, w_up, w_dn, par, bias)
 
 
 def outs_kernel(flag, att, d_attn, act, d_pre, x, w_qk, w_vo, w_up, w_dn, par, keep, give, sums):
@@ -1097,29 +1268,52 @@
     scatter_kernel(m_size, fused, *refs)
 
 
-def adam_kernel(per, *refs):
-    count = len(refs) - 7
-    grads, (weight, one, two), outs = refs[:count], refs[count : count + 3], refs[count + 3 :]
-    cols = weight.shape[2]
-    for j in range(weight.shape[1]):
-        g = grads[j // per][0, :, (j % per) * cols : (j % per + 1) * cols].astype(f32)
-        w_new, one_new, two_new = adam_step(weight[:, j, :], g, one[:, j, :], two[:, j, :])
-        for ref, value in zip(outs, (g, w_new, one_new, two_new)):
-            ref[:, j, :] = value
-
-
-def adam_update(grads, per, weight, one, two):
-    rows, kinds, width = weight.shape
-    cols = width // Z
-    spec = pl.BlockSpec((rows, kinds, cols), lambda q: (0, 0, q))
+def update_kernel(*refs):
+    rows, cotangent, back, bias, qk, vo, up, dn = refs[:8]
+    block_out, input_grad = refs[14:16]
+    normed, inverse = layer_stats(rows[...])
+    block_out[...] = rows[...] + back[0].astype(f32) + bias[...]
+    u = back[1].astype(f32)
+    input_grad[...] = cotangent[...] + inverse * (
+        u
+        - jnp.mean(u, axis=-1, keepdims=True)
+        - normed * jnp.mean(u * normed, axis=-1, keepdims=True)
+    )
+    for sources, (weight, one, two), outs in (
+        ((qk, qk, vo, vo), refs[8:11], refs[16:20]),
+        ((up, dn), refs[11:14], refs[20:24]),
+    ):
+        kinds, wide = weight.shape[1], weight.shape[2] // Z
+        for j in range(kinds):
+            at = j % (kinds // 2) * wide
+            for q in range(Z):
+                cols = slice(q * wide, (q + 1) * wide)
+                g = sources[j][q, :, at : at + wide].astype(f32)
+                updated = adam_step(weight[:, j, cols], g, one[:, j, cols], two[:, j, cols])
+                for ref, value in zip(outs, (g, *updated)):
+                    ref[:, j, cols] = value
+
+
+def update(block_in, out_grad, own_rows, bias, own, attn, mlp):
+    rows, width = block_in.shape
+    shard = attn[0].shape[0]
+    step = min(shard, 16)
+    steps = shard // step
+    by_rows = pl.BlockSpec((rows // steps, width), lambda i: (i, 0))
+    block = lambda v: pl.BlockSpec((step,) + v.shape[1:], lambda i: (i, 0, 0))
     return pl.pallas_call(
-        functools.partial(adam_kernel, per),
-        grid=(Z,),
-        in_specs=[pl.BlockSpec((1, rows, per * cols), lambda q: (q, 0, 0))] * len(grads) + [spec] * 3,
-        out_specs=[spec] * 4,
-        out_shape=[jax.ShapeDtypeStruct(weight.shape, f32)] * 4,
-        name="adam_update",
-    )(*grads, weight, one, two)
+        update_kernel,
+        grid=(steps,),
+        in_specs=[by_rows, by_rows, pl.BlockSpec((2, rows // steps, width), lambda i: (0, i, 0)), fixed(1, width)]
+        + [pl.BlockSpec((Z, step, g.shape[2]), lambda i: (0, i, 0)) for g in own]
+        + [block(v) for v in (*attn, *mlp)],
+        out_specs=[by_rows, by_rows] + [block(attn[0])] * 4 + [block(mlp[0])] * 4,
+        out_shape=[jax.ShapeDtypeStruct((rows, width), f32)] * 2
+        + [jax.ShapeDtypeStruct(attn[0].shape, f32)] * 4
+        + [jax.ShapeDtypeStruct(mlp[0].shape, f32)] * 4,
+        compiler_params=pltpu.CompilerParams(vmem_limit_bytes=VMEM_BYTES),
+        name="update",
+    )(block_in, out_grad, own_rows, bias, *own, *attn, *mlp)
 
 
 def body(
@@ -1143,32 +1337,20 @@
     seq = 2 * rows
     part = small_params.shape[1]
 
-    normed, inverse = layer_stats(block_in)
-    x_low, g_low = normed.astype(bf16), out_grad.astype(bf16)
-
-    pieces = split_weights(attn_weight, mlp_weight)
-    tile = -(-12 * part // 1024) * 1024
+    pieces, low = prepare(block_in, out_grad, attn_weight, mlp_weight)
     small_tile = jnp.concatenate(
-        [small_params.reshape(-1), jnp.zeros((tile - 12 * part,), f32), positions[0].astype(f32)]
-        + [jnp.zeros((1024 - seq,), f32)]
-    ).reshape(-1, 128)
-    weights, acts, table = gather(pieces, jnp.stack([x_low, g_low]), small_tile, grid.m)
-    w_qk, w_vo, w_up, w_dn = weights
-    everyone = jnp.take(table.reshape(devices, -1), jnp.array(table_order(grid.m)), axis=0)
-    small_all = jnp.transpose(everyone[:, : 12 * part].reshape(devices, 12, part), (1, 0, 2)).reshape(12, width)
-    group = (jnp.arange(Z) * grid.m + m) * 4 + t * 2
-    places = jnp.take(everyone[:, tile : tile + seq], group, axis=0)
+        [jnp.pad(small_params, ((0, 0), (0, 128 - part))), positions.astype(f32).reshape(-1, 128)]
+    )
+    small_tile = jnp.pad(small_tile, ((0, 16 - small_tile.shape[0]), (0, 0)))
+    weights, acts, norms, (attended, d_attn, activation, d_pre), (head_sums, up_sums), table = gather(
+        pieces, low, small_tile, grid.m
+    )
+    everyone = jnp.take(table[:, :12, :part], jnp.array(table_order(grid.m)), axis=0)
+    small_all = jnp.transpose(everyone, (1, 0, 2)).reshape(12, width)
     par = small_all[:4]
     head = c * Z + z
-    hidden = w_up.shape[1]
-    head_bias = lax.dynamic_slice_in_dim(small_all[4:6], head * HEAD_DIM, HEAD_DIM, axis=1)
-    up_bias = lax.dynamic_slice_in_dim(small_all[8:12].reshape(1, -1), head * hidden, hidden, axis=1)
-
-    one_low, attended, d_attn, head_sums = run_attention(acts, w_qk, w_vo, par, head_bias, places)
-    two_low, activation, d_pre, up_sums = run_hidden(acts, w_up, w_dn, par, up_bias)
     keep, give, norm_sums = run_outs(diag, attended, d_attn, activation, d_pre, acts, weights, par)
-    factors = (one_low, two_low, acts, attended, d_attn, activation, d_pre)
-
+    factors = (*norms, acts, attended, d_attn, activation, d_pre)
     spread_cols = lambda v, n: lax.dynamic_update_slice_in_dim(
         jnp.zeros((n,), f32), v, head * v.shape[0], 0
     )
@@ -1187,17 +1369,13 @@
     terms = jnp.transpose(small_terms.reshape(12, devices, part), (1, 0, 2)).reshape(devices, 12 * part)
     places_of = table_order(grid.m)
     terms = jnp.take(terms, jnp.array([places_of.index(i) for i in range(devices)]), axis=0)
-    terms = jnp.pad(terms, ((0, 0), (0, tile - 12 * part))).reshape(devices, -1, 128)
+    terms = jnp.pad(terms, ((0, 0), (0, 1024 - 12 * part))).reshape(devices, -1, 128)
     own, own_rows, own_small = scatter(factors, keep, give, terms, grid.m, rows)
-    y_rows, u_rows = own_rows[0].astype(f32), own_rows[1].astype(f32)
-    block_out = block_in + y_rows + small_all[6] + small_all[7]
-    input_grad = out_grad + inverse * (
-        u_rows
-        - jnp.mean(u_rows, axis=-1, keepdims=True)
-        - normed * jnp.mean(u_rows * normed, axis=-1, keepdims=True)
-    )
-    attn_out = adam_update(own[:2], 2, attn_weight, attn_first, attn_second)
-    mlp_out = adam_update(own[2:], 1, mlp_weight, mlp_first, mlp_second)
+    row_bias = (small_all[6] + small_all[7])[None]
+    attn = (attn_weight, attn_first, attn_second)
+    mlp = (mlp_weight, mlp_first, mlp_second)
+    block_out, input_grad, *updated = update(block_in, out_grad, own_rows, row_bias, own, attn, mlp)
+    attn_out, mlp_out = updated[:4], updated[4:]
     small_grad = own_small.reshape(-1)[: 12 * part].reshape(12, part)
     small_new, small_first_new, small_second_new = adam_step(small_params, small_grad, small_first, small_second)
 

time: 419 us -> 387 us (0.924); the launches traced: 412 us -> 386 us
  Pallas kernels: 376 us -> 364 us
  other arithmetic: 22.2 us -> 14.2 us
  local copies, waits for them, and re-layouts: 12.6 us -> 7.21 us
    pallas_call x5 -> x2, Pallas kernels: 62.6 us -> 37.1 us  [the longest x1 25 us: update(): pl.pallas_call(update_kernel, grid=(steps,), in_specs=[by_rows, by_rows,...]
    pallas_call x1, Pallas kernels: 142 us -> 156 us  [gather(): pl.pallas_call(functools.partial(gather_kernel, m_size), out_shape=[shape...]
    unnamed x1 -> x8, other arithmetic: 0.07 us -> 9.22 us
    reduce_sum x4 -> x0, other arithmetic: 5.79 us -> none  [the longest x1 1.68 us: body(): jnp.mean(u_rows * normed, axis=-1, keepdims=True)]
    select_n x4 -> x0, other arithmetic: 4.75 us -> none  [the longest x1 3.16 us: turn_tables(): jnp.where((column >= half) & (column < ROT), sin, 0.0)]
where the time goes in v4:
time: 387 us; the launch traced here: 386 us
  Pallas kernels  364 us (94%)
  other arithmetic  14.2 us (4%)
  local copies, waits for them, and re-layouts  7.21 us (2%)
    pallas_call x1, Pallas kernels, gather(): pl.pallas_call(functools.partial(gather_kernel, m_size), out_shape=[shape...  156 us
    pallas_call x1, Pallas kernels, scatter(): pl.pallas_call(functools.partial(scatter_entry, m_size, fused), out_shape...  150 us
    pallas_call x1, Pallas kernels, update(): pl.pallas_call(update_kernel, grid=(steps,), in_specs=[by_rows, by_rows,...  25 us
    pallas_call x1, Pallas kernels, run_outs(): pl.pallas_call(outs_kernel, grid_spec=pltpu.PrefetchScalarGridSpec(num_sc...  21.7 us
    pallas_call x1, Pallas kernels, prepare(): pl.pallas_call(prepare_kernel, grid=(steps,), in_specs=[by_rows, by_rows,...  12 us
    unnamed x8, other arithmetic  9.22 us

profile of v4, /device:TPU:0, one launch (start us, length us, event | category | flops | bytes accessed | tf_op | source)
XLA Modules:
  0.0 386.4 jit_solution(8407205555244641098)
XLA Ops:
  0.7 1.1 fusion.17
  1.8 1.1 fusion.14
  3.0 1.2 fusion.12
  4.1 1.1 fusion.16
  5.3 1.2 fusion.13
  6.4 1.2 fusion.10
  7.6 1.1 fusion.18
  8.8 1.2 fusion.15
  9.9 1.2 fusion.11.refs_6_
  11.1 12.0 %prepare.1 = (bf16[4,128,512]{2,1,0:T(8,128)(2,1)}, bf16[4,128,512]{2,1,0:T(8,128)(2,1)}, bf16[4,128,1024]{2,1,0:T(8,128)(2,1)}, bf16[4,128,1024]{2,1,0:T(8,128)(2,1)}, bf16[2,128,2048]{2,1,0:T(8,128)(2,1)}) custom-call(f32[128,2048]{1,0:T(8,128)} %refs_0_.1, f32[128,2048]{1,0:T(8,128)} %refs_1_.1, f32[128,4,1024]{2,1,0:T(4,128)} %refs_8_.1, ...), custom_call_target="tpu_custom_call" | custom-call | tf_op jit(solution)/shard_map/prepare/pallas_call | solution.py:78
  23.7 155.5 %gather_all.1 = (bf16[2048,512]{1,0:T(8,128)(2,1)}, bf16[2048,512]{1,0:T(8,128)(2,1)}, bf16[2048,1024]{1,0:T(8,128)(2,1)}, bf16[2048,1024]{1,0:T(8,128)(2,1)}, b...) custom-call(bf16[4,128,512]{2,1,0:T(8,128)(2,1)} %get-tuple-element., ...), custom_call_target="tpu_custom_call" | custom-call | tf_op jit(solution)/shard_map/gather_all/pallas_call | solution.py:679
  179.3 0.7 pad_clamp_fusion
  180.0 1.5 gather_fusion
  181.5 0.7 slice.29.par
  182.3 21.7 %outputs.1 = (bf16[1024,2048]{1,0:T(8,128)(2,1)}, bf16[1024,2048]{1,0:T(8,128)(2,1)}, f32[4,2048]{1,0:T(4,128)}) custom-call(s32[1]{0:T(128)} %bitcast.1.flag, bf16[1024,256]{1,0:T(8,128)(2,1)} %get-tuple-element.60.att.refs_3_, bf16[1024,768]{1,0:T(8,128)(2,1)} %get-tuple-element.61.d_attn.refs_4_, bf16[1024,1024]{1,0:T(8,128)(2,1)} %get-tuple-element.62.act.refs_5_, ...), custom_call_target="tpu_custom_call" | custom-call | tf_op jit(solution)/shard_map/outputs/pallas_call | solution.py:772
  203.9 0.9 concatenate.22
  205.4 0.7 reduce.10
  206.1 0.7 reduce.11
  208.3 0.7 copy.34
  209.0 149.9 %scatter_all.1 = (bf16[4,2,2,128,512]{4,3,2,1,0:T(8,128)(2,1)}, bf16[4,2,2,128,512]{4,3,2,1,0:T(8,128)(2,1)}, bf16[4,2,2,128,1024]{4,3,2,1,0:T(8,128)(2,1)}, bf1...) custom-call(bf16[1024,2048]{1,0:T(8,128)(2,1)} %get-tuple-element.57, ...), custom_call_target="tpu_custom_call" | custom-call | tf_op jit(solution)/shard_map/scatter_all/pallas_call | solution.py:1252
  358.9 1.0 fusion.19
  360.0 0.7 add.98.refs_3_
  360.7 25.0 %update.1 = (f32[128,2048]{1,0:T(8,128)}, f32[128,2048]{1,0:T(8,128)}, f32[128,4,1024]{2,1,0:T(4,128)}, f32[128,4,1024]{2,1,0:T(4,128)}, f32[128,4,1024]{2,1,0:T...) custom-call(f32[128,2048]{1,0:T(8,128)} %refs_0_.1, ...), custom_call_target="tpu_custom_call" | custom-call | tf_op jit(solution)/shard_map/update/pallas_call | solution.py:1304
  385.8 0.6 multiply_subtract_fusion
  (55 shorter events, 2.9 us)
Async XLA Ops:
  11.1 12.0 %copy-start.10 = (s32[1,256]{1,0:T(1,128)S(1)}, s32[1,256]{1,0:T(1,128)}, u32[]{:S(2)}) copy-start(s32[1,256]{1,0:T(1,128)} %param.15) | copy-start | bytes 3076
  11.1 12.0 %copy-start.2 = (f32[12,64]{1,0:T(8,128)S(1)}, f32[12,64]{1,0:T(8,128)}, u32[]{:S(2)}) copy-start(f32[12,64]{1,0:T(8,128)} %param.19) | copy-start | bytes 9220
  181.5 0.8 copy-start.1
  182.3 22.6 %copy-start.9 = (f32[2,256]{1,0:T(2,128)S(1)}, f32[2,256]{1,0:T(2,128)}, u32[]{:S(2)}) copy-start(f32[2,256]{1,0:T(2,128)} %get-tuple-element.72) | copy-start | bytes 6148
  182.3 24.6 %copy-start = (f32[128,2048]{1,0:T(8,128)S(1)}, f32[128,2048]{1,0:T(8,128)}, u32[]{:S(2)}) copy-start(f32[128,2048]{1,0:T(8,128)} %refs_1_.1) | copy-start | bytes 3145732
  182.3 24.8 %copy-start.8 = (f32[1,1024]{1,0:T(1,128)S(1)}, f32[1,1024]{1,0:T(1,128)}, u32[]{:S(2)}) copy-start(f32[1,1024]{1,0:T(1,128)} %get-tuple-element.73) | copy-start | bytes 12292
  360.7 25.1 %copy-start.7 = (f32[8,128]{1,0:T(8,128)S(1)}, f32[8,128]{1,0:T(8,128)}, u32[]{:S(2)}) copy-start(f32[8,128]{1,0:T(8,128)} %get-tuple-element.83) | copy-start | bytes 12292
  360.7 25.1 %copy-start.3 = (f32[12,64]{1,0:T(8,128)S(1)}, f32[12,64]{1,0:T(8,128)}, u32[]{:S(2)}) copy-start(f32[12,64]{1,0:T(8,128)} %param.19) | copy-start | bytes 9220
  360.7 25.1 %copy-start.5 = (f32[12,64]{1,0:T(8,128)S(1)}, f32[12,64]{1,0:T(8,128)}, u32[]{:S(2)}) copy-start(f32[12,64]{1,0:T(8,128)} %param.24) | copy-start | bytes 9220
  360.7 25.1 %copy-start.6 = (f32[12,64]{1,0:T(8,128)S(1)}, f32[12,64]{1,0:T(8,128)}, u32[]{:S(2)}) copy-start(f32[12,64]{1,0:T(8,128)} %param.25) | copy-start | bytes 9220
  385.8 0.6 copy-start.4

commit v5 on v4

--- a/solution.py
+++ b/solution.py
@@ -1,4 +1,5 @@
 import functools
+import math
 
 import jax
 import jax.numpy as jnp
@@ -40,96 +41,43 @@
     return (weight - learn_rate * (corrected + weight_decay * weight), one_new, two_new)
 
 
-class Grid:
-    def __init__(self, dp, tensor):
-        assert tensor == 2 and dp % (2 * Z) == 0
-        self.dp, self.m = dp, dp // (2 * Z)
-        index = lax.axis_index("dp")
-        self.index = index * 2 + lax.axis_index("tensor")
-        self.z_now = index // (2 * self.m)
-        self.m_now = (index // 2) % self.m
-        self.c_now = index % 2
-        self.t_now = lax.axis_index("tensor")
-        self.diag = self.c_now == self.t_now
-
-
-def prepare_kernel(rows, cotangent, attn, mlp, qk, vo, up, dn, low):
-    normed, _ = layer_stats(rows[...])
-    low[0] = normed.astype(bf16)
-    low[1] = cotangent[...].astype(bf16)
-    quarter_a = attn.shape[2] // Z
-    quarter_m = mlp.shape[2] // Z
-    for q in range(Z):
-        for j in range(4):
-            block = attn[:, j, q * quarter_a : (q + 1) * quarter_a].astype(bf16)
-            (qk, qk, vo, vo)[j][q, :, (j % 2) * quarter_a : (j % 2 + 1) * quarter_a] = block
-        for j in range(2):
-            (up, dn)[j][q] = mlp[:, j, q * quarter_m : (q + 1) * quarter_m].astype(bf16)
-
-
-def prepare(block_in, out_grad, attn_weight, mlp_weight):
-    own, width = block_in.shape
-    rows, _, half = attn_weight.shape
-    hidden = mlp_weight.shape[2]
-    step = min(rows, 16)
-    steps = rows // step
-    shapes = [2 * half // Z] * 2 + [hidden // Z] * 2
-    by_rows = pl.BlockSpec((own // steps, width), lambda i: (i, 0))
-    outs = pl.pallas_call(
-        prepare_kernel,
-        grid=(steps,),
-        in_specs=[
-            by_rows,
-            by_rows,
-            pl.BlockSpec((step, 4, half), lambda i: (i, 0, 0)),
-            pl.BlockSpec((step, 2, hidden), lambda i: (i, 0, 0)),
-        ],
-        out_specs=[pl.BlockSpec((Z, step, n), lambda i: (0, i, 0)) for n in shapes]
-        + [pl.BlockSpec((2, own // steps, width), lambda i: (0, i, 0))],
-        out_shape=[jax.ShapeDtypeStruct((Z, rows, n), bf16) for n in shapes]
-        + [jax.ShapeDtypeStruct((2, own, width), bf16)],
-        name="prepare",
-    )(block_in, out_grad, attn_weight, mlp_weight)
-    return outs[:4], outs[4]
-
-
 MESH = pl.DeviceIdType.MESH
 PARTS = (1, 1, 2, 2)
 CHUNKS = ((0, 0, True), (1, 0, False), (2, 0, True), (2, 1, False), (3, 0, True), (3, 1, False))
 GATHER_ORDER = {
     (False, False): (
-        0, 10, 500, 510, 520, 530, 540, 550, 700, 20, 1100, 600, 501, 900, 620, 511, 910, 640, 601, 1101, 801, 1110,
-        521, 710, 30, 40, 50, 502, 621, 512, 602, 610, 1010, 630, 811, 1111, 920, 1030, 650, 531, 1000, 541, 551,
-        1050, 1020, 641, 611, 930, 1040, 1001, 802, 1011, 522, 1120, 940, 503, 1021, 622, 513, 612, 603, 1002, 1012,
-        631, 651, 812, 1121, 1041, 1031, 532, 1051, 542, 1022, 552, 642, 1003, 632, 613, 652, 803, 1042, 1032, 523,
-        1013, 1200, 1052, 1130, 1201, 623, 1202, 1023, 813, 1131, 1203, 533, 1204, 543, 1205, 553, 633, 643, 653,
-        1043, 1033, 1206, 1207, 1053, 1208, 1209, 1210, 1211,
+        1201, 0, 10, 1200, 1202, 20, 700, 500, 501, 510, 520, 530, 540, 550, 900, 511, 1100, 521, 600, 1101, 601,
+        620, 640, 710, 30, 40, 50, 801, 621, 910, 1110, 502, 512, 610, 602, 522, 630, 1010, 1111, 622, 650, 811,
+        1030, 611, 531, 920, 1050, 541, 1000, 551, 1011, 1001, 641, 1020, 1040, 1021, 802, 930, 503, 1120, 513, 940,
+        612, 603, 1002, 523, 1012, 623, 1022, 631, 1121, 812, 651, 1031, 532, 1041, 542, 1051, 552, 642, 1003, 613,
+        632, 803, 1013, 1203, 652, 1023, 1032, 1042, 1130, 1204, 1205, 1052, 813, 533, 1131, 1206, 543, 1207, 553,
+        633, 1208, 643, 653, 1033, 1043, 1209, 1210, 1053, 1211, 1212, 1213, 1214,
     ),
     (False, True): (
-        0, 10, 700, 20, 500, 510, 520, 530, 540, 550, 610, 630, 650, 501, 600, 1100, 900, 1000, 511, 620, 1020, 611,
-        640, 1040, 710, 30, 40, 50, 1010, 1030, 801, 1050, 601, 1001, 521, 910, 1110, 1011, 502, 1101, 621, 1021,
-        602, 1002, 811, 531, 541, 1111, 930, 631, 551, 641, 512, 612, 940, 651, 1031, 1041, 920, 1012, 802, 522,
-        1120, 1051, 503, 622, 1022, 603, 1003, 812, 532, 542, 1121, 632, 552, 642, 513, 613, 652, 1032, 1042, 1013,
-        1200, 1052, 1201, 803, 1202, 523, 1130, 623, 1023, 813, 533, 1131, 1203, 543, 1204, 633, 553, 1205, 643, 653,
-        1043, 1033, 1206, 1207, 1208, 1053, 1209, 1210, 1211,
+        1201, 0, 10, 1200, 1202, 20, 700, 500, 501, 510, 520, 530, 540, 550, 900, 511, 1100, 610, 630, 710, 30, 40,
+        50, 650, 611, 521, 600, 1000, 601, 1001, 620, 1020, 640, 1040, 801, 910, 1010, 1101, 1110, 502, 1030, 1050,
+        1011, 811, 621, 1021, 531, 602, 1002, 541, 551, 1111, 641, 631, 930, 512, 612, 522, 651, 1031, 940, 1041,
+        1012, 622, 1022, 920, 802, 1051, 503, 1120, 603, 1003, 812, 532, 542, 552, 1121, 642, 632, 513, 613, 523,
+        652, 1032, 1042, 1013, 1203, 623, 1023, 1204, 803, 1205, 1052, 1130, 813, 533, 1131, 1206, 543, 633, 1207,
+        553, 1208, 643, 653, 1043, 1033, 1209, 1210, 1211, 1053, 1212, 1213, 1214,
     ),
     (True, False): (
-        0, 10, 500, 510, 520, 530, 540, 550, 900, 700, 20, 1100, 600, 200, 503, 620, 100, 300, 640, 501, 513, 603,
-        210, 310, 1101, 601, 110, 511, 710, 30, 40, 50, 803, 523, 1130, 610, 801, 320, 623, 220, 400, 1110, 630,
-        1010, 120, 502, 521, 410, 910, 650, 512, 1030, 1000, 602, 621, 1050, 1020, 1131, 811, 1040, 813, 230, 1111,
-        533, 130, 920, 613, 330, 531, 1003, 543, 240, 1001, 1013, 340, 140, 611, 553, 643, 541, 350, 250, 1023, 150,
-        1011, 551, 641, 930, 802, 612, 420, 1120, 1002, 940, 522, 1021, 1012, 1200, 633, 622, 631, 1201, 1202, 653,
-        1043, 1033, 1031, 812, 651, 430, 1121, 1203, 532, 1022, 1041, 1053, 1204, 1051, 440, 1205, 542, 632, 450,
-        552, 642, 1032, 1206, 652, 1207, 1042, 1208, 1052, 1209, 1210, 1211,
+        1201, 0, 10, 1200, 1202, 20, 700, 500, 503, 510, 520, 530, 540, 550, 200, 900, 100, 300, 1100, 501, 513, 600,
+        210, 310, 1101, 603, 110, 523, 620, 511, 320, 640, 220, 710, 30, 40, 50, 601, 120, 623, 521, 803, 610, 621,
+        400, 1130, 502, 630, 1010, 801, 410, 910, 602, 512, 1110, 650, 420, 613, 1030, 1131, 1000, 811, 1050, 1003,
+        230, 1111, 813, 130, 1013, 533, 1020, 531, 920, 330, 611, 240, 543, 1040, 140, 340, 1001, 541, 1011, 553,
+        1023, 250, 643, 350, 150, 641, 522, 1021, 551, 622, 930, 1002, 940, 802, 633, 612, 631, 1120, 1033, 1012,
+        1203, 1031, 812, 1204, 653, 1041, 1043, 430, 1121, 1205, 532, 651, 1206, 542, 1022, 1053, 440, 1207, 632,
+        1051, 450, 1208, 552, 642, 1032, 1209, 652, 1042, 1210, 1211, 1052, 1212, 1213, 1214,
     ),
     (True, True): (
-        0, 10, 700, 20, 500, 510, 520, 530, 540, 550, 900, 610, 630, 650, 600, 200, 503, 1100, 1000, 620, 100, 300,
-        1020, 640, 501, 513, 1040, 710, 30, 613, 40, 50, 210, 310, 1010, 110, 1030, 511, 611, 1050, 603, 1003, 601,
-        1001, 803, 1101, 1013, 523, 1130, 801, 320, 1011, 220, 400, 1110, 623, 1023, 120, 502, 521, 910, 602, 621,
-        1002, 813, 1021, 533, 811, 330, 230, 1111, 543, 1131, 130, 633, 930, 340, 531, 643, 631, 553, 240, 350, 140,
-        1033, 410, 541, 940, 653, 1043, 512, 612, 250, 1031, 150, 641, 551, 651, 920, 1053, 1041, 802, 1012, 1200,
-        420, 1120, 1201, 522, 1051, 1202, 622, 1022, 812, 430, 1121, 1203, 532, 1204, 632, 440, 1205, 542, 450, 1032,
-        1206, 552, 642, 1207, 652, 1042, 1208, 1209, 1052, 1210, 1211,
+        1201, 0, 10, 1200, 1202, 20, 700, 500, 503, 510, 520, 530, 540, 550, 200, 900, 100, 300, 1100, 610, 501, 513,
+        630, 710, 30, 40, 50, 650, 600, 613, 210, 310, 1000, 603, 110, 523, 1003, 620, 511, 320, 1020, 640, 611, 220,
+        1040, 120, 1101, 1010, 601, 1001, 521, 803, 1030, 400, 1130, 1050, 502, 801, 910, 1013, 1110, 623, 1023, 813,
+        1011, 533, 811, 621, 1021, 330, 230, 1111, 602, 1002, 543, 130, 340, 1131, 531, 643, 633, 631, 553, 240, 930,
+        350, 140, 410, 541, 1033, 512, 612, 250, 653, 420, 150, 1031, 1043, 940, 522, 551, 641, 1041, 651, 920, 1012,
+        1203, 1053, 1204, 622, 1022, 802, 1205, 1051, 1120, 812, 430, 1121, 1206, 532, 1207, 440, 1208, 542, 632,
+        450, 642, 552, 652, 1042, 1032, 1209, 1210, 1052, 1211, 1212, 1213, 1214,
     ),
 }
 SCATTER_ORDER = {
@@ -229,15 +177,15 @@
 
 
 def gather_kernel(m_size, *refs):
-    pieces, low, mine_small, base = refs[:4], refs[4], refs[5], refs[6]
-    full, act_out, one_out, two_out = refs[7:11], refs[11], refs[12], refs[13]
-    att, d_attn, hidden_out, d_pre, head_sums, up_sums, table = refs[14:21]
+    weights, rows_in, small, positions = refs[:2], refs[2:4], refs[4], refs[5]
+    full, act_out, one_out, two_out = refs[6:10], refs[10], refs[11], refs[12]
+    att, d_attn, hidden_out, d_pre, head_sums, up_sums, par, row_bias, out_sum = refs[13:22]
     count = len(CHUNKS)
-    stage, stage_m, relay = (refs[21 + i * count : 21 + (i + 1) * count] for i in range(3))
-    refs = refs[21 + 3 * count :]
+    stage, stage_m, relay = (refs[22 + i * count : 22 + (i + 1) * count] for i in range(3))
+    refs = refs[22 + 3 * count :]
     (zs, zr, gs, gr, ps, pr, ms, mr, near_s, far_s, xr, as_, ar, ws, wr, ss, sr, lin, lout, ls, os_) = refs[:21]
-    bounce, refs = refs[21 : 21 + count], refs[21 + count :]
-    act, w_qk, w_vo, one_v, two_v, tile_v, slope, par, bias, up_bias = refs
+    pieces, refs = refs[21 : 21 + count], refs[21 + count :]
+    act, w_qk, w_vo, one_v, two_v, tile_v, slope, bias, up_bias, table, base, attn_v, mlp_v, rows_v, low = refs
     net = Links(m_size)
     z, m, c, t = net.z, net.m, net.c, net.t
     rows = pieces[0].shape[1]
@@ -250,12 +198,11 @@
 
     def columns(ch):
         array, part, _ = CHUNKS[ch]
-        wide = pieces[array].shape[2] // PARTS[array]
+        wide = pieces[ch].shape[2]
         return array, slice(part * wide, (part + 1) * wide)
 
     def piece(ch, zz):
-        array, cols = columns(ch)
-        return pieces[array].at[zz, :, cols]
+        return pieces[ch].at[zz]
 
     def whole(ch, zz, mm, cc, size=1):
         array, cols = columns(ch)
@@ -265,25 +212,24 @@
     own_place = pl.ds(pl.multiple_of(z * seq + t * half, half), half)
     place = lambda zz, h: pl.ds(pl.multiple_of(zz * seq + (t ^ h) * half, half), half)
 
-    def load_own(ch):
-        return pltpu.make_async_copy(piece(ch, z), bounce[ch], lin.at[ch])
-
     def store_own(ch):
-        return pltpu.make_async_copy(bounce[ch], whole(ch, z, m, c), lout.at[ch])
-
-    def low_own():
-        return pltpu.make_async_copy(low.at[0], act.at[0, own_place], lin.at[count])
-
-    @pl.when(role == 0)
-    def _():
-        for ch in range(count):
-            load_own(ch).start()
-        low_own().start()
-
+        return pltpu.make_async_copy(pieces[ch].at[z], whole(ch, z, m, c), lout.at[ch])
+
+    def inputs():
+        sources = (*weights, *rows_in)
+        return [
+            pltpu.make_async_copy(src, dst, lin.at[i])
+            for i, (src, dst) in enumerate(zip(sources, (attn_v, mlp_v, rows_v.at[0], rows_v.at[1])))
+        ]
+
+    for one in inputs():
+        one.start()
     flat, steps = net.doubling()
-    pltpu.make_async_copy(mine_small, table.at[flat], ss.at[len(steps)]).start()
+    table[flat] = jnp.zeros(table.shape[1:], f32)
+    table[flat, 0:12, 0 : small.shape[1]] = small[...]
+    for e in range(seq // 128):
+        table[flat, 12 + e : 13 + e, :] = positions[:, e * 128 : (e + 1) * 128].astype(f32)
     net.meet()
-    pltpu.make_async_copy(mine_small, table.at[flat], ss.at[len(steps)]).wait()
 
     def program(inner, diag):
         state = {"small": 0}
@@ -392,6 +338,8 @@
         def first(ch, k):
             if k:
                 net.landed(spot(ch, z ^ k, 0), zr.at[ch, k])
+            elif diag:
+                store_own(ch).start()
             if CHUNKS[ch][2]:
                 for j in range(1, m_size):
 
@@ -432,9 +380,7 @@
         def rows_start(h, _):
             if h:
                 net.landed(act.at[0 if diag else 1, place(z, 1)], xr.at[1])
-            elif diag:
-                low_own().wait()
-            else:
+            elif not diag:
                 net.landed(act.at[1, place(z, 0)], xr.at[0])
             if inner:
                 rows_on(h, 0, 0, 3, 3)
@@ -451,13 +397,9 @@
         def swapped(k, h):
             net.landed(act.at[1 - role, place(z ^ k, h)], wr.at[k, h])
 
-        def begin():
-            small_send()
+        def rows_out():
             if diag:
                 send(lambda: (low.at[1], act.at[1, own_place], near_s, xr.at[0], net.to(c=1 - c)))
-                for ch in range(count):
-                    load_own(ch).wait()
-                    store_own(ch).start()
             else:
                 send(lambda: (low.at[0], act.at[0, own_place], near_s, xr.at[1], net.to(t=1 - t)))
                 send(lambda: (low.at[1], act.at[1, own_place], far_s, xr.at[1], net.to(c=1 - c, t=1 - t)))
@@ -473,14 +415,12 @@
             for parts in sent:
                 net.copy(*parts()).wait_send()
 
-        return begin, run, small_last, end
+        return small_send, run, rows_out, small_last, end
 
     programs = {key: program(*key) for key in GATHER_ORDER}
     work = len(runs_before(GATHER_ORDER[True, True]))
 
-    def device_rows(index):
-        zz, rest = index // (4 * m_size), lax.rem(index, 4 * m_size)
-        return rest * 4 + lax.rem(zz + zz // 2, 2) * 2 + zz // 2
+    device_rows = functools.partial(table_place, m_size)
 
     def parameters():
         part = width // (8 * m_size * 2)
@@ -495,11 +435,69 @@
             got = [table[device_rows(start + e), 4:6, 0:part] for e in range(per)]
             bias[:, b * 128 : (b + 1) * 128] = jnp.concatenate(got, axis=1)
         wide = up_bias.shape[1]
+        for b in range(width // 128):
+            got = [table[static[b * per + e], 6:8, 0:part] for e in range(per)]
+            both = jnp.concatenate(got, axis=1)
+            row_bias[:, b * 128 : (b + 1) * 128] = both[0:1] + both[1:2]
         row = 8 + head * wide // width
         for b in range(wide // 128):
             start = (lax.rem(head * wide, width) + b * 128) // part
             got = [table[device_rows(start + e), pl.ds(row, 1), 0:part] for e in range(per)]
             up_bias[:, b * 128 : (b + 1) * 128] = jnp.concatenate(got, axis=1)
+
+    step = 16
+
+    def attn_in():
+        inputs()[0].wait()
+        wide = attn_v.shape[2] // Z
+
+        @pl.loop(0, rows // step)
+        def _(i):
+            span = pl.ds(pl.multiple_of(i * step, step), step)
+            for j in range(4):
+                block = attn_v[span, j, :].astype(bf16)
+                for q in range(Z):
+                    at = j % 2 * wide
+                    pieces[j // 2][q, span, at : at + wide] = block[:, q * wide : (q + 1) * wide]
+
+    def mlp_in():
+        inputs()[1].wait()
+        wide = mlp_v.shape[2] // (2 * Z)
+
+        @pl.loop(0, rows // step)
+        def _(i):
+            span = pl.ds(pl.multiple_of(i * step, step), step)
+            for j in range(2):
+                block = mlp_v[span, j, :].astype(bf16)
+                for q in range(2 * Z):
+                    pieces[2 + 2 * j + q % 2][q // 2, span, :] = block[:, q * wide : (q + 1) * wide]
+
+    def rows_low():
+        for one in inputs()[2:]:
+            one.wait()
+        out_sum[...] = jnp.zeros_like(out_sum)
+
+        @pl.loop(0, half // step)
+        def _(i):
+            start = pl.multiple_of(i * step, step)
+            span = pl.ds(start, step)
+            normed, _ = layer_stats(rows_v[0, span, :])
+            normed = normed.astype(bf16)
+            low[0, span, :] = normed
+            given = rows_v[1, span, :]
+            low[1, span, :] = given.astype(bf16)
+            out_sum[...] += jnp.sum(given, axis=0, keepdims=True)
+
+            @pl.when(role == 0)
+            def _():
+                act[0, pl.ds(pl.multiple_of(z * seq + t * half + start, step), step), :] = normed
+
+    def turns_in():
+        for a, value in enumerate(turn_tables(lax.broadcasted_iota(jnp.int32, (seq, 128), 0).astype(f32))):
+            for e in range(3):
+                term = value.astype(bf16)
+                base[:, (3 * a + e) * 128 : (3 * a + e + 1) * 128] = term
+                value = value - term.astype(f32)
 
     def weights_in():
         return [
@@ -522,6 +520,7 @@
             for one in weights_in():
                 one.start()
             parameters()
+            turns_in()
             head_sums[...] = jnp.zeros_like(head_sums)
             for one in weights_in():
                 one.wait()
@@ -568,7 +567,7 @@
         head_sums[0:1, :] += jnp.sum(d_q, axis=0, keepdims=True)
         head_sums[1:2, :] += jnp.sum(d_v, axis=0, keepdims=True)
 
-    wide = pieces[2].shape[2] // Z
+    wide = full[2].shape[1] // Z
 
     def tile_in(array, j):
         cols = pl.ds(pl.multiple_of(j * wide, wide), wide)
@@ -599,29 +598,32 @@
         d_pre[:, cols] = value.astype(bf16)
         up_sums[:, cols] = jnp.sum(value, axis=0, keepdims=True)
 
-    def begin(inner, diag):
-        start, run, small_last, _ = programs[inner, diag]
-        start()
-        run(runs_before(GATHER_ORDER[inner, diag])[0])
-        small_last()
-
     def part(i, inner, diag):
-        programs[inner, diag][1](runs_before(GATHER_ORDER[inner, diag])[i + 1])
-
-    by_class(inner_z, role, begin)
+        _, run, rows_out, small_last, _ = programs[inner, diag]
+        if i == 1:
+            rows_out()
+        run(runs_before(GATHER_ORDER[inner, diag])[i + 1])
+        if i == 2:
+            small_last()
+
+    by_class(inner_z, role, lambda inner, diag: programs[inner, diag][0]())
+    ahead = 3
 
     @pl.loop(0, work - 1)
     def _(i):
-        pl.when(i < Z)(lambda: attention(i))
-        pl.when((i >= Z) & (i < 2 * Z))(lambda: hidden(i))
-        pl.when(i >= 2 * Z)(lambda: hidden_back(i))
+        pl.when(i == 0)(attn_in)
+        pl.when(i == 1)(rows_low)
+        pl.when(i == 2)(mlp_in)
+        pl.when((i >= ahead) & (i < ahead + Z))(lambda: attention(i - ahead))
+        pl.when((i >= ahead + Z) & (i < ahead + 2 * Z))(lambda: hidden(i - ahead))
+        pl.when(i >= ahead + 2 * Z)(lambda: hidden_back(i - ahead))
         for e in range(work - 1):
 
             @pl.when(i == e)
             def _(e=e):
                 by_class(inner_z, role, functools.partial(part, e))
 
-    by_class(inner_z, role, lambda inner, diag: programs[inner, diag][3]())
+    by_class(inner_z, role, lambda inner, diag: programs[inner, diag][4]())
     for i in range(Z):
         saved = rows_saved(i)
         for copy in saved[1:] if i < 2 else saved:
@@ -633,22 +635,13 @@
     return [order[lo:hi] for lo, hi in zip([0] + [i + 1 for i in cuts], cuts + [len(order)])]
 
 
-def turn_base(seq):
-    terms = []
-    for value in turn_tables(jnp.arange(seq).astype(f32)):
-        for _ in range(3):
-            low = lax.reduce_precision(value, 8, 7)
-            terms.append(low.astype(bf16))
-            value = value - low
-    return jnp.concatenate(terms, axis=1)
+def table_place(m_size, index):
+    z, rest = index // (4 * m_size), index % (4 * m_size)
+    return rest * 4 + (z + z // 2) % 2 * 2 + z // 2
 
 
 def table_order(m_size):
-    order = []
-    for z in range(Z):
-        for rest in range(4 * m_size):
-            order.append(rest * 4 + (z + z // 2) % 2 * 2 + z // 2)
-    return order
+    return [table_place(m_size, i) for i in range(4 * m_size * Z)]
 
 
 def by_class(inner_z, role, program):
@@ -660,12 +653,13 @@
                 program(inner, diag)
 
 
-def gather(pieces, low, small, m_size):
-    rows = pieces[0].shape[1]
-    own, width = low.shape[1:]
+def gather(attn_weight, mlp_weight, block_in, out_grad, small, positions, m_size):
+    rows = attn_weight.shape[0]
+    own, width = block_in.shape
     tokens = Z * 2 * own
     devices = m_size * 4 * Z
-    cols = [p.shape[2] for p in pieces]
+    hidden, n = mlp_weight.shape[2] // Z, HEAD_DIM
+    cols = [2 * n, 2 * n, hidden, hidden]
     count = len(CHUNKS)
     parts = [cols[array] // PARTS[array] for array, _, _ in CHUNKS]
     sem = pltpu.SemaphoreType.DMA
@@ -674,19 +668,19 @@
     in_vmem = pl.BlockSpec(memory_space=pltpu.VMEM)
     shape = lambda *dims: jax.ShapeDtypeStruct(dims, bf16)
     exact = lambda *dims: jax.ShapeDtypeStruct(dims, f32)
-    hidden, n = cols[2], HEAD_DIM
     vmem = lambda *dims: pltpu.VMEM(dims, bf16)
+    wide = lambda *dims: pltpu.VMEM(dims, f32)
     outs = pl.pallas_call(
         functools.partial(gather_kernel, m_size),
         out_shape=[shape(width, n) for n in cols]
         + [shape(2, tokens, width), shape(tokens, width), shape(tokens, width)]
         + [shape(tokens, n), shape(tokens, 3 * n), shape(tokens, hidden), shape(tokens, hidden)]
-        + [exact(2, n), exact(1, hidden), exact(devices, *small.shape)]
+        + [exact(2, n), exact(1, hidden), exact(4, width), exact(1, width), exact(1, width)]
         + [shape(Z, rows, n) for n in parts]
         + [shape(m_size, Z, rows, n) for n in parts]
         + [shape(4, rows, n) for n in parts],
-        in_specs=[in_place] * 6 + [in_vmem],
-        out_specs=[in_place] * 7 + [in_vmem] * 7 + [in_place] * (3 * count),
+        in_specs=[in_place] * 4 + [in_vmem] * 2,
+        out_specs=[in_place] * 7 + [in_vmem] * 9 + [in_place] * (3 * count),
         scratch_shapes=[
             sem((count, 3)),
             sem((count, Z)),
@@ -703,21 +697,22 @@
             sem((2, Z)),
             sem((Z, 2)),
             sem((Z, 2)),
-            sem((doubling + 1,)),
             sem((doubling,)),
-            sem((count + 1,)),
+            sem((doubling,)),
+            sem((4,)),
             sem((count,)),
             sem((2,)),
             sem((3, Z)),
         ]
-        + [vmem(rows, n) for n in parts]
+        + [vmem(Z, rows, n) for n in parts]
         + [vmem(2, tokens, width), vmem(width, 2 * n), vmem(width, 2 * n), vmem(2, 2 * own, width)]
-        + [vmem(tokens, width), vmem(2, width, hidden // Z), pltpu.VMEM((Z, tokens, hidden // Z), f32)]
-        + [pltpu.VMEM((4, width), f32), pltpu.VMEM((2, n), f32), pltpu.VMEM((1, hidden), f32)],
+        + [vmem(tokens, width), vmem(2, width, hidden // Z), wide(Z, tokens, hidden // Z)]
+        + [wide(2, n), wide(1, hidden), wide(devices, 16, 128), vmem(2 * own, 9 * 128)]
+        + [wide(*attn_weight.shape), wide(*mlp_weight.shape), wide(2, own, width), vmem(2, own, width)],
         compiler_params=pltpu.CompilerParams(collective_id=0, has_side_effects=True, vmem_limit_bytes=67043328),
         name="gather_all",
-    )(*pieces, low, small, turn_base(2 * own))
-    return outs[:4], outs[4], outs[5:7], outs[7:11], outs[11:13], outs[13]
+    )(attn_weight, mlp_weight, block_in, out_grad, small, positions)
+    return outs[:4], outs[4], outs[5:7], outs[7:11], outs[11:13], outs[13], outs[14], outs[15]
 
 
 VMEM_BYTES = 60 * 1024 * 1024
@@ -738,9 +733,9 @@
 
 def turn_tables(places):
     half = ROT // 2
-    column = jnp.arange(128)
-    frequency = 10000.0 ** (-((column % half).astype(f32) * (2.0 / ROT)))
-    angles = places.reshape(-1, 1) * frequency
+    column = lax.broadcasted_iota(jnp.int32, places.shape, 1)
+    frequency = jnp.exp(lax.rem(column, half).astype(f32) * (-2.0 / ROT * math.log(10000.0)))
+    angles = places * frequency
     cos = jnp.where(column < ROT, jnp.cos(angles), 1.0)
     sin = jnp.sin(angles)
     return cos, jnp.where(column < half, -sin, 0.0), jnp.where((column >= half) & (column < ROT), sin, 0.0)
@@ -829,10 +824,10 @@
 def scatter_kernel(m_size, fused, *refs):
     if fused:
         ones, twos, acts, att, d_attn, act, d_pre = refs[:7]
-        keep, give, terms = refs[7:10]
-        grads, refs = refs[10:14], refs[14:]
+        keep, give, *sums = refs[7:13]
+        grads, refs = refs[13:17], refs[17:]
     else:
-        grads, (keep, give, terms), refs = refs[:4], refs[4:7], refs[7:]
+        grads, (keep, give, *sums), refs = refs[:4], refs[4:10], refs[10:]
     own, rows_out, small_out, refs = refs[:4], refs[4], refs[5], refs[6:]
     count = len(CHUNKS)
     buffers = []
@@ -872,7 +867,25 @@
     loads_keep = [pltpu.make_async_copy(keep.at[z ^ k], kept.at[k], kl.at[k]) for k in range(Z)]
     for one in loads_keep:
         one.start()
-    current[...] = terms[...]
+    norm_sums, head_sums, up_sums, out_sum = sums
+
+    def small_terms():
+        current[...] = jnp.zeros_like(current)
+        width, hidden, n = out_sum.shape[1], up_sums.shape[1], HEAD_DIM
+        part = width // (4 * m_size * Z)
+        for i, at in enumerate(table_order(m_size)):
+            cols = slice(i * part, (i + 1) * part)
+            current[at, 0:4, 0:part] = norm_sums[:, cols]
+            current[at, 6:7, 0:part] = out_sum[:, cols]
+            current[at, 7:8, 0:part] = out_sum[:, cols]
+        head = c * Z + z
+        for e in range(n // part):
+            at = table_place(m_size, head * n // part + e)
+            current[at, 4:6, 0:part] = head_sums[:, e * part : (e + 1) * part]
+        row = 8 + head * hidden // width
+        for e in range(hidden // part):
+            at = table_place(m_size, head * hidden % width // part + e)
+            current[at, pl.ds(row, 1), 0:part] = up_sums[:, e * part : (e + 1) * part]
 
     def tile_loads(i, slot):
         block = (z ^ (Z - 1 - lax.rem(i, Z))) * m_size + (m ^ (1 - i // Z))
@@ -1159,8 +1172,7 @@
     }
 
     def begin(inner, diag):
-        small_send, run, _ = programs[inner, diag]
-        small_send()
+        _, run, _ = programs[inner, diag]
         run(SCATTER_ORDER[inner, diag][: cuts[inner, diag][0]])
 
     def part(i, inner, diag):
@@ -1168,6 +1180,8 @@
         programs[inner, diag][1](SCATTER_ORDER[inner, diag][lo:hi])
 
     by_class(inner_z, role, begin)
+    small_terms()
+    by_class(inner_z, role, lambda inner, diag: programs[inner, diag][0]())
     if fused:
 
         @pl.loop(0, 2 * Z)
@@ -1185,7 +1199,7 @@
     by_class(inner_z, role, lambda inner, diag: programs[inner, diag][2]())
 
 
-def scatter(factors, keep, give, terms, m_size, rows):
+def scatter(factors, keep, give, sums, m_size, rows):
     one, two, acts, att, d_attn, act, d_pre = factors
     width = keep.shape[1]
     block = width // (2 * Z * m_size)
@@ -1202,7 +1216,7 @@
     far = m_size - 1
     term_shapes = [jax.ShapeDtypeStruct((Z, m_size, 2, block, n), bf16) for n in cols]
     out_shape = [jax.ShapeDtypeStruct((Z, block, n), bf16) for n in cols]
-    out_shape += [jax.ShapeDtypeStruct((2, rows, width), bf16), jax.ShapeDtypeStruct(terms.shape[1:], f32)]
+    out_shape += [jax.ShapeDtypeStruct((2, rows, width), bf16), jax.ShapeDtypeStruct((16, 128), f32)]
     out_specs = [in_place] * 5 + [in_vmem]
     if fused:
         inputs = [one, two, acts, att, d_attn, act, d_pre]
@@ -1220,7 +1234,7 @@
             scratch += [vmem(Z, block, n)] * 3
     scratch += [vmem(4, block, n) for n in parts]
     scratch += [vmem(Z, seq, width)] * 2 + [vmem(5, seq, width), vmem(2, rows, width)]
-    scratch += [pltpu.VMEM(terms.shape, f32)] * 2
+    scratch += [pltpu.VMEM((4 * m_size * Z, 16, 128), f32)] * 2
     scratch += [
         sem((Z, 2)),
         sem((Z, 2)),
@@ -1252,12 +1266,12 @@
     outs = pl.pallas_call(
         functools.partial(scatter_entry, m_size, fused),
         out_shape=out_shape,
-        in_specs=in_specs + [in_place] * 2 + [in_vmem],
+        in_specs=in_specs + [in_place] * 2 + [in_vmem] * 4,
         out_specs=out_specs,
         scratch_shapes=scratch + (made + scratch_made if fused else []),
         compiler_params=pltpu.CompilerParams(collective_id=1, has_side_effects=True, vmem_limit_bytes=67043328),
         name="scatter_all",
-    )(*inputs, keep.reshape(Z, seq, width), give.reshape(Z, seq, width), terms)
+    )(*inputs, keep.reshape(Z, seq, width), give.reshape(Z, seq, width), *sums)
     outs = outs[4:] if fused else outs
     return outs[:4], outs[4], outs[5]
 
@@ -1330,53 +1344,22 @@
     small_first,
     small_second,
 ):
-    grid = Grid(lax.axis_size("dp"), lax.axis_size("tensor"))
-    z, m, c, t, diag = grid.z_now, grid.m_now, grid.c_now, grid.t_now, grid.diag
-    devices = grid.dp * 2
-    rows, width = block_in.shape
-    seq = 2 * rows
+    m_size = lax.axis_size("dp") // (2 * Z)
+    diag = lax.axis_index("dp") % 2 == lax.axis_index("tensor")
+    rows = block_in.shape[0]
     part = small_params.shape[1]
-
-    pieces, low = prepare(block_in, out_grad, attn_weight, mlp_weight)
-    small_tile = jnp.concatenate(
-        [jnp.pad(small_params, ((0, 0), (0, 128 - part))), positions.astype(f32).reshape(-1, 128)]
+    weights, acts, norms, (attended, d_attn, activation, d_pre), (head_sums, up_sums), par, row_bias, out_sum = gather(
+        attn_weight, mlp_weight, block_in, out_grad, small_params, positions, m_size
     )
-    small_tile = jnp.pad(small_tile, ((0, 16 - small_tile.shape[0]), (0, 0)))
-    weights, acts, norms, (attended, d_attn, activation, d_pre), (head_sums, up_sums), table = gather(
-        pieces, low, small_tile, grid.m
-    )
-    everyone = jnp.take(table[:, :12, :part], jnp.array(table_order(grid.m)), axis=0)
-    small_all = jnp.transpose(everyone, (1, 0, 2)).reshape(12, width)
-    par = small_all[:4]
-    head = c * Z + z
     keep, give, norm_sums = run_outs(diag, attended, d_attn, activation, d_pre, acts, weights, par)
     factors = (*norms, acts, attended, d_attn, activation, d_pre)
-    spread_cols = lambda v, n: lax.dynamic_update_slice_in_dim(
-        jnp.zeros((n,), f32), v, head * v.shape[0], 0
-    )
-    out_sum = jnp.sum(out_grad, axis=0)
-    small_terms = jnp.concatenate(
-        [
-            norm_sums,
-            spread_cols(head_sums[0], width)[None],
-            spread_cols(head_sums[1], width)[None],
-            out_sum[None],
-            out_sum[None],
-            spread_cols(up_sums[0], 4 * width).reshape(4, width),
-        ],
-        axis=0,
-    )
-    terms = jnp.transpose(small_terms.reshape(12, devices, part), (1, 0, 2)).reshape(devices, 12 * part)
-    places_of = table_order(grid.m)
-    terms = jnp.take(terms, jnp.array([places_of.index(i) for i in range(devices)]), axis=0)
-    terms = jnp.pad(terms, ((0, 0), (0, 1024 - 12 * part))).reshape(devices, -1, 128)
-    own, own_rows, own_small = scatter(factors, keep, give, terms, grid.m, rows)
-    row_bias = (small_all[6] + small_all[7])[None]
+    sums = (norm_sums, head_sums, up_sums, out_sum)
+    own, own_rows, own_small = scatter(factors, keep, give, sums, m_size, rows)
     attn = (attn_weight, attn_first, attn_second)
     mlp = (mlp_weight, mlp_first, mlp_second)
     block_out, input_grad, *updated = update(block_in, out_grad, own_rows, row_bias, own, attn, mlp)
     attn_out, mlp_out = updated[:4], updated[4:]
-    small_grad = own_small.reshape(-1)[: 12 * part].reshape(12, part)
+    small_grad = own_small[:12, :part]
     small_new, small_first_new, small_second_new = adam_step(small_params, small_grad, small_first, small_second)
 
     attn_grad, attn_new, attn_first_new, attn_second_new = attn_out

time: 387 us -> 364 us (0.941)
  other arithmetic: 14.2 us -> 1.38 us
  local copies, waits for them, and re-layouts: 7.21 us -> 0 us
    pallas_call x1 -> x0, Pallas kernels: 12 us -> none  [prepare(): pl.pallas_call(prepare_kernel, grid=(steps,), in_specs=[by_rows, by_rows,...]
    pallas_call x1, Pallas kernels: 156 us -> 166 us  [gather(): pl.pallas_call(functools.partial(gather_kernel, m_size), out_shape=[shape...]
    unnamed x8 -> x0, other arithmetic: 9.22 us -> none
where the time goes in v5:
time: 364 us; the launch traced here: 363 us
  Pallas kernels  361 us (99%)
    pallas_call x1, Pallas kernels, gather(): pl.pallas_call(functools.partial(gather_kernel, m_size), out_shape=[shape...  166 us
    pallas_call x1, Pallas kernels, scatter(): pl.pallas_call(functools.partial(scatter_entry, m_size, fused), out_shape...  149 us
    pallas_call x1, Pallas kernels, update(): pl.pallas_call(update_kernel, grid=(steps,), in_specs=[by_rows, by_rows,...  25 us
    pallas_call x1, Pallas kernels, run_outs(): pl.pallas_call(outs_kernel, grid_spec=pltpu.PrefetchScalarGridSpec(num_sc...  21.6 us

profile of v5, /device:TPU:0, one launch (start us, length us, event | category | flops | bytes accessed | tf_op | source)
XLA Modules:
  0.0 363.3 jit_solution(7468685096190633063)
XLA Ops:
  0.7 165.9 %gather_all.1 = (bf16[2048,512]{1,0:T(8,128)(2,1)}, bf16[2048,512]{1,0:T(8,128)(2,1)}, bf16[2048,1024]{1,0:T(8,128)(2,1)}, bf16[2048,1024]{1,0:T(8,128)(2,1)}, b...) custom-call(f32[128,4,1024]{2,1,0:T(4,128)} %refs_8_.1, ...), custom_call_target="tpu_custom_call" | custom-call | tf_op jit(solution)/shard_map/gather_all/pallas_call | solution.py:673
  166.6 21.6 %outputs.1 = (bf16[1024,2048]{1,0:T(8,128)(2,1)}, bf16[1024,2048]{1,0:T(8,128)(2,1)}, f32[4,2048]{1,0:T(4,128)}) custom-call(s32[1]{0:T(128)} %bitcast.flag, bf16[1024,256]{1,0:T(8,128)(2,1)} %get-tuple-element.52.att.refs_3_, bf16[1024,768]{1,0:T(8,128)(2,1)} %get-tuple-element.53.d_attn.refs_4_, bf16[1024,1024]{1,0:T(8,128)(2,1)} %get-tuple-element.54.act.refs_5_, ...), custom_call_target="tpu_custom_call" | custom-call | tf_op jit(solution)/shard_map/outputs/pallas_call | solution.py:767
  188.2 148.6 %scatter_all.1 = (bf16[4,2,2,128,512]{4,3,2,1,0:T(8,128)(2,1)}, bf16[4,2,2,128,512]{4,3,2,1,0:T(8,128)(2,1)}, bf16[4,2,2,128,1024]{4,3,2,1,0:T(8,128)(2,1)}, bf1...) custom-call(bf16[1024,2048]{1,0:T(8,128)(2,1)} %get-tuple-element.49, ...), custom_call_target="tpu_custom_call" | custom-call | tf_op jit(solution)/shard_map/scatter_all/pallas_call | solution.py:1266
  336.7 1.4 multiply_subtract_fusion
  338.1 25.0 %update.1 = (f32[128,2048]{1,0:T(8,128)}, f32[128,2048]{1,0:T(8,128)}, f32[128,4,1024]{2,1,0:T(4,128)}, f32[128,4,1024]{2,1,0:T(4,128)}, f32[128,4,1024]{2,1,0:T...) custom-call(f32[128,2048]{1,0:T(8,128)} %refs_0_.3, ...), custom_call_target="tpu_custom_call" | custom-call | tf_op jit(solution)/shard_map/update/pallas_call | solution.py:1318

commit v6 on v5

--- a/solution.py
+++ b/solution.py
@@ -33,10 +33,8 @@
 def adam_step(weight, gradient, moment_one, moment_two):
     one_new = beta_first * moment_one + (1.0 - beta_first) * gradient
     two_new = beta_second * moment_two + (1.0 - beta_second) * gradient * gradient
-    corrected = (
-        one_new
-        / (1.0 - beta_first**ADAM_STEP)
-        / (jnp.sqrt(two_new / (1.0 - beta_second**ADAM_STEP)) + adam_epsilon)
+    corrected = (one_new * (1.0 / (1.0 - beta_first**ADAM_STEP))) / (
+        jnp.sqrt(two_new * (1.0 / (1.0 - beta_second**ADAM_STEP))) + adam_epsilon
     )
     return (weight - learn_rate * (corrected + weight_decay * weight), one_new, two_new)
 
@@ -46,75 +44,75 @@
 CHUNKS = ((0, 0, True), (1, 0, False), (2, 0, True), (2, 1, False), (3, 0, True), (3, 1, False))
 GATHER_ORDER = {
     (False, False): (
-        1201, 0, 10, 1200, 1202, 20, 700, 500, 501, 510, 520, 530, 540, 550, 900, 511, 1100, 521, 600, 1101, 601,
-        620, 640, 710, 30, 40, 50, 801, 621, 910, 1110, 502, 512, 610, 602, 522, 630, 1010, 1111, 622, 650, 811,
-        1030, 611, 531, 920, 1050, 541, 1000, 551, 1011, 1001, 641, 1020, 1040, 1021, 802, 930, 503, 1120, 513, 940,
-        612, 603, 1002, 523, 1012, 623, 1022, 631, 1121, 812, 651, 1031, 532, 1041, 542, 1051, 552, 642, 1003, 613,
-        632, 803, 1013, 1203, 652, 1023, 1032, 1042, 1130, 1204, 1205, 1052, 813, 533, 1131, 1206, 543, 1207, 553,
-        633, 1208, 643, 653, 1033, 1043, 1209, 1210, 1053, 1211, 1212, 1213, 1214,
+        1201, 0, 10, 1200, 500, 510, 900, 501, 700, 1202, 20, 511, 520, 530, 540, 550, 600, 601, 1100, 910, 1101,
+        620, 640, 801, 1110, 710, 30, 40, 50, 521, 502, 621, 610, 512, 602, 503, 611, 1010, 603, 630, 1111, 1011,
+        811, 1030, 650, 531, 920, 1000, 541, 1050, 1001, 551, 641, 930, 1020, 1040, 940, 802, 1120, 522, 1021, 513,
+        612, 622, 1002, 1012, 812, 1121, 631, 1003, 532, 542, 651, 1031, 552, 1041, 642, 613, 1051, 1022, 632, 803,
+        652, 1042, 1013, 1203, 523, 1032, 1130, 1204, 533, 1052, 1205, 623, 1131, 1023, 813, 1206, 543, 553, 633,
+        1207, 1208, 643, 653, 1033, 1209, 1043, 1210, 1053, 1211, 1212, 1213, 1214,
     ),
     (False, True): (
-        1201, 0, 10, 1200, 1202, 20, 700, 500, 501, 510, 520, 530, 540, 550, 900, 511, 1100, 610, 630, 710, 30, 40,
-        50, 650, 611, 521, 600, 1000, 601, 1001, 620, 1020, 640, 1040, 801, 910, 1010, 1101, 1110, 502, 1030, 1050,
-        1011, 811, 621, 1021, 531, 602, 1002, 541, 551, 1111, 641, 631, 930, 512, 612, 522, 651, 1031, 940, 1041,
-        1012, 622, 1022, 920, 802, 1051, 503, 1120, 603, 1003, 812, 532, 542, 552, 1121, 642, 632, 513, 613, 523,
-        652, 1032, 1042, 1013, 1203, 623, 1023, 1204, 803, 1205, 1052, 1130, 813, 533, 1131, 1206, 543, 633, 1207,
-        553, 1208, 643, 653, 1043, 1033, 1209, 1210, 1211, 1053, 1212, 1213, 1214,
+        1201, 0, 10, 1200, 700, 1202, 20, 500, 501, 510, 520, 530, 540, 550, 610, 900, 511, 1100, 600, 710, 30, 40,
+        50, 601, 611, 630, 650, 1000, 1001, 620, 1020, 640, 801, 1040, 1010, 521, 910, 1110, 1011, 502, 1101, 1030,
+        1050, 621, 1021, 811, 602, 1002, 531, 541, 551, 1111, 641, 631, 512, 612, 930, 920, 651, 1031, 1041, 1012,
+        802, 940, 522, 1051, 503, 1120, 622, 603, 1003, 1022, 812, 532, 542, 1121, 632, 552, 642, 513, 613, 652,
+        1032, 1042, 1013, 1203, 803, 1204, 523, 1052, 1130, 1205, 623, 813, 533, 633, 1023, 543, 1033, 553, 643,
+        1131, 1206, 653, 1207, 1208, 1043, 1209, 1053, 1210, 1211, 1212, 1213, 1214,
     ),
     (True, False): (
-        1201, 0, 10, 1200, 1202, 20, 700, 500, 503, 510, 520, 530, 540, 550, 200, 900, 100, 300, 1100, 501, 513, 600,
-        210, 310, 1101, 603, 110, 523, 620, 511, 320, 640, 220, 710, 30, 40, 50, 601, 120, 623, 521, 803, 610, 621,
-        400, 1130, 502, 630, 1010, 801, 410, 910, 602, 512, 1110, 650, 420, 613, 1030, 1131, 1000, 811, 1050, 1003,
-        230, 1111, 813, 130, 1013, 533, 1020, 531, 920, 330, 611, 240, 543, 1040, 140, 340, 1001, 541, 1011, 553,
-        1023, 250, 643, 350, 150, 641, 522, 1021, 551, 622, 930, 1002, 940, 802, 633, 612, 631, 1120, 1033, 1012,
-        1203, 1031, 812, 1204, 653, 1041, 1043, 430, 1121, 1205, 532, 651, 1206, 542, 1022, 1053, 440, 1207, 632,
-        1051, 450, 1208, 552, 642, 1032, 1209, 652, 1042, 1210, 1211, 1052, 1212, 1213, 1214,
+        1201, 0, 10, 1200, 500, 510, 900, 200, 503, 700, 1202, 20, 520, 530, 540, 550, 600, 603, 100, 300, 1100, 501,
+        513, 210, 310, 1101, 620, 110, 400, 640, 511, 910, 601, 710, 30, 40, 50, 803, 1130, 610, 523, 801, 320, 1110,
+        220, 1010, 502, 630, 120, 623, 410, 521, 602, 512, 650, 1000, 1030, 1003, 621, 1131, 811, 1050, 613, 813,
+        230, 1111, 533, 1020, 130, 1013, 330, 1040, 531, 920, 543, 611, 240, 340, 930, 140, 1001, 643, 553, 541, 350,
+        250, 1011, 150, 1023, 940, 551, 641, 1002, 802, 420, 1120, 1021, 522, 633, 612, 622, 631, 1033, 1043, 1012,
+        1203, 653, 1031, 430, 812, 1121, 1204, 532, 651, 1041, 1205, 1022, 1053, 440, 1206, 542, 632, 1051, 450,
+        1207, 552, 1208, 642, 1032, 1209, 652, 1210, 1042, 1211, 1052, 1212, 1213, 1214,
     ),
     (True, True): (
-        1201, 0, 10, 1200, 1202, 20, 700, 500, 503, 510, 520, 530, 540, 550, 200, 900, 100, 300, 1100, 610, 501, 513,
-        630, 710, 30, 40, 50, 650, 600, 613, 210, 310, 1000, 603, 110, 523, 1003, 620, 511, 320, 1020, 640, 611, 220,
-        1040, 120, 1101, 1010, 601, 1001, 521, 803, 1030, 400, 1130, 1050, 502, 801, 910, 1013, 1110, 623, 1023, 813,
-        1011, 533, 811, 621, 1021, 330, 230, 1111, 602, 1002, 543, 130, 340, 1131, 531, 643, 633, 631, 553, 240, 930,
-        350, 140, 410, 541, 1033, 512, 612, 250, 653, 420, 150, 1031, 1043, 940, 522, 551, 641, 1041, 651, 920, 1012,
-        1203, 1053, 1204, 622, 1022, 802, 1205, 1051, 1120, 812, 430, 1121, 1206, 532, 1207, 440, 1208, 542, 632,
-        450, 642, 552, 652, 1042, 1032, 1209, 1210, 1052, 1211, 1212, 1213, 1214,
+        1201, 0, 10, 1200, 700, 1202, 20, 500, 503, 510, 520, 530, 540, 550, 610, 200, 900, 100, 300, 1100, 600, 501,
+        513, 710, 30, 40, 50, 603, 630, 650, 1000, 1003, 613, 210, 310, 620, 110, 1020, 640, 511, 1040, 611, 1010,
+        601, 1001, 803, 1101, 1030, 523, 1050, 801, 320, 1130, 1013, 220, 400, 1110, 120, 502, 1011, 521, 910, 623,
+        1023, 602, 1002, 621, 813, 533, 811, 1021, 330, 230, 1111, 543, 1131, 130, 633, 340, 531, 643, 631, 553, 240,
+        930, 920, 1033, 350, 140, 410, 541, 1043, 1031, 653, 512, 612, 250, 940, 150, 641, 551, 651, 1053, 1041, 802,
+        1012, 1203, 1051, 420, 1120, 1204, 522, 1205, 622, 1022, 812, 430, 532, 1121, 1206, 632, 440, 1207, 542,
+        1208, 1032, 450, 1209, 552, 642, 1210, 652, 1042, 1211, 1212, 1052, 1213, 1214,
     ),
 }
 SCATTER_ORDER = {
     (False, False): (
         30, 31, 20, 21, 10, 11, 0, 1, 131, 530, 531, 520, 521, 510, 511, 500, 501, 1600, 203, 413, 223, 433, 243,
-        453, 121, 1610, 202, 412, 222, 432, 242, 452, 111, 903, 1620, 201, 411, 221, 431, 241, 451, 101, 923, 943,
-        1630, 200, 410, 220, 430, 240, 450, 130, 902, 1013, 1033, 303, 323, 922, 343, 120, 942, 1053, 302, 322, 342,
-        110, 901, 1012, 921, 301, 321, 341, 100, 941, 300, 320, 340, 1032, 900, 920, 800, 1052, 940, 1113, 1133,
-        1011, 1103, 810, 1031, 1051, 1153, 1123, 1143, 1640, 1010, 1112, 1030, 1050, 1102, 1122, 1142, 1101, 1132,
-        1121, 1152, 1141, 1111, 1100, 1120, 1140, 1131, 1151, 1110, 1130, 1150,
+        453, 121, 1610, 202, 412, 222, 432, 242, 903, 452, 111, 923, 1620, 201, 411, 221, 431, 241, 451, 101, 943,
+        1630, 200, 410, 220, 430, 240, 450, 130, 902, 1013, 922, 1033, 303, 323, 343, 120, 942, 1053, 302, 322, 342,
+        110, 901, 1012, 921, 301, 321, 341, 100, 800, 1032, 900, 941, 300, 320, 340, 920, 940, 1052, 1113, 810, 1133,
+        1011, 1103, 1031, 1123, 1051, 1153, 1143, 1640, 1010, 1112, 1030, 1050, 1102, 1132, 1122, 1142, 1101, 1121,
+        1152, 1100, 1141, 1120, 1111, 1140, 1131, 1151, 1110, 1130, 1150,
     ),
     (False, True): (
         30, 31, 20, 21, 10, 11, 0, 1, 131, 530, 531, 520, 521, 510, 511, 500, 501, 1600, 203, 413, 223, 433, 243,
-        453, 121, 1610, 903, 202, 412, 222, 432, 242, 452, 111, 923, 201, 411, 221, 431, 241, 451, 101, 943, 1620,
-        200, 410, 220, 430, 240, 450, 130, 902, 1013, 922, 1033, 1630, 303, 323, 343, 120, 942, 1053, 901, 302, 322,
-        342, 110, 921, 301, 321, 341, 100, 1012, 941, 300, 320, 340, 900, 920, 1032, 940, 800, 1113, 1052, 1133,
-        1103, 1123, 810, 1011, 1031, 1153, 1051, 1143, 1640, 1010, 1112, 1030, 1050, 1102, 1122, 1142, 1132, 1101,
-        1152, 1121, 1111, 1141, 1100, 1120, 1131, 1140, 1151, 1110, 1130, 1150,
+        453, 121, 903, 1610, 202, 412, 222, 432, 242, 452, 111, 923, 201, 411, 221, 431, 241, 451, 101, 943, 1620,
+        902, 200, 410, 220, 430, 240, 450, 130, 1013, 922, 1033, 1630, 303, 323, 942, 343, 120, 901, 1053, 302, 322,
+        342, 110, 921, 301, 321, 341, 100, 1012, 900, 800, 941, 300, 320, 340, 920, 1032, 940, 1113, 1052, 1133, 810,
+        1103, 1011, 1123, 1031, 1153, 1051, 1143, 1102, 1640, 1112, 1010, 1030, 1132, 1050, 1122, 1142, 1101, 1152,
+        1121, 1100, 1141, 1111, 1120, 1131, 1140, 1151, 1110, 1130, 1150,
     ),
     (True, False): (
         30, 31, 20, 21, 10, 11, 0, 1, 131, 530, 531, 520, 521, 510, 511, 500, 501, 1600, 203, 413, 223, 433, 243,
-        453, 121, 1610, 202, 412, 222, 432, 242, 452, 111, 620, 903, 923, 1620, 201, 411, 221, 431, 241, 451, 101,
-        943, 200, 410, 220, 430, 240, 450, 130, 902, 1013, 621, 922, 1033, 303, 323, 343, 1053, 120, 700, 901, 942,
-        302, 322, 342, 110, 1012, 630, 921, 941, 301, 321, 341, 100, 710, 900, 920, 1032, 300, 320, 340, 1052, 940,
-        631, 1113, 1133, 1103, 1011, 1123, 800, 1031, 1153, 1051, 1143, 810, 1630, 1310, 1112, 1010, 1330, 1300,
-        1640, 1030, 1350, 1510, 1320, 1410, 1050, 1340, 1530, 1102, 1132, 1210, 1500, 1122, 1550, 1200, 1101, 1520,
-        1220, 1142, 1540, 1240, 1121, 1152, 1400, 1141, 1111, 1430, 1230, 1100, 1131, 1120, 1151, 1420, 1250, 1140,
-        1110, 1440, 1130, 1150, 1450,
+        453, 121, 1610, 202, 412, 222, 432, 242, 903, 620, 452, 111, 923, 1620, 201, 411, 221, 431, 241, 451, 101,
+        943, 200, 410, 220, 430, 240, 450, 130, 621, 700, 902, 1013, 922, 1033, 942, 1053, 303, 323, 343, 120, 901,
+        1012, 921, 302, 322, 342, 110, 630, 710, 900, 1032, 941, 301, 321, 341, 100, 920, 300, 320, 340, 940, 1052,
+        631, 1113, 1133, 1153, 1011, 1103, 800, 1123, 1031, 1112, 1051, 1143, 810, 1630, 1310, 1010, 1330, 1410,
+        1300, 1132, 1030, 1640, 1320, 1510, 1350, 1050, 1530, 1340, 1102, 1500, 1210, 1122, 1430, 1200, 1142, 1520,
+        1230, 1101, 1550, 1220, 1121, 1540, 1152, 1240, 1100, 1400, 1111, 1141, 1131, 1120, 1420, 1151, 1250, 1140,
+        1440, 1110, 1130, 1450, 1150,
     ),
     (True, True): (
         30, 31, 20, 21, 10, 11, 0, 1, 131, 530, 531, 520, 521, 510, 511, 500, 501, 1600, 203, 413, 223, 433, 243,
-        453, 121, 1610, 903, 202, 412, 222, 432, 242, 452, 111, 620, 923, 201, 411, 221, 431, 241, 451, 101, 943,
-        1620, 902, 200, 410, 220, 430, 240, 450, 130, 1013, 621, 922, 1033, 942, 1053, 303, 323, 343, 120, 700, 901,
-        921, 302, 322, 342, 110, 630, 1012, 941, 900, 301, 321, 341, 100, 710, 920, 1032, 940, 300, 320, 340, 1113,
-        1052, 631, 1133, 1103, 1123, 1011, 800, 1153, 1031, 1051, 1143, 810, 1630, 1112, 1102, 1310, 1330, 1010,
-        1300, 1640, 1320, 1410, 1030, 1350, 1400, 1340, 1510, 1132, 1050, 1210, 1530, 1122, 1500, 1200, 1142, 1520,
-        1220, 1101, 1550, 1240, 1152, 1121, 1540, 1230, 1111, 1141, 1430, 1131, 1100, 1250, 1151, 1120, 1420, 1140,
+        453, 121, 903, 1610, 202, 412, 620, 222, 432, 242, 452, 111, 923, 943, 201, 411, 221, 431, 241, 451, 101,
+        902, 1620, 200, 410, 220, 430, 240, 450, 130, 621, 700, 1013, 922, 1033, 942, 901, 1053, 303, 323, 343, 120,
+        921, 302, 322, 342, 110, 630, 710, 900, 1012, 941, 301, 321, 341, 920, 100, 1032, 940, 300, 320, 340, 1113,
+        1052, 631, 1133, 1153, 1103, 1123, 1011, 800, 1143, 1112, 1031, 1051, 810, 1630, 1102, 1310, 1330, 1132,
+        1010, 1300, 1410, 1640, 1320, 1400, 1030, 1350, 1510, 1340, 1530, 1050, 1200, 1430, 1122, 1210, 1500, 1142,
+        1230, 1520, 1101, 1220, 1152, 1550, 1121, 1240, 1111, 1540, 1100, 1131, 1141, 1250, 1151, 1420, 1120, 1140,
         1440, 1110, 1130, 1150, 1450,
     ),
 }
@@ -216,11 +214,10 @@
         return pltpu.make_async_copy(pieces[ch].at[z], whole(ch, z, m, c), lout.at[ch])
 
     def inputs():
-        sources = (*weights, *rows_in)
-        return [
-            pltpu.make_async_copy(src, dst, lin.at[i])
-            for i, (src, dst) in enumerate(zip(sources, (attn_v, mlp_v, rows_v.at[0], rows_v.at[1])))
-        ]
+        pairs = [(weights[0].at[:, j, :], attn_v.at[j]) for j in range(4)]
+        pairs += [(rows_in[i], rows_v.at[i]) for i in range(2)]
+        pairs += [(weights[1].at[:, j, :], mlp_v.at[j]) for j in range(2)]
+        return [pltpu.make_async_copy(src, dst, lin.at[i]) for i, (src, dst) in enumerate(pairs)]
 
     for one in inputs():
         one.start()
@@ -448,32 +445,34 @@
     step = 16
 
     def attn_in():
-        inputs()[0].wait()
+        for one in inputs()[:4]:
+            one.wait()
         wide = attn_v.shape[2] // Z
 
         @pl.loop(0, rows // step)
         def _(i):
             span = pl.ds(pl.multiple_of(i * step, step), step)
             for j in range(4):
-                block = attn_v[span, j, :].astype(bf16)
+                block = attn_v[j, span, :].astype(bf16)
                 for q in range(Z):
                     at = j % 2 * wide
                     pieces[j // 2][q, span, at : at + wide] = block[:, q * wide : (q + 1) * wide]
 
     def mlp_in():
-        inputs()[1].wait()
+        for one in inputs()[6:]:
+            one.wait()
         wide = mlp_v.shape[2] // (2 * Z)
 
         @pl.loop(0, rows // step)
         def _(i):
             span = pl.ds(pl.multiple_of(i * step, step), step)
             for j in range(2):
-                block = mlp_v[span, j, :].astype(bf16)
+                block = mlp_v[j, span, :].astype(bf16)
                 for q in range(2 * Z):
                     pieces[2 + 2 * j + q % 2][q // 2, span, :] = block[:, q * wide : (q + 1) * wide]
 
     def rows_low():
-        for one in inputs()[2:]:
+        for one in inputs()[4:6]:
             one.wait()
         out_sum[...] = jnp.zeros_like(out_sum)
 
@@ -699,7 +698,7 @@
             sem((Z, 2)),
             sem((doubling,)),
             sem((doubling,)),
-            sem((4,)),
+            sem((8,)),
             sem((count,)),
             sem((2,)),
             sem((3, Z)),
@@ -708,7 +707,8 @@
         + [vmem(2, tokens, width), vmem(width, 2 * n), vmem(width, 2 * n), vmem(2, 2 * own, width)]
         + [vmem(tokens, width), vmem(2, width, hidden // Z), wide(Z, tokens, hidden // Z)]
         + [wide(2, n), wide(1, hidden), wide(devices, 16, 128), vmem(2 * own, 9 * 128)]
-        + [wide(*attn_weight.shape), wide(*mlp_weight.shape), wide(2, own, width), vmem(2, own, width)],
+        + [wide(4, rows, attn_weight.shape[2]), wide(2, rows, mlp_weight.shape[2])]
+        + [wide(2, own, width), vmem(2, own, width)],
         compiler_params=pltpu.CompilerParams(collective_id=0, has_side_effects=True, vmem_limit_bytes=67043328),
         name="gather_all",
     )(attn_weight, mlp_weight, block_in, out_grad, small, positions)
@@ -1282,9 +1282,37 @@
     scatter_kernel(m_size, fused, *refs)
 
 
-def update_kernel(*refs):
+def update_kernel(step, steps, *refs):
     rows, cotangent, back, bias, qk, vo, up, dn = refs[:8]
-    block_out, input_grad = refs[14:16]
+    attn, mlp, (block_out, input_grad) = refs[8:11], refs[11:14], refs[14:16]
+    attn_outs, mlp_outs = refs[16:20], refs[20:24]
+    attn_v, mlp_v, attn_new, mlp_new, in_sem, out_sem = refs[24:]
+    i = pl.program_id(0)
+
+    def copies(i, sources, buffer, sems, at, out):
+        slot = lax.rem(i, 2)
+        span = pl.ds(pl.multiple_of(i * step, step), step)
+        made = []
+        for n, ref in enumerate(sources):
+            for j in range(ref.shape[1]):
+                far, near = ref.at[span, j, :], buffer.at[slot, n, j]
+                pair = (near, far) if out else (far, near)
+                made.append(pltpu.make_async_copy(*pair, sems.at[slot, at + n, j]))
+        return made
+
+    loads = lambda i: copies(i, attn, attn_v, in_sem, 0, False) + copies(i, mlp, mlp_v, in_sem, 3, False)
+    stores = lambda i: copies(i, attn_outs, attn_new, out_sem, 0, True) + copies(i, mlp_outs, mlp_new, out_sem, 4, True)
+
+    @pl.when(i == 0)
+    def _():
+        for one in loads(0):
+            one.start()
+
+    @pl.when(i + 1 < steps)
+    def _():
+        for one in loads(i + 1):
+            one.start()
+
     normed, inverse = layer_stats(rows[...])
     block_out[...] = rows[...] + back[0].astype(f32) + bias[...]
     u = back[1].astype(f32)
@@ -1293,38 +1321,57 @@
         - jnp.mean(u, axis=-1, keepdims=True)
         - normed * jnp.mean(u * normed, axis=-1, keepdims=True)
     )
-    for sources, (weight, one, two), outs in (
-        ((qk, qk, vo, vo), refs[8:11], refs[16:20]),
-        ((up, dn), refs[11:14], refs[20:24]),
-    ):
-        kinds, wide = weight.shape[1], weight.shape[2] // Z
+
+    @pl.when(i >= 2)
+    def _():
+        for one in stores(i - 2):
+            one.wait()
+
+    for one in loads(i):
+        one.wait()
+    slot = lax.rem(i, 2)
+    for sources, olds, news in (((qk, qk, vo, vo), attn_v, attn_new), ((up, dn), mlp_v, mlp_new)):
+        kinds, wide = olds.shape[2], olds.shape[4] // Z
         for j in range(kinds):
             at = j % (kinds // 2) * wide
             for q in range(Z):
                 cols = slice(q * wide, (q + 1) * wide)
                 g = sources[j][q, :, at : at + wide].astype(f32)
-                updated = adam_step(weight[:, j, cols], g, one[:, j, cols], two[:, j, cols])
-                for ref, value in zip(outs, (g, *updated)):
-                    ref[:, j, cols] = value
+                updated = adam_step(olds[slot, 0, j, :, cols], g, olds[slot, 1, j, :, cols], olds[slot, 2, j, :, cols])
+                for n, value in enumerate((g, *updated)):
+                    news[slot, n, j, :, cols] = value
+    for one in stores(i):
+        one.start()
+
+    @pl.when(i == steps - 1)
+    def _():
+        if steps > 1:
+            for one in stores(i - 1):
+                one.wait()
+        for one in stores(i):
+            one.wait()
 
 
 def update(block_in, out_grad, own_rows, bias, own, attn, mlp):
     rows, width = block_in.shape
     shard = attn[0].shape[0]
-    step = min(shard, 16)
+    step = min(shard, 32)
     steps = shard // step
     by_rows = pl.BlockSpec((rows // steps, width), lambda i: (i, 0))
-    block = lambda v: pl.BlockSpec((step,) + v.shape[1:], lambda i: (i, 0, 0))
+    in_place = pl.BlockSpec(memory_space=pl.ANY)
+    slots = lambda count, v: pltpu.VMEM((2, count, v.shape[1], step, v.shape[2]), f32)
     return pl.pallas_call(
-        update_kernel,
+        functools.partial(update_kernel, step, steps),
         grid=(steps,),
         in_specs=[by_rows, by_rows, pl.BlockSpec((2, rows // steps, width), lambda i: (0, i, 0)), fixed(1, width)]
         + [pl.BlockSpec((Z, step, g.shape[2]), lambda i: (0, i, 0)) for g in own]
-        + [block(v) for v in (*attn, *mlp)],
-        out_specs=[by_rows, by_rows] + [block(attn[0])] * 4 + [block(mlp[0])] * 4,
+        + [in_place] * 6,
+        out_specs=[by_rows, by_rows] + [in_place] * 8,
         out_shape=[jax.ShapeDtypeStruct((rows, width), f32)] * 2
         + [jax.ShapeDtypeStruct(attn[0].shape, f32)] * 4
         + [jax.ShapeDtypeStruct(mlp[0].shape, f32)] * 4,
+        scratch_shapes=[slots(3, attn[0]), slots(3, mlp[0]), slots(4, attn[0]), slots(4, mlp[0])]
+        + [pltpu.SemaphoreType.DMA((2, 6, 4)), pltpu.SemaphoreType.DMA((2, 8, 4))],
         compiler_params=pltpu.CompilerParams(vmem_limit_bytes=VMEM_BYTES),
         name="update",
     )(block_in, out_grad, own_rows, bias, *own, *attn, *mlp)

time: 364 us -> 347 us (0.953)
  Pallas kernels: 361 us -> 344 us
    pallas_call x1, Pallas kernels: 166 us -> 153 us  [gather(): pl.pallas_call(functools.partial(gather_kernel, m_size), out_shape=[shape...]
    pallas_call x1, Pallas kernels: 25 us -> 21.2 us  [update(): pl.pallas_call(functools.partial(update_kernel, step, steps), grid=(steps...]
where the time goes in v6:
time: 347 us; the launch traced here: 346 us
  Pallas kernels  344 us (99%)
    pallas_call x1, Pallas kernels, gather(): pl.pallas_call(functools.partial(gather_kernel, m_size), out_shape=[shape...  153 us
    pallas_call x1, Pallas kernels, scatter(): pl.pallas_call(functools.partial(scatter_entry, m_size, fused), out_shape...  148 us
    pallas_call x1, Pallas kernels, run_outs(): pl.pallas_call(outs_kernel, grid_spec=pltpu.PrefetchScalarGridSpec(num_sc...  21.6 us
    pallas_call x1, Pallas kernels, update(): pl.pallas_call(functools.partial(update_kernel, step, steps), grid=(steps...  21.2 us

profile of v6, /device:TPU:0, one launch (start us, length us, event | category | flops | bytes accessed | tf_op | source)
XLA Modules:
  0.0 346.2 jit_solution(9258518764045699893)
XLA Ops:
  0.7 153.0 %gather_all.1 = (bf16[2048,512]{1,0:T(8,128)(2,1)}, bf16[2048,512]{1,0:T(8,128)(2,1)}, bf16[2048,1024]{1,0:T(8,128)(2,1)}, bf16[2048,1024]{1,0:T(8,128)(2,1)}, b...) custom-call(f32[128,4,1024]{2,1,0:T(4,128)} %refs_8_.1, ...), custom_call_target="tpu_custom_call" | custom-call | tf_op jit(solution)/shard_map/gather_all/pallas_call | solution.py:672
  153.7 21.6 %outputs.1 = (bf16[1024,2048]{1,0:T(8,128)(2,1)}, bf16[1024,2048]{1,0:T(8,128)(2,1)}, f32[4,2048]{1,0:T(4,128)}) custom-call(s32[1]{0:T(128)} %bitcast.flag, bf16[1024,256]{1,0:T(8,128)(2,1)} %get-tuple-element.52.att.refs_3_, bf16[1024,768]{1,0:T(8,128)(2,1)} %get-tuple-element.53.d_attn.refs_4_, bf16[1024,1024]{1,0:T(8,128)(2,1)} %get-tuple-element.54.act.refs_5_, ...), custom_call_target="tpu_custom_call" | custom-call | tf_op jit(solution)/shard_map/outputs/pallas_call | solution.py:767
  175.3 148.2 %scatter_all.1 = (bf16[4,2,2,128,512]{4,3,2,1,0:T(8,128)(2,1)}, bf16[4,2,2,128,512]{4,3,2,1,0:T(8,128)(2,1)}, bf16[4,2,2,128,1024]{4,3,2,1,0:T(8,128)(2,1)}, bf1...) custom-call(bf16[1024,2048]{1,0:T(8,128)(2,1)} %get-tuple-element.49, ...), custom_call_target="tpu_custom_call" | custom-call | tf_op jit(solution)/shard_map/scatter_all/pallas_call | solution.py:1266
  323.5 1.4 multiply_subtract_fusion
  324.9 21.2 %update.1 = (f32[128,2048]{1,0:T(8,128)}, f32[128,2048]{1,0:T(8,128)}, f32[128,4,1024]{2,1,0:T(4,128)}, f32[128,4,1024]{2,1,0:T(4,128)}, f32[128,4,1024]{2,1,0:T...) custom-call(f32[128,2048]{1,0:T(8,128)} %refs_0_.3, ...), custom_call_target="tpu_custom_call" | custom-call | tf_op jit(solution)/shard_map/update/pallas_call | solution.py:1363

commit v7 on v6

--- a/solution.py
+++ b/solution.py
@@ -177,13 +177,16 @@
 def gather_kernel(m_size, *refs):
     weights, rows_in, small, positions = refs[:2], refs[2:4], refs[4], refs[5]
     full, act_out, one_out, two_out = refs[6:10], refs[10], refs[11], refs[12]
-    att, d_attn, hidden_out, d_pre, head_sums, up_sums, par, row_bias, out_sum = refs[13:22]
+    made_out, rows_made = refs[13:17], refs[17:19]
+    head_sums, up_sums, norm_sums, row_bias, out_sum = refs[19:24]
     count = len(CHUNKS)
-    stage, stage_m, relay = (refs[22 + i * count : 22 + (i + 1) * count] for i in range(3))
-    refs = refs[22 + 3 * count :]
-    (zs, zr, gs, gr, ps, pr, ms, mr, near_s, far_s, xr, as_, ar, ws, wr, ss, sr, lin, lout, ls, os_) = refs[:21]
-    pieces, refs = refs[21 : 21 + count], refs[21 + count :]
-    act, w_qk, w_vo, one_v, two_v, tile_v, slope, bias, up_bias, table, base, attn_v, mlp_v, rows_v, low = refs
+    stage, stage_m, relay = (refs[24 + i * count : 24 + (i + 1) * count] for i in range(3))
+    refs = refs[24 + 3 * count :]
+    (zs, zr, gs, gr, ps, pr, ms, mr, near_s, far_s, xr, as_, ar, ws, wr, ss, sr, lin, lout, ls, os_, made_s, tile_s, rows_s) = refs[:24]
+    pieces, refs = refs[24 : 24 + count], refs[24 + count :]
+    act, w_qk, w_vo, one_v, two_v, tile_v, slope, bias, up_bias, table, base, attn_v, mlp_v, rows_v, low = refs[:15]
+    par, att, d_attn, hidden_out, d_pre = refs[15:20]
+    tiles, both_v = refs[20:24], refs[24]
     net = Links(m_size)
     z, m, c, t = net.z, net.m, net.c, net.t
     rows = pieces[0].shape[1]
@@ -597,6 +600,63 @@
         d_pre[:, cols] = value.astype(bf16)
         up_sums[:, cols] = jnp.sum(value, axis=0, keepdims=True)
 
+        @pl.when(j == Z - 1)
+        def _():
+            for one in tile_rows(0) + made_saved():
+                one.start()
+
+    def made_saved():
+        pairs = zip((att, d_attn, hidden_out, d_pre), made_out)
+        return [pltpu.make_async_copy(src, dst, made_s.at[i]) for i, (src, dst) in enumerate(pairs)]
+
+    tall = 256
+    last = width // tall
+
+    def tile_rows(p):
+        span = pl.ds(pl.multiple_of(p * tall, tall), tall)
+        slot = lax.rem(p, 2)
+        return [
+            pltpu.make_async_copy(src.at[span], dst.at[slot], tile_s.at[slot, i])
+            for i, (src, dst) in enumerate(zip(full, tiles))
+        ]
+
+    def rows_stored(p):
+        cols = pl.ds(pl.multiple_of(p * tall, tall), tall)
+        slot = lax.rem(p, 2)
+        return [
+            pltpu.make_async_copy(both_v.at[slot, i], ref.at[:, cols], rows_s.at[slot, i])
+            for i, ref in enumerate(rows_made)
+        ]
+
+    def outputs(p):
+        slot = lax.rem(p, 2)
+
+        @pl.when(p + 1 < last)
+        def _():
+            for one in tile_rows(p + 1):
+                one.start()
+
+        @pl.when(p >= 2)
+        def _():
+            for one in rows_stored(p - 2):
+                one.wait()
+
+        for one in tile_rows(p):
+            one.wait()
+        cols = pl.ds(pl.multiple_of(p * tall, tall), tall)
+        t_qk, t_vo, t_up, t_dn = (tile[slot] for tile in tiles)
+        y = dot(att[...], t_vo[:, n:], 1, 1) + dot(hidden_out[...], t_dn, 1, 1)
+        d_one = dot(d_attn[:, 0 : 2 * n], t_qk, 1, 1) + dot(d_attn[:, 2 * n :], t_vo[:, :n], 1, 1)
+        d_two = dot(d_pre[...], t_up, 1, 1)
+        u = d_one * par[0:1, cols] + d_two * par[2:3, cols]
+        both_v[slot, 0] = jnp.where(role == 0, y, u).astype(bf16)
+        both_v[slot, 1] = jnp.where(role == 0, u, y).astype(bf16)
+        plain = act[0, :, cols].astype(f32)
+        for i, value in enumerate((d_one * plain, d_one, d_two * plain, d_two)):
+            norm_sums[i : i + 1, cols] = jnp.sum(value, axis=0, keepdims=True)
+        for one in rows_stored(p):
+            one.start()
+
     def part(i, inner, diag):
         _, run, rows_out, small_last, _ = programs[inner, diag]
         if i == 1:
@@ -608,14 +668,15 @@
     by_class(inner_z, role, lambda inner, diag: programs[inner, diag][0]())
     ahead = 3
 
-    @pl.loop(0, work - 1)
+    @pl.loop(0, work - 1 + last)
     def _(i):
         pl.when(i == 0)(attn_in)
         pl.when(i == 1)(rows_low)
         pl.when(i == 2)(mlp_in)
         pl.when((i >= ahead) & (i < ahead + Z))(lambda: attention(i - ahead))
         pl.when((i >= ahead + Z) & (i < ahead + 2 * Z))(lambda: hidden(i - ahead))
-        pl.when(i >= ahead + 2 * Z)(lambda: hidden_back(i - ahead))
+        pl.when((i >= ahead + 2 * Z) & (i < ahead + 3 * Z))(lambda: hidden_back(i - ahead))
+        pl.when(i >= ahead + 3 * Z)(lambda: outputs(i - ahead - 3 * Z))
         for e in range(work - 1):
 
             @pl.when(i == e)
@@ -627,6 +688,8 @@
         saved = rows_saved(i)
         for copy in saved[1:] if i < 2 else saved:
             copy.wait()
+    for copy in made_saved() + rows_stored(last - 2) + rows_stored(last - 1):
+        copy.wait()
 
 
 def runs_before(order):
@@ -674,12 +737,13 @@
         out_shape=[shape(width, n) for n in cols]
         + [shape(2, tokens, width), shape(tokens, width), shape(tokens, width)]
         + [shape(tokens, n), shape(tokens, 3 * n), shape(tokens, hidden), shape(tokens, hidden)]
+        + [shape(tokens, width)] * 2
         + [exact(2, n), exact(1, hidden), exact(4, width), exact(1, width), exact(1, width)]
         + [shape(Z, rows, n) for n in parts]
         + [shape(m_size, Z, rows, n) for n in parts]
         + [shape(4, rows, n) for n in parts],
         in_specs=[in_place] * 4 + [in_vmem] * 2,
-        out_specs=[in_place] * 7 + [in_vmem] * 9 + [in_place] * (3 * count),
+        out_specs=[in_place] * 13 + [in_vmem] * 5 + [in_place] * (3 * count),
         scratch_shapes=[
             sem((count, 3)),
             sem((count, Z)),
@@ -702,17 +766,23 @@
             sem((count,)),
             sem((2,)),
             sem((3, Z)),
+            sem((4,)),
+            sem((2, 4)),
+            sem((2, 2)),
         ]
         + [vmem(Z, rows, n) for n in parts]
         + [vmem(2, tokens, width), vmem(width, 2 * n), vmem(width, 2 * n), vmem(2, 2 * own, width)]
         + [vmem(tokens, width), vmem(2, width, hidden // Z), wide(Z, tokens, hidden // Z)]
         + [wide(2, n), wide(1, hidden), wide(devices, 16, 128), vmem(2 * own, 9 * 128)]
         + [wide(4, rows, attn_weight.shape[2]), wide(2, rows, mlp_weight.shape[2])]
-        + [wide(2, own, width), vmem(2, own, width)],
+        + [wide(2, own, width), vmem(2, own, width), wide(4, width)]
+        + [vmem(tokens, n), vmem(tokens, 3 * n), vmem(tokens, hidden), vmem(tokens, hidden)]
+        + [vmem(2, 256, cols) for cols in cols]
+        + [vmem(2, 2, tokens, 256)],
         compiler_params=pltpu.CompilerParams(collective_id=0, has_side_effects=True, vmem_limit_bytes=67043328),
         name="gather_all",
     )(attn_weight, mlp_weight, block_in, out_grad, small, positions)
-    return outs[:4], outs[4], outs[5:7], outs[7:11], outs[11:13], outs[13], outs[14], outs[15]
+    return (*outs[5:7], outs[4], *outs[7:11]), outs[11:13], outs[13:18]
 
 
 VMEM_BYTES = 60 * 1024 * 1024
@@ -743,42 +813,6 @@
 
 def fixed(*shape):
     return pl.BlockSpec(shape, lambda i: (0,) * len(shape))
-
-
-def outs_kernel(flag, att, d_attn, act, d_pre, x, w_qk, w_vo, w_up, w_dn, par, keep, give, sums):
-    diag = flag[0] == 1
-    n = HEAD_DIM
-    y = dot(att[...], w_vo[:, n:], 1, 1) + dot(act[...], w_dn[...], 1, 1)
-    d_one = dot(d_attn[:, : 2 * n], w_qk[...], 1, 1) + dot(d_attn[:, 2 * n :], w_vo[:, :n], 1, 1)
-    d_two = dot(d_pre[...], w_up[...], 1, 1)
-    u = d_one * par[0:1, :] + d_two * par[2:3, :]
-    keep[...] = jnp.where(diag, y, u).astype(bf16)
-    give[...] = jnp.where(diag, u, y).astype(bf16)
-    plain = x[...].astype(f32)
-    for i, value in enumerate((d_one * plain, d_one, d_two * plain, d_two)):
-        sums[i : i + 1, :] = jnp.sum(value, axis=0, keepdims=True)
-
-
-def run_outs(diag, att, d_attn, act, d_pre, acts, weights, par):
-    _, rows, width = acts.shape
-    step = 256
-    fix = lambda v: pl.BlockSpec(v.shape, lambda i, s: (0, 0), pipeline_mode=pl.Buffered(1))
-    tile = lambda height: pl.BlockSpec((height, step), lambda i, s: (0, i))
-    return pl.pallas_call(
-        outs_kernel,
-        grid_spec=pltpu.PrefetchScalarGridSpec(
-            num_scalar_prefetch=1,
-            grid=(width // step,),
-            in_specs=[fix(v) for v in (att, d_attn, act, d_pre)]
-            + [pl.BlockSpec((None, rows, step), lambda i, s: (0, 0, i))]
-            + [pl.BlockSpec((step, v.shape[1]), lambda i, s: (i, 0)) for v in weights]
-            + [tile(4)],
-            out_specs=[tile(rows), tile(rows), tile(4)],
-        ),
-        out_shape=[jax.ShapeDtypeStruct((rows, width), bf16)] * 2 + [jax.ShapeDtypeStruct((4, width), f32)],
-        compiler_params=pltpu.CompilerParams(vmem_limit_bytes=VMEM_BYTES),
-        name="outputs",
-    )(diag.astype(jnp.int32).reshape(1), att, d_attn, act, d_pre, acts, *weights, par)
 
 
 def grads_kernel(one, two, g, att, d_attn, act, d_pre, qk, vo, up, dn):
@@ -823,7 +857,7 @@
 
 def scatter_kernel(m_size, fused, *refs):
     if fused:
-        ones, twos, acts, att, d_attn, act, d_pre = refs[:7]
+        ones, twos, acts, *factors_in = refs[:7]
         keep, give, *sums = refs[7:13]
         grads, refs = refs[13:17], refs[17:]
     else:
@@ -839,7 +873,8 @@
     got, kept, got_z, final, current, got_small = refs[:6]
     (gs, gr, kl, as_, ar, ys, yr, yl, ws, wr, wl, fs, fr, xs, xr, zs, zr, zl, ps, pr, ss, sr) = refs[6:28]
     if fused:
-        tiles, made, tl, ml = refs[28:]
+        tiles, made, tl, ml, factors, fl = refs[28:]
+        att, d_attn, act, d_pre = factors
     net = Links(m_size)
     z, m, c, t = net.z, net.m, net.c, net.t
     half = rows_out.shape[1]
@@ -904,6 +939,12 @@
 
         for one in tile_loads(i, slot):
             one.wait()
+
+        @pl.when(i == 0)
+        def _():
+            for one in factor_loads():
+                one.wait()
+
         n = HEAD_DIM
         high = made[0].shape[1]
         for array, at, left, right, lo, hi in (
@@ -927,8 +968,11 @@
         for one in stores:
             one.wait()
 
+    def factor_loads():
+        return [pltpu.make_async_copy(src, dst, fl.at[n]) for n, (src, dst) in enumerate(zip(factors_in, factors))]
+
     if fused:
-        for one in tile_loads(0, 0):
+        for one in tile_loads(0, 0) + factor_loads():
             one.start()
     net.meet()
 
@@ -1220,7 +1264,7 @@
     out_specs = [in_place] * 5 + [in_vmem]
     if fused:
         inputs = [one, two, acts, att, d_attn, act, d_pre]
-        in_specs = [in_place] * 3 + [in_vmem] * 4
+        in_specs = [in_place] * 7
         out_shape, out_specs = term_shapes + out_shape, [in_place] * 4 + out_specs
     else:
         inputs = [g.reshape(s.shape) for g, s in zip(run_grads(*factors), term_shapes)]
@@ -1263,12 +1307,13 @@
         scratch.append(vmem(2, 3, keep.shape[0], 2 * block))
         made = [vmem(2, block, n) for n in cols]
         scratch_made = [sem((2, 3)), sem((4,))]
+        loaded = [pltpu.VMEM(v.shape, bf16) for v in (att, d_attn, act, d_pre)] + [sem((4,))]
     outs = pl.pallas_call(
         functools.partial(scatter_entry, m_size, fused),
         out_shape=out_shape,
         in_specs=in_specs + [in_place] * 2 + [in_vmem] * 4,
         out_specs=out_specs,
-        scratch_shapes=scratch + (made + scratch_made if fused else []),
+        scratch_shapes=scratch + (made + scratch_made + loaded if fused else []),
         compiler_params=pltpu.CompilerParams(collective_id=1, has_side_effects=True, vmem_limit_bytes=67043328),
         name="scatter_all",
     )(*inputs, keep.reshape(Z, seq, width), give.reshape(Z, seq, width), *sums)
@@ -1278,15 +1323,15 @@
 
 def scatter_entry(m_size, fused, *refs):
     if fused:
-        refs = refs[:-6] + (refs[-6:-2],) + refs[-2:]
+        refs = refs[:-11] + (refs[-11:-7],) + refs[-7:-5] + (refs[-5:-1],) + refs[-1:]
     scatter_kernel(m_size, fused, *refs)
 
 
 def update_kernel(step, steps, *refs):
     rows, cotangent, back, bias, qk, vo, up, dn = refs[:8]
-    attn, mlp, (block_out, input_grad) = refs[8:11], refs[11:14], refs[14:16]
-    attn_outs, mlp_outs = refs[16:20], refs[20:24]
-    attn_v, mlp_v, attn_new, mlp_new, in_sem, out_sem = refs[24:]
+    attn, mlp, small_sums, small, refs = refs[8:11], refs[11:14], refs[14], refs[15:18], refs[18:]
+    (block_out, input_grad), attn_outs, mlp_outs, small_outs = refs[:2], refs[2:6], refs[6:10], refs[10:14]
+    attn_v, mlp_v, attn_new, mlp_new, in_sem, out_sem = refs[14:]
     i = pl.program_id(0)
 
     def copies(i, sources, buffer, sems, at, out):
@@ -1307,6 +1352,9 @@
     def _():
         for one in loads(0):
             one.start()
+        g = small_sums[0 : small[0].shape[0], 0 : small[0].shape[1]]
+        for ref, value in zip(small_outs, (g, *adam_step(small[0][...], g, small[1][...], small[2][...]))):
+            ref[...] = value
 
     @pl.when(i + 1 < steps)
     def _():
@@ -1352,7 +1400,7 @@
             one.wait()
 
 
-def update(block_in, out_grad, own_rows, bias, own, attn, mlp):
+def update(block_in, out_grad, own_rows, bias, own, attn, mlp, small_sums, small):
     rows, width = block_in.shape
     shard = attn[0].shape[0]
     step = min(shard, 32)
@@ -1365,16 +1413,18 @@
         grid=(steps,),
         in_specs=[by_rows, by_rows, pl.BlockSpec((2, rows // steps, width), lambda i: (0, i, 0)), fixed(1, width)]
         + [pl.BlockSpec((Z, step, g.shape[2]), lambda i: (0, i, 0)) for g in own]
-        + [in_place] * 6,
-        out_specs=[by_rows, by_rows] + [in_place] * 8,
+        + [in_place] * 6
+        + [fixed(*v.shape) for v in (small_sums, *small)],
+        out_specs=[by_rows, by_rows] + [in_place] * 8 + [fixed(*small[0].shape)] * 4,
         out_shape=[jax.ShapeDtypeStruct((rows, width), f32)] * 2
         + [jax.ShapeDtypeStruct(attn[0].shape, f32)] * 4
-        + [jax.ShapeDtypeStruct(mlp[0].shape, f32)] * 4,
+        + [jax.ShapeDtypeStruct(mlp[0].shape, f32)] * 4
+        + [jax.ShapeDtypeStruct(small[0].shape, f32)] * 4,
         scratch_shapes=[slots(3, attn[0]), slots(3, mlp[0]), slots(4, attn[0]), slots(4, mlp[0])]
         + [pltpu.SemaphoreType.DMA((2, 6, 4)), pltpu.SemaphoreType.DMA((2, 8, 4))],
         compiler_params=pltpu.CompilerParams(vmem_limit_bytes=VMEM_BYTES),
         name="update",
-    )(block_in, out_grad, own_rows, bias, *own, *attn, *mlp)
+    )(block_in, out_grad, own_rows, bias, *own, *attn, *mlp, small_sums, *small)
 
 
 def body(
@@ -1392,22 +1442,22 @@
     small_second,
 ):
     m_size = lax.axis_size("dp") // (2 * Z)
-    diag = lax.axis_index("dp") % 2 == lax.axis_index("tensor")
     rows = block_in.shape[0]
-    part = small_params.shape[1]
-    weights, acts, norms, (attended, d_attn, activation, d_pre), (head_sums, up_sums), par, row_bias, out_sum = gather(
+    factors, (keep, give), sums = gather(
         attn_weight, mlp_weight, block_in, out_grad, small_params, positions, m_size
     )
-    keep, give, norm_sums = run_outs(diag, attended, d_attn, activation, d_pre, acts, weights, par)
-    factors = (*norms, acts, attended, d_attn, activation, d_pre)
-    sums = (norm_sums, head_sums, up_sums, out_sum)
-    own, own_rows, own_small = scatter(factors, keep, give, sums, m_size, rows)
+    head_sums, up_sums, norm_sums, row_bias, out_sum = sums
+    own, own_rows, own_small = scatter(
+        factors, keep, give, (norm_sums, head_sums, up_sums, out_sum), m_size, rows
+    )
     attn = (attn_weight, attn_first, attn_second)
     mlp = (mlp_weight, mlp_first, mlp_second)
-    block_out, input_grad, *updated = update(block_in, out_grad, own_rows, row_bias, own, attn, mlp)
-    attn_out, mlp_out = updated[:4], updated[4:]
-    small_grad = own_small[:12, :part]
-    small_new, small_first_new, small_second_new = adam_step(small_params, small_grad, small_first, small_second)
+    small = (small_params, small_first, small_second)
+    block_out, input_grad, *updated = update(
+        block_in, out_grad, own_rows, row_bias, own, attn, mlp, own_small, small
+    )
+    attn_out, mlp_out = updated[:4], updated[4:8]
+    small_grad, small_new, small_first_new, small_second_new = updated[8:]
 
     attn_grad, attn_new, attn_first_new, attn_second_new = attn_out
     mlp_grad, mlp_new, mlp_first_new, mlp_second_new = mlp_out

time: 347 us -> 341 us (0.983)
  Pallas kernels: 344 us -> 340 us
    pallas_call x1 -> x0, Pallas kernels: 21.6 us -> none  [run_outs(): pl.pallas_call(outs_kernel, grid_spec=pltpu.PrefetchScalarGridSpec(num_sc...]
    pallas_call x1, Pallas kernels: 153 us -> 171 us  [gather(): pl.pallas_call(functools.partial(gather_kernel, m_size), out_shape=[shape...]
where the time goes in v7:
time: 341 us
  Pallas kernels  340 us (100%)
    pallas_call x1, Pallas kernels, gather(): pl.pallas_call(functools.partial(gather_kernel, m_size), out_shape=[shape...  171 us
    pallas_call x1, Pallas kernels, scatter(): pl.pallas_call(functools.partial(scatter_entry, m_size, fused), out_shape...  147 us
    pallas_call x1, Pallas kernels, update(): pl.pallas_call(functools.partial(update_kernel, step, steps), grid=(steps...  21.3 us

profile of v7, /device:TPU:0, one launch (start us, length us, event | category | flops | bytes accessed | tf_op | source)
XLA Modules:
  0.0 340.5 jit_solution(2893511732420932856)
XLA Ops:
  0.6 171.5 %gather_all.1 = (bf16[2048,512]{1,0:T(8,128)(2,1)}, bf16[2048,512]{1,0:T(8,128)(2,1)}, bf16[2048,1024]{1,0:T(8,128)(2,1)}, bf16[2048,1024]{1,0:T(8,128)(2,1)}, b...) custom-call(f32[128,4,1024]{2,1,0:T(4,128)} %refs_8_.1, ...), custom_call_target="tpu_custom_call" | custom-call | tf_op jit(solution)/shard_map/gather_all/pallas_call | solution.py:735
  172.1 147.0 %scatter_all.1 = (bf16[4,2,2,128,512]{4,3,2,1,0:T(8,128)(2,1)}, bf16[4,2,2,128,512]{4,3,2,1,0:T(8,128)(2,1)}, bf16[4,2,2,128,1024]{4,3,2,1,0:T(8,128)(2,1)}, bf1...) custom-call(bf16[1024,2048]{1,0:T(8,128)(2,1)} %get-tuple-element.48, ...), custom_call_target="tpu_custom_call" | custom-call | tf_op jit(solution)/shard_map/scatter_all/pallas_call | solution.py:1311
  319.1 21.3 %update.1 = (f32[128,2048]{1,0:T(8,128)}, f32[128,2048]{1,0:T(8,128)}, f32[128,4,1024]{2,1,0:T(4,128)}, f32[128,4,1024]{2,1,0:T(4,128)}, f32[128,4,1024]{2,1,0:T...) custom-call(f32[128,2048]{1,0:T(8,128)} %refs_0_.3, ...), custom_call_target="tpu_custom_call" | custom-call | tf_op jit(solution)/shard_map/update/pallas_call | solution.py:1411

commit v8 on v7

--- a/solution.py
+++ b/solution.py
@@ -166,12 +166,12 @@
             j *= 2
         return place, steps
 
+    def greet(self):
+        for target in self.partners():
+            pl.semaphore_signal(pltpu.get_barrier_semaphore(), inc=1, device_id=target, device_id_type=MESH)
+
     def meet(self):
-        barrier = pltpu.get_barrier_semaphore()
-        everyone = self.partners()
-        for target in everyone:
-            pl.semaphore_signal(barrier, inc=1, device_id=target, device_id_type=MESH)
-        pl.semaphore_wait(barrier, len(everyone))
+        pl.semaphore_wait(pltpu.get_barrier_semaphore(), len(self.partners()))
 
 
 def gather_kernel(m_size, *refs):
@@ -222,6 +222,7 @@
         pairs += [(weights[1].at[:, j, :], mlp_v.at[j]) for j in range(2)]
         return [pltpu.make_async_copy(src, dst, lin.at[i]) for i, (src, dst) in enumerate(pairs)]
 
+    net.greet()
     for one in inputs():
         one.start()
     flat, steps = net.doubling()
@@ -229,7 +230,6 @@
     table[flat, 0:12, 0 : small.shape[1]] = small[...]
     for e in range(seq // 128):
         table[flat, 12 + e : 13 + e, :] = positions[:, e * 128 : (e + 1) * 128].astype(f32)
-    net.meet()
 
     def program(inner, diag):
         state = {"small": 0}
@@ -665,19 +665,21 @@
         if i == 2:
             small_last()
 
+    attn_in()
+    net.meet()
     by_class(inner_z, role, lambda inner, diag: programs[inner, diag][0]())
+    by_class(inner_z, role, functools.partial(part, 0))
     ahead = 3
 
-    @pl.loop(0, work - 1 + last)
+    @pl.loop(1, work - 1 + last)
     def _(i):
-        pl.when(i == 0)(attn_in)
         pl.when(i == 1)(rows_low)
         pl.when(i == 2)(mlp_in)
         pl.when((i >= ahead) & (i < ahead + Z))(lambda: attention(i - ahead))
         pl.when((i >= ahead + Z) & (i < ahead + 2 * Z))(lambda: hidden(i - ahead))
         pl.when((i >= ahead + 2 * Z) & (i < ahead + 3 * Z))(lambda: hidden_back(i - ahead))
         pl.when(i >= ahead + 3 * Z)(lambda: outputs(i - ahead - 3 * Z))
-        for e in range(work - 1):
+        for e in range(1, work - 1):
 
             @pl.when(i == e)
             def _(e=e):
@@ -947,6 +949,11 @@
 
         n = HEAD_DIM
         high = made[0].shape[1]
+
+        def stored(array):
+            there = grads[array].at[z ^ (Z - 1 - lax.rem(i, Z)), m ^ (1 - i // Z)]
+            return pltpu.make_async_copy(made[array], there, ml.at[array])
+
         for array, at, left, right, lo, hi in (
             (0, 0, 0, d_attn, 0, 2 * n),
             (1, 0, 0, d_attn, 2 * n, 3 * n),
@@ -957,23 +964,19 @@
             value = dot(tiles[slot, left], right[:, lo:hi], 0, 0).astype(bf16)
             for cc in range(2):
                 made[array][cc, :, at : at + hi - lo] = value[cc * high : (cc + 1) * high]
-        stores = [
-            pltpu.make_async_copy(
-                made[array], grads[array].at[z ^ (Z - 1 - lax.rem(i, Z)), m ^ (1 - i // Z)], ml.at[array]
-            )
-            for array in range(4)
-        ]
-        for one in stores:
-            one.start()
-        for one in stores:
-            one.wait()
+            if array != 1 or at:
+                stored(array).start()
+        for array in range(4):
+            stored(array).wait()
 
     def factor_loads():
         return [pltpu.make_async_copy(src, dst, fl.at[n]) for n, (src, dst) in enumerate(zip(factors_in, factors))]
 
+    net.greet()
     if fused:
         for one in tile_loads(0, 0) + factor_loads():
             one.start()
+    small_terms()
     net.meet()
 
     def program(inner, diag):
@@ -1224,7 +1227,6 @@
         programs[inner, diag][1](SCATTER_ORDER[inner, diag][lo:hi])
 
     by_class(inner_z, role, begin)
-    small_terms()
     by_class(inner_z, role, lambda inner, diag: programs[inner, diag][0]())
     if fused:
 

time: 341 us -> 341 us (level)
  no operation moved by 1% of the time
where the time goes in v8:
time: 341 us
  Pallas kernels  340 us (100%)
    pallas_call x1, Pallas kernels, gather(): pl.pallas_call(functools.partial(gather_kernel, m_size), out_shape=[shape...  171 us
    pallas_call x1, Pallas kernels, scatter(): pl.pallas_call(functools.partial(scatter_entry, m_size, fused), out_shape...  148 us
    pallas_call x1, Pallas kernels, update(): pl.pallas_call(functools.partial(update_kernel, step, steps), grid=(steps...  21.3 us

profile of v8, /device:TPU:0, one launch (start us, length us, event | category | flops | bytes accessed | tf_op | source)
XLA Modules:
  0.0 340.9 jit_solution(4874475113333679295)
XLA Ops:
  0.6 170.9 %gather_all.1 = (bf16[2048,512]{1,0:T(8,128)(2,1)}, bf16[2048,512]{1,0:T(8,128)(2,1)}, bf16[2048,1024]{1,0:T(8,128)(2,1)}, bf16[2048,1024]{1,0:T(8,128)(2,1)}, b...) custom-call(f32[128,4,1024]{2,1,0:T(4,128)} %refs_8_.1, ...), custom_call_target="tpu_custom_call" | custom-call | tf_op jit(solution)/shard_map/gather_all/pallas_call | solution.py:737
  171.6 147.9 %scatter_all.1 = (bf16[4,2,2,128,512]{4,3,2,1,0:T(8,128)(2,1)}, bf16[4,2,2,128,512]{4,3,2,1,0:T(8,128)(2,1)}, bf16[4,2,2,128,1024]{4,3,2,1,0:T(8,128)(2,1)}, bf1...) custom-call(bf16[1024,2048]{1,0:T(8,128)(2,1)} %get-tuple-element.48, ...), custom_call_target="tpu_custom_call" | custom-call | tf_op jit(solution)/shard_map/scatter_all/pallas_call | solution.py:1313
  319.4 21.3 %update.1 = (f32[128,2048]{1,0:T(8,128)}, f32[128,2048]{1,0:T(8,128)}, f32[128,4,1024]{2,1,0:T(4,128)}, f32[128,4,1024]{2,1,0:T(4,128)}, f32[128,4,1024]{2,1,0:T...) custom-call(f32[128,2048]{1,0:T(8,128)} %refs_0_.3, ...), custom_call_target="tpu_custom_call" | custom-call | tf_op jit(solution)/shard_map/update/pallas_call | solution.py:1413
